TPU v7x, 8 devices: a whole 2x2x1 slice. The times are simulated.
8 devices in a mesh: dp: 1 (over z), tp: 2 (over y), sp: 4 (over x, core).
Axes of the slice: x: 2, y: 2, z: 1, core: 2. Of those that a mesh axis runs over, the one named last changes fastest.
Arguments:
- tokens: bfloat16 [16, 6144], P(('dp', 'sp'))
- states: float32 [4, 16, 64, 128, 128], P('sp', 'dp', 'tp')
- k_cache: bfloat16 [16, 8, 4096, 128], P('dp', 'tp', 'sp')
- v_cache: bfloat16 [16, 8, 4096, 128], P('dp', 'tp', 'sp')
- slopes: float32 [64], P('tp')
- lin_gain: float32 [6144], replicated
- w_lin_qkv: bfloat16 [6144, 3, 8192], P(None, None, 'tp')
- w_lin_gate: bfloat16 [6144, 8192], P(None, 'tp')
- out_gain: float32 [8192], P('tp')
- w_lin_out: bfloat16 [8192, 6144], P('tp')
- attn_gain: float32 [6144], replicated
- w_attn_in: bfloat16 [6144, 8, 10, 128], P(None, 'tp')
- w_attn_out: bfloat16 [8192, 6144], P('tp')
Outputs:
- output 1: bfloat16 [16, 6144], P(('dp', 'sp'))
- output 2: float32 [16, 64, 128, 128], P(('dp', 'sp'), 'tp')
- output 3: bfloat16 [16, 8, 4112, 128], P(('dp', 'sp'), 'tp')
- output 4: bfloat16 [16, 8, 4112, 128], P(('dp', 'sp'), 'tp')
All inputs are finite; a program needn't handle non-finite values.
Results may differ from a plain program's by a relative error of at most 0.0124783.
Values are sent between devices in bfloat16 or wider.
A program may use at most 2 GiB of HBM per device.

v0:
```python
import jax
import jax.numpy as jnp
from jax import lax
from jax.sharding import PartitionSpec as P

NORM_EPS = 1e-6
ROPE_BASE = 10000000.0
RES_ALPHA = 1.0
RES_BETA = 1.0
CACHE_EXTRA = 16


def rms_norm(vals_in, gain_vec):
    vals32 = vals_in.astype(jnp.float32)
    inv_rms = lax.rsqrt(jnp.mean(vals32 * vals32, axis=-1, keepdims=True) + NORM_EPS)
    return vals32 * inv_rms * gain_vec


def rotary(vals_in, position):
    rope_dim = vals_in.shape[-1] // 2
    half_dim = rope_dim // 2
    inv_freq = ROPE_BASE ** (-jnp.arange(0, rope_dim, 2, dtype=jnp.float32) / rope_dim)
    angles = position * inv_freq
    cosine = jnp.cos(angles)
    sine_vals = jnp.sin(angles)
    vals32 = vals_in.astype(jnp.float32)
    first_half = vals32[..., :half_dim]
    second_half = vals32[..., half_dim:rope_dim]
    return jnp.concatenate([first_half * cosine - second_half * sine_vals, second_half * cosine + first_half * sine_vals, vals32[..., rope_dim:]], axis=-1).astype(jnp.bfloat16)


def lightning_layer(tokens, moved_state, slopes, lin_gain, w_lin_qkv, w_lin_gate, out_gain, w_lin_out, hidden_width):
    rows = tokens.shape[0]
    heads_dev = slopes.shape[0]
    head_dim = moved_state.shape[-1]
    normed = rms_norm(tokens, lin_gain).astype(jnp.bfloat16)
    lin_proj = jnp.einsum('bd,dkn->bkn', normed, w_lin_qkv, preferred_element_type=jnp.float32)
    act_vals = jax.nn.silu(lin_proj).astype(jnp.bfloat16).reshape(rows, 3, heads_dev, head_dim)
    state_new = jnp.exp(-slopes)[None, :, None, None] * moved_state + jnp.einsum('bhd,bhe->bhde', act_vals[:, 1], act_vals[:, 2], preferred_element_type=jnp.float32)
    lin_attn = jnp.einsum('bhd,bhde->bhe', act_vals[:, 0].astype(jnp.float32), state_new).reshape(rows, heads_dev * head_dim)
    square_sum = lax.psum(jnp.sum(lin_attn * lin_attn, axis=-1, keepdims=True), 'tp')
    inv_rms = lax.rsqrt(square_sum / hidden_width + NORM_EPS)
    gate_vals = jax.nn.sigmoid(jnp.dot(normed, w_lin_gate, preferred_element_type=jnp.float32))
    mixed_out = (lin_attn * inv_rms * out_gain * gate_vals).astype(jnp.bfloat16)
    lin_out = lax.psum(jnp.dot(mixed_out, w_lin_out, preferred_element_type=jnp.float32), 'tp')
    hidden = (RES_ALPHA * normed.astype(jnp.float32) + RES_BETA * lin_out).astype(jnp.bfloat16)
    return hidden, state_new


def solution(mesh):
    seq_shards = mesh.shape['sp']
    tp_size = mesh.shape['tp']

    def device_step(tokens, states, k_cache, v_cache, slopes, lin_gain, w_lin_qkv, w_lin_gate, out_gain, w_lin_out, attn_gain, w_attn_in, w_attn_out):
        rows = tokens.shape[0]
        kv_dev = k_cache.shape[1]
        shard_len = k_cache.shape[2]
        head_dim = k_cache.shape[3]
        group = w_attn_in.shape[2] - 2
        prompt_len = seq_shards * shard_len
        k_moved = lax.all_to_all(k_cache, 'sp', 0, 2, tiled=True)
        v_moved = lax.all_to_all(v_cache, 'sp', 0, 2, tiled=True)
        shard_idx = lax.axis_index('sp')
        offset = (shard_len * (seq_shards - 1 - shard_idx)).astype(jnp.float32)
        weighted = states[0] * jnp.exp(-slopes * offset)[None, :, None, None]
        moved_state = lax.psum_scatter(weighted, 'sp', scatter_dimension=0, tiled=True)
        hidden, state_new = lightning_layer(tokens, moved_state, slopes, lin_gain, w_lin_qkv, w_lin_gate, out_gain, w_lin_out, tp_size * slopes.shape[0] * head_dim)

        normed = rms_norm(hidden, attn_gain).astype(jnp.bfloat16)
        attn_proj = jnp.einsum('bd,dkjn->bkjn', normed, w_attn_in, preferred_element_type=jnp.float32).astype(jnp.bfloat16)
        query_rot = rotary(attn_proj[:, :, :group], prompt_len)
        key_new = rotary(attn_proj[:, :, group], prompt_len)
        value_new = attn_proj[:, :, group + 1]
        score_scale = head_dim ** -0.5
        scores = jnp.einsum('bkgd,bktd->bkgt', query_rot, k_moved, preferred_element_type=jnp.float32) * score_scale
        new_score = jnp.einsum('clhe,cle->clh', query_rot, key_new, preferred_element_type=jnp.float32) * score_scale
        row_max = jnp.maximum(jnp.max(scores, axis=-1), new_score)
        probs = jnp.exp(scores - row_max[..., None])
        new_prob = jnp.exp(new_score - row_max)
        prob_sum = jnp.sum(probs, axis=-1) + new_prob
        weighted_sum = jnp.einsum('bkgt,bktd->bkgd', probs.astype(jnp.bfloat16), v_moved, preferred_element_type=jnp.float32)
        weighted_sum = weighted_sum + new_prob.astype(jnp.bfloat16).astype(jnp.float32)[..., None] * value_new.astype(jnp.float32)[:, :, None, :]
        head_out = (weighted_sum / prob_sum[..., None]).astype(jnp.bfloat16).reshape(rows, kv_dev * group * head_dim)
        attn_out = lax.psum(jnp.dot(head_out, w_attn_out, preferred_element_type=jnp.float32), 'tp')
        hidden_out = (RES_ALPHA * normed.astype(jnp.float32) + RES_BETA * attn_out).astype(jnp.bfloat16)
        tail_zeros = jnp.zeros((rows, kv_dev, CACHE_EXTRA - 1, head_dim), jnp.bfloat16)
        k_out = jnp.concatenate([k_moved, key_new[:, :, None, :], tail_zeros], axis=2)
        v_out = jnp.concatenate([v_moved, value_new[:, :, None, :], tail_zeros], axis=2)
        return hidden_out, state_new, k_out, v_out

    batch_spec = P(('dp', 'sp'), None)
    head_spec = P(('dp', 'sp'), 'tp', None, None)
    cache_spec = P('dp', 'tp', 'sp', None)
    in_specs = (batch_spec, P('sp', 'dp', 'tp', None, None), cache_spec, cache_spec, P('tp'), P(None), P(None, None, 'tp'), P(None, 'tp'), P('tp'), P('tp', None), P(None), P(None, 'tp', None, None), P('tp', None))
    out_specs = (batch_spec, head_spec, head_spec, head_spec)
    return jax.shard_map(device_step, mesh=mesh, in_specs=in_specs, out_specs=out_specs, check_vma=False)
```

profile of v0, /device:TPU:0, one launch (start us, length us, event | category | flops | bytes accessed | tf_op | source)
XLA Modules:
  0.0 813.8 jit_solution(11903975042135992757)
XLA Ops:
  7.2 0.7 negate_exponential_fusion
  7.9 23.9 %bitcast_multiply_fusion = f32[16,32,128,128]{3,2,1,0:T(8,128)} fusion(f32[1,16,32,128,128]{4,3,2,1,0:T(8,128)} %param.14, f32[32]{0:T(128)S(1)} %get-tuple-element.17), kind=kLoop, calls=%fused_computation.2 | loop fusion | flops 8388608 | bytes 67108992 | tf_op jit(solution)/shard_map/mul | solution.py:65
  31.8 7.2 all-to-all-start
  39.2 324.0 %all-to-all-done = bf16[16,4,1024,128]{3,2,1,0:T(8,128)(2,1)} async-done(((bf16[16,4,1024,128]{3,2,1,0:T(8,128)(2,1)}), bf16[16,4,1024,128]{3,2,1,0:T(8,128)(2,1)}, u32[]{:S(2)}, u32[]{:S(2)}) %all-to-all-start) | async-done | bytes 16777248 | tf_op jit(solution)/shard_map/all_to_all | solution.py:61
  363.2 7.1 all-to-all-start.1
  370.4 48.0 %fusion.18 = bf16[4,3,4096]{2,0,1:T(4,128)(2,1)S(1)} fusion(bf16[6144,3,4096]{2,0,1:T(8,128)(2,1)} %param.19, bf16[4,6144]{1,0:T(4,128)(2,1)S(1)} %copy-done.1, f32[6144]{0:T(1024)S(1)} %copy-done.2, f32[4]{0:T(128)S(1)} %add_rsqrt_fusion.1), kind=kOutput, calls=%fused_computation.22 | convolution fusion | flops 604323840 | bytes 151166992 | tf_op jit(solution)/shard_map/bd,dkn->bkn/dot_general | solution.py:37
  418.5 14.6 %reduce-scatter.2.cloned.1.call-done = f32[4,32,128,128]{3,2,1,0:T(8,128)} async-done(((f32[16,32,128,128]{3,2,1,0:T(8,128)}), f32[4,32,128,128]{3,2,1,0:T(8,128)}) %reduce-scatter.2.cloned.1.call-update) | async-done | bytes 8388624 | tf_op jit(solution)/shard_map/reduce_scatter | solution.py:66
  433.1 5.3 multiply_add_fusion
  438.4 3.4 copy-done
  441.8 1.2 fusion.28
  443.1 4.9 psum.21
  448.1 34.4 %fusion.7 = f32[4,6144]{1,0:T(4,128)} fusion(bf16[4096,6144]{1,0:T(8,128)(2,1)} %param.22, bf16[6144,4096]{1,0:T(8,128)(2,1)} %param.20, f32[1,4,32,128]{3,2,1,0:T(8,128)S(1)} %bitcast.83, f32[4096]{0:T(1024)S(1)} %copy-done.3, f32[4]{0:T(128)S(1)} %rsqrt_bitcast_fusion, bf16[4,6144]{1,0:T(4,128)(2,1)S(1)} %copy-done.1, f32[6144]{0:T(1024)S(1)} %copy-done.2, ...), kind=kOutput, calls=%fused_computation.11 | convolution fusion | flops 402866176 | bytes 100917280 | tf_op jit(solution)/shard_map/dot_general | solution.py:45
  482.7 13.9 %copy.25 = bf16[4,4,4,1024,128]{4,3,0,2,1:T(8,128)(2,1)} copy(bf16[4,4,4,1024,128]{4,3,2,1,0:T(8,128)(2,1)} %bitcast.12) | data formatting | bytes 33554432 | tf_op jit(solution)/shard_map/all_to_all | solution.py:61
  496.6 85.6 %all-to-all-done.1 = bf16[16,4,1024,128]{3,2,1,0:T(8,128)(2,1)} async-done(((bf16[16,4,1024,128]{3,2,1,0:T(8,128)(2,1)}), bf16[16,4,1024,128]{3,2,1,0:T(8,128)(2,1)}, u32[]{:S(2)}, u32[]{:S(2)}) %all-to-all-start.1) | async-done | bytes 16777248 | tf_op jit(solution)/shard_map/all_to_all | solution.py:62
  582.2 13.8 %copy.27 = bf16[4,4,4,1024,128]{4,3,0,2,1:T(8,128)(2,1)} copy(bf16[4,4,4,1024,128]{4,3,2,1,0:T(8,128)(2,1)} %bitcast.20) | data formatting | bytes 33554432 | tf_op jit(solution)/shard_map/all_to_all | solution.py:62
  596.0 1.1 fusion.22
  597.2 1.0 fusion.24
  598.2 30.3 %fusion.11 = bf16[4,4,10,128]{3,0,2,1:T(4,128)(2,1)S(1)} fusion(bf16[6144,4,10,128]{3,1,2,0:T(4,128)(2,1)} %param.24, bf16[4,6144]{1,0:T(4,128)(2,1)S(1)} %fusion.24), kind=kOutput, calls=%fused_computation.17 | convolution fusion | flops 251678720 | bytes 63004672 | tf_op jit(solution)/shard_map/bd,dkjn->bkjn/dot_general | solution.py:70
  629.3 8.1 fusion.53
  637.9 7.1 fusion.15
  645.0 19.6 %fusion.32 = f32[4,6144]{1,0:T(4,128)} fusion(bf16[4096,6144]{1,0:T(8,128)(2,1)} %param.25, bf16[1,4,32,128]{3,2,1,0:T(8,128)(2,1)S(1)} %fusion.15), kind=kOutput, calls=%fused_computation.45 | convolution fusion | flops 201326592 | bytes 50462720 | tf_op jit(solution)/shard_map/dot_general | solution.py:84
  664.8 70.5 %concatenate.36 = bf16[4,4,4112,128]{3,2,1,0:T(8,128)(2,1)} concatenate(bf16[4,4,4096,128]{3,2,1,0:T(8,128)(2,1)} %bitcast.79, bf16[4,4,1,128]{3,2,1,0:T(2,128)(2,1)S(1)} %copy.29, bf16[4,4,15,128]{3,2,1,0:T(8,128)(2,1)S(1)} %broadcast_in_dim.5), dimensions={2} | concatenate | bytes 33685504 | tf_op jit(solution)/shard_map/concatenate | solution.py:87
  735.2 70.5 %concatenate.37 = bf16[4,4,4112,128]{3,2,1,0:T(8,128)(2,1)} concatenate(bf16[4,4,4096,128]{3,2,1,0:T(8,128)(2,1)} %bitcast.81, bf16[4,4,1,128]{3,2,1,0:T(2,128)(2,1)S(1)} %copy.30, bf16[4,4,15,128]{3,2,1,0:T(8,128)(2,1)S(1)} %broadcast_in_dim.5), dimensions={2} | concatenate | bytes 33685504 | tf_op jit(solution)/shard_map/concatenate | solution.py:88
  805.7 1.5 add_convert_fusion
  (43 shorter events, 2.2 us)
Async XLA Ops:
  7.2 425.9 %reduce-scatter.2.cloned.1.call-start = ((), (), s32[]{:S(2)}) async-start(), calls=%async_computation.3 | async-start | bytes 41943040 | tf_op jit(solution)/shard_map/reduce_scatter | solution.py:66
  31.8 7.2 copy-start.1
  31.8 331.4 %all-to-all-start = ((bf16[16,4,1024,128]{3,2,1,0:T(8,128)(2,1)}), bf16[16,4,1024,128]{3,2,1,0:T(8,128)(2,1)}, u32[]{:S(2)}, u32[]{:S(2)}) async-start(bf16[16,4,1024,128]{3,2,1,0:T(8,128)(2,1)} %param.15), calls=%async_computation.1 | async-start | bytes 33554432 | tf_op jit(solution)/shard_map/all_to_all | solution.py:61
  39.2 331.1 %copy-start.2 = (f32[6144]{0:T(1024)S(1)}, f32[6144]{0:T(1024)}, u32[]{:S(2)}) copy-start(f32[6144]{0:T(1024)} %param.18) | copy-start | bytes 73732
  363.2 219.0 %all-to-all-start.1 = ((bf16[16,4,1024,128]{3,2,1,0:T(8,128)(2,1)}), bf16[16,4,1024,128]{3,2,1,0:T(8,128)(2,1)}, u32[]{:S(2)}, u32[]{:S(2)}) async-start(bf16[16,4,1024,128]{3,2,1,0:T(8,128)(2,1)} %param.16), calls=%async_computation.2 | async-start | bytes 33554432 | tf_op jit(solution)/shard_map/all_to_all | solution.py:62
  370.3 225.8 %all-reduce.3.cloned.1.call-start = ((), (), s32[]{:S(2)}) async-start(), calls=%async_computation.4 | async-start | bytes 196608 | tf_op jit(solution)/shard_map/psum | solution.py:45
  418.3 29.7 %copy-start.3 = (f32[4096]{0:T(1024)S(1)}, f32[4096]{0:T(1024)}, u32[]{:S(2)}) copy-start(f32[4096]{0:T(1024)} %param.21) | copy-start | bytes 49156
  438.4 3.4 copy-start
  482.4 323.2 %all-reduce.5.cloned.1.call-start = ((), (), s32[]{:S(2)}) async-start(), calls=%async_computation.5 | async-start | bytes 196608 | tf_op jit(solution)/shard_map/psum | solution.py:84
  582.2 15.0 %copy-start.4 = (f32[6144]{0:T(1024)S(1)}, f32[6144]{0:T(1024)}, u32[]{:S(2)}) copy-start(f32[6144]{0:T(1024)} %param.23) | copy-start | bytes 73732
Sparse Core Ops, SparseCore 0:
  31.9 401.1 reduce-scatter.1
  482.6 15.7 all-reduce.2
  664.7 16.4 all-reduce.4
where the time goes:
time: 818 us; the launch traced here: 814 us
  waiting for transfers between devices  424 us (52%)
  local copies, waits for them, and re-layouts  172 us (21%)
  matrix products  149 us (18%)
  other arithmetic  34.9 us (4%)
  starting transfers between devices  14.6 us (2%)
  between operations  13.9 us (2%)
    all_to_all x1, waiting for transfers between devices, device_step(): k_moved = lax.all_to_all(k_cache, 'sp', 0, 2, tiled=True)  324 us
    all_to_all x1, waiting for transfers between devices, device_step(): v_moved = lax.all_to_all(v_cache, 'sp', 0, 2, tiled=True)  85.6 us
    concatenate x1, local copies, waits for them, and re-layouts, device_step(): jnp.concatenate([k_moved, key_new[:, :, None, :], tail_zeros], axis=2)  70.5 us
    concatenate x1, local copies, waits for them, and re-layouts, device_step(): jnp.concatenate([v_moved, value_new[:, :, None, :], tail_zeros], axis=2)  70.5 us
    dot_general x1, matrix products, lightning_layer(): jnp.einsum('bd,dkn->bkn', normed, w_lin_qkv, preferred_element_type=jnp.f...  48 us
    dot_general x1, matrix products, lightning_layer(): jnp.dot(mixed_out, w_lin_out, preferred_element_type=jnp.float32)  34.4 us
    dot_general x1, matrix products, device_step(): jnp.einsum('bd,dkjn->bkjn', normed, w_attn_in, preferred_element_type=jnp...  30.3 us
    mul x1, other arithmetic, device_step(): weighted = states[0] * jnp.exp(-slopes * offset)[None, :, None, None]  23.9 us
  transfers between devices with their start and end apart: 5, of which 3 were waited for; matrix products, arithmetic and copies ran while one was open for 32% of the time, Pallas kernels for 0%

commit v1 on v0

v1 whole, which is shorter than its diff:
```python
import jax
import jax.numpy as jnp
from jax import lax
from jax.experimental import pallas as pl
from jax.experimental.pallas import tpu as pltpu
from jax.sharding import PartitionSpec as P


NORM_EPS = 1e-6
ROPE_BASE = 10000000.0
RES_ALPHA = 1.0
RES_BETA = 1.0
CACHE_EXTRA = 16


F32 = jnp.float32
BF16 = jnp.bfloat16


def rms_norm(vals_in, gain_vec):
    vals32 = vals_in.astype(F32)
    inv_rms = lax.rsqrt(jnp.mean(vals32 * vals32, axis=-1, keepdims=True) + NORM_EPS)
    return vals32 * inv_rms * gain_vec


def rotary(vals_in, position):
    rope_dim = vals_in.shape[-1] // 2
    half_dim = rope_dim // 2
    inv_freq = ROPE_BASE ** (-jnp.arange(0, rope_dim, 2, dtype=F32) / rope_dim)
    angles = position * inv_freq
    cosine = jnp.cos(angles)
    sine_vals = jnp.sin(angles)
    vals32 = vals_in.astype(F32)
    first_half = vals32[..., :half_dim]
    second_half = vals32[..., half_dim:rope_dim]
    return jnp.concatenate([first_half * cosine - second_half * sine_vals, second_half * cosine + first_half * sine_vals, vals32[..., rope_dim:]], axis=-1).astype(BF16)


def merge(out_a, stats_a, out_b, stats_b):
    top = jnp.maximum(stats_a[:, 0], stats_b[:, 0])
    scale_a = jnp.exp(stats_a[:, 0] - top)
    scale_b = jnp.exp(stats_b[:, 0] - top)
    total = stats_a[:, 1] * scale_a + stats_b[:, 1] * scale_b
    return out_a * scale_a[..., None] + out_b * scale_b[..., None], jnp.stack([top, total], axis=1)


def pack(out, stats):
    rows, _, heads, group = stats.shape
    tail = jnp.transpose(stats, (2, 3, 0, 1)).reshape(1, heads, group, 2 * rows)
    return jnp.concatenate([out, jnp.pad(tail, ((0, 0), (0, 0), (0, 0), (0, out.shape[-1] - 2 * rows)))])


def unpack(packed):
    rows, heads, group = packed.shape[0] - 1, packed.shape[1], packed.shape[2]
    tail = packed[rows, :, :, :2 * rows].reshape(heads, group, rows, 2)
    return packed[:rows], jnp.transpose(tail, (2, 3, 0, 1))


def place_last_block(src_ref, total_ref, out_ref, buf, in_sems, out_sems):
    heads, length = src_ref.shape[1], src_ref.shape[2]
    row = out_ref.shape[0] - 1
    pos = pl.multiple_of((3 - lax.axis_index('sp')) * length, length)
    reads = [pltpu.make_async_copy(src_ref.at[0, j], buf.at[j], in_sems.at[j]) for j in range(heads)]
    writes = [pltpu.make_async_copy(buf.at[j], out_ref.at[row, j, pl.ds(pos, length)], out_sems.at[j]) for j in range(heads)]
    for copy in reads:
        copy.start()
    for read, write in zip(reads, writes):
        read.wait()
        write.start()
    for copy in writes:
        copy.wait()


def place_last(total, block):
    heads, length, dim = block.shape[1:]
    return pl.pallas_call(
        place_last_block,
        in_specs=[pl.BlockSpec(memory_space=pl.ANY), pl.BlockSpec(memory_space=pl.ANY)],
        out_specs=pl.BlockSpec(memory_space=pl.ANY),
        out_shape=jax.ShapeDtypeStruct(total.shape, total.dtype),
        scratch_shapes=[pltpu.VMEM((heads, length, dim), block.dtype), pltpu.SemaphoreType.DMA((heads,)), pltpu.SemaphoreType.DMA((heads,))],
        input_output_aliases={1: 0},
        compiler_params=pltpu.CompilerParams(vmem_limit_bytes=67043328),
        name="place_last",
    )(block, total)


def copy_block(_, src_ref, *refs):
    refs[-1][...] = src_ref[...]


def place(total, block, first, pos_block, out_shape, count=None, out_first=0):
    rows, heads, _, dim = out_shape
    length = block.shape[2]
    if length > CACHE_EXTRA:
        count = rows if count is None else count
        grid, shape = (count, heads // 2), (1, 2, length, dim)
    else:
        count, grid, shape = rows, (1, 1), (rows, heads, length, dim)
    scalars = jnp.stack([jnp.asarray(first, jnp.int32), jnp.asarray(pos_block, jnp.int32)])
    in_specs = [pl.BlockSpec(shape, lambda i, j, s: (s[0] + i, j, 0, 0))]
    operands = [scalars, block]
    aliases = {}
    if total is not None:
        in_specs.append(pl.BlockSpec(memory_space=pl.ANY))
        operands.append(total)
        aliases = {2: 0}
    nbytes = 2 * count * heads * length * dim * 2
    return pl.pallas_call(
        copy_block,
        grid_spec=pltpu.PrefetchScalarGridSpec(
            num_scalar_prefetch=1,
            grid=grid,
            in_specs=in_specs,
            out_specs=pl.BlockSpec(shape, lambda i, j, s: (out_first + i, j, s[1], 0)),
        ),
        out_shape=jax.ShapeDtypeStruct(out_shape, block.dtype),
        input_output_aliases=aliases,
        compiler_params=pltpu.CompilerParams(vmem_limit_bytes=67043328),
        cost_estimate=pl.CostEstimate(flops=nbytes * 30, bytes_accessed=nbytes, transcendentals=0),
        name="place",
    )(*operands)


def solution(mesh):
    seq_shards = mesh.shape['sp']
    tp_size = mesh.shape['tp']

    def send(value, mask):
        return lax.ppermute(value, 'sp', [(i, i ^ mask) for i in range(seq_shards)])

    def tp_sum(value):
        return value + lax.ppermute(value, 'tp', [(0, 1), (1, 0)])

    def step(tokens, states, k_cache, v_cache, slopes, lin_gain, w_lin_qkv, w_lin_gate, out_gain, w_lin_out, attn_gain, w_attn_in, w_attn_out):
        rows = tokens.shape[0]
        kv_dev = k_cache.shape[1]
        shard_len = k_cache.shape[2]
        head_dim = k_cache.shape[3]
        group = w_attn_in.shape[2] - 2
        heads_dev = slopes.shape[0]
        prompt_len = seq_shards * shard_len
        me = lax.axis_index('sp')

        def rows_of(value, mask, first=0, count=rows):
            return lax.dynamic_slice_in_dim(value, rows * (me ^ mask) + first, count, 0)

        kx0_rows = rows_of(k_cache, 2, 0, 1)
        kx0 = send(kx0_rows, 2)
        k_src, slopes_a = lax.optimization_barrier((k_cache, slopes, kx0_rows))[:2]
        kx1_rows = rows_of(k_src, 2, 1, rows - 1)
        kx1 = send(kx1_rows, 2)

        own = states[0]
        offset = (shard_len * (seq_shards - 1 - me)).astype(F32)
        decay = jnp.exp(-slopes_a * offset)[None, :, None, None]
        sa_rows = rows_of(own, 3) * decay
        sb_rows = rows_of(own, 1) * decay
        sa = send(sa_rows, 1)
        sb = send(sb_rows, 1)

        normed = rms_norm(tokens, lin_gain).astype(BF16)
        lin_proj = jnp.einsum('bd,dkn->bkn', normed, w_lin_qkv, preferred_element_type=F32)
        act_vals = jax.nn.silu(lin_proj).astype(BF16).reshape(rows, 3, heads_dev, head_dim)

        part_x = rows_of(own, 2) * decay + sa
        sx = send(part_x, 2)

        k_src, v_src, _ = lax.optimization_barrier((k_cache, v_cache, part_x))
        ky_rows = rows_of(k_src, 3)
        kd_rows = rows_of(k_src, 1)
        vd_rows = rows_of(v_src, 1)
        vx_rows = rows_of(v_src, 2)
        vy0_rows = rows_of(v_src, 3, 0, rows - 1)
        vy1_rows = rows_of(v_src, 3, rows - 1, 1)
        ky = send(ky_rows, 3)
        kd = send(kd_rows, 1)
        vd = send(vd_rows, 1)

        gate_vals = jax.nn.sigmoid(jnp.dot(normed, w_lin_gate, preferred_element_type=F32))
        gate_vals = lax.optimization_barrier(gate_vals)

        moved_state = rows_of(own, 0) * decay + sb + sx
        state_new = jnp.exp(-slopes)[None, :, None, None] * moved_state + jnp.einsum('bhd,bhe->bhde', act_vals[:, 1], act_vals[:, 2], preferred_element_type=F32)
        lin_attn = jnp.einsum('bhd,bhde->bhe', act_vals[:, 0].astype(F32), state_new).reshape(rows, heads_dev * head_dim)
        square_sum = tp_sum(jnp.sum(lin_attn * lin_attn, axis=-1, keepdims=True))
        inv_rms = lax.rsqrt(square_sum / (tp_size * heads_dev * head_dim) + NORM_EPS)
        mixed_out = (lin_attn * inv_rms * out_gain * gate_vals).astype(BF16)
        lin_out = jnp.dot(mixed_out, w_lin_out, preferred_element_type=F32)
        lin_out = tp_sum(lin_out)
        hidden = (RES_ALPHA * normed.astype(F32) + RES_BETA * lin_out).astype(BF16)
        normed_two = rms_norm(hidden, attn_gain).astype(BF16)
        attn_proj = jnp.einsum('bd,dkjn->bkjn', normed_two, w_attn_in, preferred_element_type=F32).astype(BF16)
        query_rot = rotary(attn_proj[:, :, :group], prompt_len)
        key_new = rotary(attn_proj[:, :, group], prompt_len)
        value_new = attn_proj[:, :, group + 1]

        qx = send(query_rot, 2)
        vx = send(vx_rows, 2)
        qd = send(jnp.stack([query_rot, qx]), 1)

        score_scale = head_dim ** -0.5
        order = jnp.arange(seq_shards) ^ me
        query_all = jnp.take(jnp.stack([query_rot, qd[0], qx, qd[1]]), order, axis=0).reshape(seq_shards * rows, kv_dev, group, head_dim)
        scores = jnp.einsum('bkgd,bktd->bkgt', query_all, k_cache, preferred_element_type=F32) * score_scale
        part_max = jnp.max(scores, axis=-1)
        probs = jnp.exp(scores - part_max[..., None])
        part_sum = jnp.sum(probs, axis=-1)
        part_out = jnp.einsum('bkgt,bktd->bkgd', probs.astype(BF16), v_cache, preferred_element_type=F32)
        stats = jnp.stack([part_max, part_sum], axis=1)

        pair = pack(jnp.concatenate([rows_of(part_out, 3), rows_of(part_out, 1)]), jnp.concatenate([rows_of(stats, 3), rows_of(stats, 1)]))
        pair_out, pair_stats = unpack(send(pair, 1))
        far = pack(*merge(rows_of(part_out, 2), rows_of(stats, 2), pair_out[:rows], pair_stats[:rows]))
        ax, axs = unpack(send(far, 2))
        vy0 = send(vy0_rows, 3)
        vy1 = send(vy1_rows, 3)

        near_out, near_stats = merge(rows_of(part_out, 0), rows_of(stats, 0), pair_out[rows:], pair_stats[rows:])
        all_out, all_stats = merge(near_out, near_stats, ax, axs)
        new_score = jnp.einsum('clhe,cle->clh', query_rot, key_new, preferred_element_type=F32) * score_scale
        row_max = jnp.maximum(all_stats[:, 0], new_score)
        scale = jnp.exp(all_stats[:, 0] - row_max)
        new_prob = jnp.exp(new_score - row_max)
        prob_sum = all_stats[:, 1] * scale + new_prob
        weighted_sum = all_out * scale[..., None]
        weighted_sum = weighted_sum + new_prob.astype(BF16).astype(F32)[..., None] * value_new.astype(F32)[:, :, None, :]
        head_out = (weighted_sum / prob_sum[..., None]).astype(BF16).reshape(rows, kv_dev * group * head_dim)
        attn_out = jnp.dot(head_out, w_attn_out, preferred_element_type=F32)
        attn_out = tp_sum(attn_out)
        hidden_out = (RES_ALPHA * normed_two.astype(F32) + RES_BETA * attn_out).astype(BF16)

        out_shape = (rows, kv_dev, prompt_len + CACHE_EXTRA, head_dim)
        tail_zeros = jnp.zeros((rows, kv_dev, CACHE_EXTRA - 1, head_dim), BF16)
        late, _ = lax.optimization_barrier((me, part_x))

        def add_tail(total, new_row):
            tail = jnp.concatenate([new_row[:, :, None, :], tail_zeros], axis=2)
            return place(total, tail, 0, prompt_len // CACHE_EXTRA, out_shape)

        k_out = place(None, k_cache, late * rows, late, out_shape)
        k_out = place(k_out, kd, 0, me ^ 1, out_shape)
        v_out = place(None, v_cache, late * rows, late, out_shape)
        v_out = place(v_out, vd, 0, me ^ 1, out_shape)
        k_out = place(k_out, kx0, 0, me ^ 2, out_shape, 1, 0)
        k_out = place(k_out, kx1, 0, me ^ 2, out_shape, rows - 1, 1)
        k_out = add_tail(k_out, key_new)
        v_out = add_tail(v_out, value_new)
        k_out = place(k_out, ky, 0, me ^ 3, out_shape)
        v_out = place(v_out, vx, 0, me ^ 2, out_shape)
        v_out = place(v_out, vy0, 0, me ^ 3, out_shape, rows - 1, 0)
        v_out = place_last(v_out, vy1)
        return hidden_out, state_new, k_out, v_out

    batch_spec = P(('dp', 'sp'), None)
    head_spec = P(('dp', 'sp'), 'tp', None, None)
    cache_spec = P('dp', 'tp', 'sp', None)
    in_specs = (batch_spec, P('sp', 'dp', 'tp', None, None), cache_spec, cache_spec, P('tp'), P(None), P(None, None, 'tp'), P(None, 'tp'), P('tp'), P('tp', None), P(None), P(None, 'tp', None, None), P('tp', None))
    out_specs = (batch_spec, head_spec, head_spec, head_spec)
    return jax.shard_map(step, mesh=mesh, in_specs=in_specs, out_specs=out_specs, check_vma=False)
```

time: 818 us -> 692 us (0.85)
  local copies, waits for them, and re-layouts: 172 us -> 34.1 us
  Pallas kernels: 0 us -> 64.8 us
  waiting for transfers between devices: 424 us -> 377 us
  between operations: 13.9 us -> 1.06 us
  other arithmetic: 34.9 us -> 43.2 us
    all_to_all x2 -> x0, waiting for transfers between devices: 410 us -> none  [the longest x1 324 us: device_step(): k_moved = lax.all_to_all(k_cache, 'sp', 0, 2, tiled=True)]
    ppermute x0 -> x18, waiting for transfers between devices: none -> 377 us  [the longest x15 375 us: send(): return lax.ppermute(value, 'sp', [(i, i ^ mask) for i in range(seq_shards)])]
    concatenate x2, local copies, waits for them, and re-layouts: 141 us -> 1.27 us  [add_tail(): tail = jnp.concatenate([new_row[:, :, None, :], tail_zeros], axis=2)]
    pallas_call x0 -> x12, Pallas kernels: none -> 64.8 us  [the longest x11 62.8 us: place(): pl.pallas_call(copy_block, grid_spec=pltpu.PrefetchScalarGridSpec(num_sca...]
    all_to_all x2 -> x0, local copies, waits for them, and re-layouts: 27.7 us -> none  [the longest x1 13.9 us: device_step(): k_moved = lax.all_to_all(k_cache, 'sp', 0, 2, tiled=True)]
    dynamic_slice x0 -> x7, local copies, waits for them, and re-layouts: none -> 27.3 us  [rows_of(): return lax.dynamic_slice_in_dim(value, rows * (me ^ mask) + first, count, 0)]
    add x1 -> x5, other arithmetic: 5.32 us -> 22.4 us  [the longest x1 12.2 us: step(): part_x = rows_of(own, 2) * decay + sa]
    ppermute x0 -> x18, starting transfers between devices: none -> 16.8 us  [the longest x15 12.7 us: send(): return lax.ppermute(value, 'sp', [(i, i ^ mask) for i in range(seq_shards)])]
  transfers between devices with their start and end apart: 5 -> 18, of which waited for: 3 -> 7; matrix products, arithmetic and copies ran while one was open for 32% -> 31% of each run, Pallas kernels for 0% -> 9%
where the time goes in v1:
time: 692 us; the launch traced here: 690 us
  waiting for transfers between devices  377 us (54%)
  matrix products  153 us (22%)
  Pallas kernels  64.8 us (9%)
  other arithmetic  43.2 us (6%)
  local copies, waits for them, and re-layouts  34.1 us (5%)
  starting transfers between devices  16.8 us (2%)
    ppermute x15, waiting for transfers between devices, send(): return lax.ppermute(value, 'sp', [(i, i ^ mask) for i in range(seq_shards)])  375 us
    pallas_call x11, Pallas kernels, place(): pl.pallas_call(copy_block, grid_spec=pltpu.PrefetchScalarGridSpec(num_sca...  62.8 us
    dot_general x1, matrix products, step(): jnp.einsum('bd,dkn->bkn', normed, w_lin_qkv, preferred_element_type=F32)  48.1 us
    dot_general x1, matrix products, step(): jnp.einsum('bd,dkjn->bkjn', normed_two, w_attn_in, preferred_element_type...  30.7 us
    dynamic_slice x7, local copies, waits for them, and re-layouts, rows_of(): return lax.dynamic_slice_in_dim(value, rows * (me ^ mask) + first, count, 0)  27.3 us
    dot_general x1, matrix products, step(): attn_out = jnp.dot(head_out, w_attn_out, preferred_element_type=F32)  19.7 us
    dot_general x1, matrix products, step(): lin_out = jnp.dot(mixed_out, w_lin_out, preferred_element_type=F32)  19.5 us
    dot_general x1, matrix products, step(): jnp.dot(normed, w_lin_gate, preferred_element_type=F32)  18.9 us
  transfers between devices with their start and end apart: 18, of which 7 were waited for; matrix products, arithmetic and copies ran while one was open for 31% of the time, Pallas kernels for 9%

profile of v1, /device:TPU:0, one launch (start us, length us, event | category | flops | bytes accessed | tf_op | source)
XLA Modules:
  0.0 689.9 jit_solution(1602704676755560834)
XLA Ops:
  3.6 11.1 %bitcast_multiply_fusion.2 = (f32[4,32,128,128]{3,2,1,0:T(8,128)}, f32[4,32,128,128]{3,2,1,0:T(8,128)}) fusion(f32[1,16,32,128,128]{4,3,2,1,0:T(8,128)} %param.14, s32[]{:T(128)S(6)} %select_n.55, f32[32]{0:T(128)S(1)} %multiply_exponential_fusion, s32[]{:T(128)S(6)} %select_n.56), kind=kLoop, calls=%fused_computation.6 | loop fusion | flops 4194304 | bytes 33554568 | tf_op jit(solution)/shard_map/mul | solution.py:158
  22.4 6.2 collective-permute-done.1
  28.7 12.2 %fusion.2 = f32[4,32,128,128]{3,2,1,0:T(8,128)} fusion(f32[4,32,128,128]{3,2,1,0:T(8,128)} %collective-permute-done.1, f32[1,16,32,128,128]{4,3,2,1,0:T(8,128)} %param.14, s32[]{:T(128)S(6)} %select_n.54, f32[32]{0:T(128)S(1)} %multiply_exponential_fusion), kind=kLoop, calls=%fused_computation.5 | loop fusion | flops 4194304 | bytes 25165956 | tf_op jit(solution)/shard_map/add | solution.py:166
  43.7 48.1 %fusion.16 = bf16[4,3,4096]{2,0,1:T(4,128)(2,1)S(1)} fusion(bf16[6144,3,4096]{2,0,1:T(8,128)(2,1)} %param.19, bf16[4,6144]{1,0:T(4,128)(2,1)S(1)} %copy-done.1, f32[6144]{0:T(1024)S(1)} %copy-done.2, f32[4]{0:T(128)S(1)} %add_rsqrt_fusion.1), kind=kOutput, calls=%fused_computation.24 | convolution fusion | flops 604323840 | bytes 151166992 | tf_op jit(solution)/shard_map/bd,dkn->bkn/dot_general | solution.py:163
  91.9 18.9 %fusion.9 = f32[4,4096]{1,0:T(4,128)S(1)} fusion(bf16[6144,4096]{1,0:T(8,128)(2,1)} %param.20, bf16[4,6144]{1,0:T(4,128)(2,1)S(1)} %copy-done.1, f32[6144]{0:T(1024)S(1)} %copy-done.2, f32[4]{0:T(128)S(1)} %add_rsqrt_fusion.1), kind=kOutput, calls=%fused_computation.15 | convolution fusion | flops 201474048 | bytes 50470928 | tf_op jit(solution)/shard_map/dot_general | solution.py:180
  115.3 7.6 %constant_dynamic-slice_fusion = (bf16[4,4,1024,128]{3,2,1,0:T(8,128)(2,1)}, bf16[4,4,1024,128]{3,2,1,0:T(8,128)(2,1)}) fusion(bf16[16,4,1024,128]{3,2,1,0:T(8,128)(2,1)} %src_ref.3, s32[]{:T(128)S(6)} %select_n.55, s32[]{:T(128)S(6)} %select_n.54), kind=kLoop, calls=%fused_computation.133 | loop fusion | bytes 16777224 | tf_op jit(solution)/shard_map/dynamic_slice | solution.py:146
  125.8 3.7 constant_dynamic-slice_fusion.2
  129.5 7.7 %constant_dynamic-slice_fusion.4 = (bf16[4,4,1024,128]{3,2,1,0:T(8,128)(2,1)}, bf16[4,4,1024,128]{3,2,1,0:T(8,128)(2,1)}) fusion(bf16[16,4,1024,128]{3,2,1,0:T(8,128)(2,1)} %src_ref.2, s32[]{:T(128)S(6)} %select_n.55, s32[]{:T(128)S(6)} %select_n.56), kind=kLoop, calls=%fused_computation.137 | loop fusion | bytes 16777224 | tf_op jit(solution)/shard_map/dynamic_slice | solution.py:146
  137.7 151.6 %collective-permute-done.2 = f32[4,32,128,128]{3,2,1,0:T(8,128)} collective-permute-done((f32[4,32,128,128]{3,2,1,0:T(8,128)}, f32[4,32,128,128]{3,2,1,0:T(8,128)}, u32[]{:S(2)}, u32[]{:S(2)}) %collective-permute-start.2) | collective-permute-done | bytes 8388640 | tf_op jit(solution)/shard_map/ppermute | solution.py:130
  289.3 10.0 %fusion.6 = f32[4,32,128,128]{3,2,1,0:T(8,128)S(1)} fusion(f32[4,32,128,128]{3,2,1,0:T(8,128)} %collective-permute-done.2, f32[4,32,128,128]{3,2,1,0:T(8,128)} %collective-permute-done, f32[1,16,32,128,128]{4,3,2,1,0:T(8,128)} %param.14, s32[]{:T(128)S(6)} %select_n.53, f32[4,32,128]{2,1,0:T(8,128)S(1)} %get-tuple-element.32, ...), kind=kLoop, calls=%fused_computation.11 | loop fusion | flops 12582912 | bytes 33685764 | tf_op jit(solution)/shard_map/add | solution.py:184
  307.6 19.5 %fusion.38 = f32[4,6144]{1,0:T(4,128)} fusion(bf16[4096,6144]{1,0:T(8,128)(2,1)} %param.22, f32[4,4096]{1,0:T(4,128)S(1)} %fusion.9, f32[1,4,32,128]{3,2,1,0:T(8,128)S(1)} %bitcast.180, f32[4096]{0:T(1024)S(1)} %copy-done.4, f32[4]{0:T(128)S(1)} %rsqrt_bitcast_fusion), kind=kOutput, calls=%fused_computation.76 | convolution fusion | flops 201392128 | bytes 50577424 | tf_op jit(solution)/shard_map/dot_general | solution.py:189
  328.9 7.3 %place.17.refs_0_ = bf16[4,4,4112,128]{3,2,1,0:T(8,128)(2,1)} custom-call(s32[2]{0:T(128)} %pad_add_fusion.3._, bf16[16,4,1024,128]{3,2,1,0:T(8,128)(2,1)} %src_ref.3), custom_call_target="tpu_custom_call" | custom-call | flops 251658240 | bytes 8388608 | tf_op jit(solution)/shard_map/place/pallas_call | solution.py:109
  336.2 7.3 %place.11.refs_0_ = bf16[4,4,4112,128]{3,2,1,0:T(8,128)(2,1)} custom-call(s32[2]{0:T(128)} %pad_add_fusion.3._, bf16[16,4,1024,128]{3,2,1,0:T(8,128)(2,1)} %src_ref.2), custom_call_target="tpu_custom_call" | custom-call | flops 251658240 | bytes 8388608 | tf_op jit(solution)/shard_map/place/pallas_call | solution.py:109
  345.0 7.3 %place.12.refs_0_ = bf16[4,4,4112,128]{3,2,1,0:T(8,128)(2,1)} custom-call(s32[2]{0:T(128)} %pad_add_fusion._, bf16[4,4,1024,128]{3,2,1,0:T(8,128)(2,1)} %collective-permute-done.13.src_ref, bf16[4,4,4112,128]{3,2,1,0:T(8,128)(2,1)} %place.11.refs_0_), custom_call_target="tpu_custom_call", output_to_operand_aliasing={{}: (2, {})} | custom-call | flops 251658240 | bytes 8388608 | tf_op jit(solution)/shard_map/place/pallas_call | solution.py:109
  356.8 6.0 place.14.refs_0_
  362.8 7.3 %place.18.refs_0_ = bf16[4,4,4112,128]{3,2,1,0:T(8,128)(2,1)} custom-call(s32[2]{0:T(128)} %pad_add_fusion._, bf16[4,4,1024,128]{3,2,1,0:T(8,128)(2,1)} %collective-permute-done.17.src_ref, bf16[4,4,4112,128]{3,2,1,0:T(8,128)(2,1)} %place.17.refs_0_), custom_call_target="tpu_custom_call", output_to_operand_aliasing={{}: (2, {})} | custom-call | flops 251658240 | bytes 8388608 | tf_op jit(solution)/shard_map/place/pallas_call | solution.py:109
  371.3 30.7 %fusion = bf16[4,4,10,128]{3,0,2,1:T(4,128)(2,1)S(1)} fusion(bf16[6144,4,10,128]{3,1,2,0:T(4,128)(2,1)} %param.24, bf16[4,6144]{1,0:T(4,128)(2,1)S(1)} %get-tuple-element.22, f32[6144]{0:T(1024)} %param.23, f32[4]{0:T(128)S(1)} %add_rsqrt_fusion), kind=kOutput, calls=%fused_computation.1 | convolution fusion | flops 251756544 | bytes 63029264 | tf_op jit(solution)/shard_map/bd,dkjn->bkjn/dot_general | solution.py:193
  403.2 211.7 %collective-permute-done.5 = bf16[4,4,8,128]{3,2,1,0:T(8,128)(2,1)S(1)} collective-permute-done((bf16[4,4,8,128]{3,2,1,0:T(8,128)(2,1)S(1)}, bf16[4,4,8,128]{3,2,1,0:T(8,128)(2,1)S(1)}, u32[]{:S(2)}, u32[]{:S(2)}) %collective-permute-start.5) | collective-permute-done | bytes 32800 | tf_op jit(solution)/shard_map/ppermute | solution.py:130
  617.2 8.1 %multiply_reduce_fusion = (f32[16,4,8]{2,1,0:T(4,128)S(1)}, f32[16,4,8,1024]{3,2,1,0:T(8,128)S(1)}) fusion(bf16[16,4,8,128]{3,2,1,0:T(8,128)(2,1)S(1)} %bitcast_select_fusion, bf16[16,4,1024,128]{3,2,1,0:T(8,128)(2,1)} %src_ref.2), kind=kOutput, calls=%fused_computation.17 | convolution fusion | flops 135265792 | bytes 19007488 | tf_op jit(solution)/shard_map/bkgd,bktd->bkgt/dot_general | solution.py:205
  625.3 7.0 %fusion.12 = f32[16,4,8,128]{3,2,1,0:T(8,128)S(1)} fusion(bf16[16,4,1024,128]{3,2,1,0:T(8,128)(2,1)} %src_ref.3, f32[16,4,8,1024]{3,2,1,0:T(8,128)S(1)} %get-tuple-element.55, f32[16,4,8]{2,1,0:T(4,128)S(1)} %get-tuple-element.54), kind=kOutput, calls=%fused_computation.20 | convolution fusion | flops 135790592 | bytes 19138560 | tf_op jit(solution)/shard_map/bkgt,bktd->bkgd/dot_general | solution.py:209
  639.7 19.7 %fusion.40 = f32[4,6144]{1,0:T(4,128)} fusion(bf16[4096,6144]{1,0:T(8,128)(2,1)} %param.25, bf16[1,4,32,128]{3,2,1,0:T(8,128)(2,1)S(1)} %fusion.47), kind=kOutput, calls=%fused_computation.77 | convolution fusion | flops 201326592 | bytes 50462720 | tf_op jit(solution)/shard_map/dot_general | solution.py:229
  663.5 7.3 %place.20.refs_0_ = bf16[4,4,4112,128]{3,2,1,0:T(8,128)(2,1)} custom-call(s32[2]{0:T(128)} %pad_add_fusion.1._, bf16[4,4,1024,128]{3,2,1,0:T(8,128)(2,1)} %collective-permute-done.16.src_ref, bf16[4,4,4112,128]{3,2,1,0:T(8,128)(2,1)} %place.19.refs_0_), custom_call_target="tpu_custom_call", output_to_operand_aliasing={{}: (2, {})} | custom-call | flops 251658240 | bytes 8388608 | tf_op jit(solution)/shard_map/place/pallas_call | solution.py:109
  670.8 6.0 place.21.total_ref
  680.9 7.3 %place.16 = bf16[4,4,4112,128]{3,2,1,0:T(8,128)(2,1)} custom-call(s32[2]{0:T(128)} %pad_add_fusion.2._, bf16[4,4,1024,128]{3,2,1,0:T(8,128)(2,1)} %collective-permute-done.10.src_ref, bf16[4,4,4112,128]{3,2,1,0:T(8,128)(2,1)} %place.15.refs_0_), custom_call_target="tpu_custom_call", output_to_operand_aliasing={{}: (2, {})} | custom-call | flops 251658240 | bytes 8388608 | tf_op jit(solution)/shard_map/place/pallas_call | solution.py:109
  (129 shorter events, 59.1 us)
Async XLA Ops:
  14.7 14.0 %collective-permute-start.1 = (f32[4,32,128,128]{3,2,1,0:T(8,128)}, f32[4,32,128,128]{3,2,1,0:T(8,128)}, u32[]{:S(2)}, u32[]{:S(2)}) collective-permute-start(f32[4,32,128,128]{3,2,1,0:T(8,128)} %get-tuple-element.24), channel_id=1, source_target_pairs={{0,1},{1,0},{2,3},{3,2},{4,5},{5,4},{6,7},{7,6}} | collective-permute-start | bytes 25165832 | tf_op jit(solution)/shard_map/ppermute | solution.py:130
  15.5 336.8 %collective-permute-start.12 = (bf16[1,4,1024,128]{3,2,1,0:T(8,128)(2,1)}, bf16[1,4,1024,128]{3,2,1,0:T(8,128)(2,1)}, u32[]{:S(2)}, u32[]{:S(2)}) collective-permute-start(bf16[1,4,1024,128]{3,2,1,0:T(8,128)(2,1)} %constant_dynamic-slice_fusion.9), channel_id=1, source_target_pairs={{0,2},{1,3},{2,0},{3,1},{4,6},{5,7},{6,4},{7,5}} | collective-permute-start | bytes 3145736 | tf_op jit(solution)/shard_map/ppermute | solution.py:130
  18.0 119.2 %collective-permute-start = (f32[4,32,128,128]{3,2,1,0:T(8,128)}, f32[4,32,128,128]{3,2,1,0:T(8,128)}, u32[]{:S(2)}, u32[]{:S(2)}) collective-permute-start(f32[4,32,128,128]{3,2,1,0:T(8,128)} %get-tuple-element.23), channel_id=1, source_target_pairs={{0,1},{1,0},{2,3},{3,2},{4,5},{5,4},{6,7},{7,6}} | collective-permute-start | bytes 25165832 | tf_op jit(solution)/shard_map/ppermute | solution.py:130
  21.9 333.1 %collective-permute-start.11 = (bf16[3,4,1024,128]{3,2,1,0:T(8,128)(2,1)}, bf16[3,4,1024,128]{3,2,1,0:T(8,128)(2,1)}, u32[]{:S(2)}, u32[]{:S(2)}) collective-permute-start(bf16[3,4,1024,128]{3,2,1,0:T(8,128)(2,1)} %constant_dynamic-slice_fusion.5), channel_id=1, source_target_pairs={{0,2},{1,3},{2,0},{3,1},{4,6},{5,7},{6,4},{7,5}} | collective-permute-start | bytes 9437192 | tf_op jit(solution)/shard_map/ppermute | solution.py:130
  22.4 69.5 %copy-start.5 = (f32[4]{0:T(128)}, f32[4]{0:T(128)S(1)}, u32[]{:S(2)}) copy-start(f32[4]{0:T(128)S(1)} %add_rsqrt_fusion.1) | copy-start | bytes 52
  40.9 248.4 %collective-permute-start.2 = (f32[4,32,128,128]{3,2,1,0:T(8,128)}, f32[4,32,128,128]{3,2,1,0:T(8,128)}, u32[]{:S(2)}, u32[]{:S(2)}) collective-permute-start(f32[4,32,128,128]{3,2,1,0:T(8,128)} %fusion.2), channel_id=1, source_target_pairs={{0,2},{1,3},{2,0},{3,1},{4,6},{5,7},{6,4},{7,5}} | collective-permute-start | bytes 25165832 | tf_op jit(solution)/shard_map/ppermute | solution.py:130
  122.9 239.9 %collective-permute-start.17 = (bf16[4,4,1024,128]{3,2,1,0:T(8,128)(2,1)}, bf16[4,4,1024,128]{3,2,1,0:T(8,128)(2,1)}, u32[]{:S(2)}, u32[]{:S(2)}) collective-permute-start(bf16[4,4,1024,128]{3,2,1,0:T(8,128)(2,1)} %get-tuple-element.25), channel_id=1, source_target_pairs={{0,1},{1,0},{2,3},{3,2},{4,5},{5,4},{6,7},{7,6}} | collective-permute-start | bytes 12582920 | tf_op jit(solution)/shard_map/ppermute | solution.py:130
  137.2 206.3 %collective-permute-start.13 = (bf16[4,4,1024,128]{3,2,1,0:T(8,128)(2,1)}, bf16[4,4,1024,128]{3,2,1,0:T(8,128)(2,1)}, u32[]{:S(2)}, u32[]{:S(2)}) collective-permute-start(bf16[4,4,1024,128]{3,2,1,0:T(8,128)(2,1)} %get-tuple-element.27), channel_id=1, source_target_pairs={{0,1},{1,0},{2,3},{3,2},{4,5},{5,4},{6,7},{7,6}} | collective-permute-start | bytes 12582920 | tf_op jit(solution)/shard_map/ppermute | solution.py:130
  304.0 3.6 collective-permute-start.3
  327.1 43.0 %collective-permute-start.4 = (f32[4,6144]{1,0:T(4,128)}, f32[4,6144]{1,0:T(4,128)}, u32[]{:S(2)}, u32[]{:S(2)}) collective-permute-start(f32[4,6144]{1,0:T(4,128)} %fusion.38), channel_id=1, source_target_pairs={{0,4},{4,0},{1,5},{5,1},{2,6},{6,2},{3,7},{7,3}} | collective-permute-start | bytes 294920 | tf_op jit(solution)/shard_map/ppermute | solution.py:133
  343.5 320.0 %collective-permute-start.16 = (bf16[4,4,1024,128]{3,2,1,0:T(8,128)(2,1)}, bf16[4,4,1024,128]{3,2,1,0:T(8,128)(2,1)}, u32[]{:S(2)}, u32[]{:S(2)}) collective-permute-start(bf16[4,4,1024,128]{3,2,1,0:T(8,128)(2,1)} %get-tuple-element.26), channel_id=1, source_target_pairs={{0,2},{1,3},{2,0},{3,1},{4,6},{5,7},{6,4},{7,5}} | collective-permute-start | bytes 12582920 | tf_op jit(solution)/shard_map/ppermute | solution.py:130
  352.3 318.5 %collective-permute-start.15 = (bf16[3,4,1024,128]{3,2,1,0:T(8,128)(2,1)}, bf16[3,4,1024,128]{3,2,1,0:T(8,128)(2,1)}, u32[]{:S(2)}, u32[]{:S(2)}) collective-permute-start(bf16[3,4,1024,128]{3,2,1,0:T(8,128)(2,1)} %constant_dynamic-slice_fusion.2), channel_id=1, source_target_pairs={{0,3},{1,2},{2,1},{3,0},{4,7},{5,6},{6,5},{7,4}} | collective-permute-start | bytes 9437192 | tf_op jit(solution)/shard_map/ppermute | solution.py:130
  355.0 321.7 %collective-permute-start.14 = (bf16[1,4,1024,128]{3,2,1,0:T(8,128)(2,1)}, bf16[1,4,1024,128]{3,2,1,0:T(8,128)(2,1)}, u32[]{:S(2)}, u32[]{:S(2)}) collective-permute-start(bf16[1,4,1024,128]{3,2,1,0:T(8,128)(2,1)} %constant_dynamic-slice_fusion.3), channel_id=1, source_target_pairs={{0,3},{1,2},{2,1},{3,0},{4,7},{5,6},{6,5},{7,4}} | collective-permute-start | bytes 3145736 | tf_op jit(solution)/shard_map/ppermute | solution.py:130
  362.8 318.1 %collective-permute-start.10 = (bf16[4,4,1024,128]{3,2,1,0:T(8,128)(2,1)}, bf16[4,4,1024,128]{3,2,1,0:T(8,128)(2,1)}, u32[]{:S(2)}, u32[]{:S(2)}) collective-permute-start(bf16[4,4,1024,128]{3,2,1,0:T(8,128)(2,1)} %get-tuple-element.28), channel_id=1, source_target_pairs={{0,3},{1,2},{2,1},{3,0},{4,7},{5,6},{6,5},{7,4}} | collective-permute-start | bytes 12582920 | tf_op jit(solution)/shard_map/ppermute | solution.py:130
  371.3 30.7 %copy-start.3 = (bf16[4,6144]{1,0:T(4,128)(2,1)}, bf16[4,6144]{1,0:T(4,128)(2,1)S(1)}, u32[]{:S(2)}) copy-start(bf16[4,6144]{1,0:T(4,128)(2,1)S(1)} %get-tuple-element.22) | copy-start | bytes 147460
  371.3 30.7 %copy-start.8 = (f32[4]{0:T(128)}, f32[4]{0:T(128)S(1)}, u32[]{:S(2)}) copy-start(f32[4]{0:T(128)S(1)} %add_rsqrt_fusion) | copy-start | bytes 52
  371.3 31.0 %copy-start.6 = (f32[32]{0:T(128)S(1)}, f32[32]{0:T(128)}, u32[]{:S(2)}) copy-start(f32[32]{0:T(128)} %get-tuple-element.56) | copy-start | bytes 388
  371.3 30.9 %copy-start.7 = (f32[32]{0:T(128)S(1)}, f32[32]{0:T(128)}, u32[]{:S(2)}) copy-start(f32[32]{0:T(128)} %get-tuple-element.57) | copy-start | bytes 388
  371.3 245.8 %copy-start.9 = (pred[16]{0:T(512)(128)(4,1)S(1)}, pred[16]{0:T(512)(128)(4,1)}, u32[]{:S(2)}) copy-start(pred[16]{0:T(512)(128)(4,1)} %broadcast_in_dim.15) | copy-start | bytes 52
  402.4 212.4 %collective-permute-start.5 = (bf16[4,4,8,128]{3,2,1,0:T(8,128)(2,1)S(1)}, bf16[4,4,8,128]{3,2,1,0:T(8,128)(2,1)S(1)}, u32[]{:S(2)}, u32[]{:S(2)}) collective-permute-start(bf16[4,4,8,128]{3,2,1,0:T(8,128)(2,1)S(1)} %pad_maximum_fusion.2), channel_id=1, source_target_pairs={{0,2},{1,3},{2,0},{3,1},{4,6},{5,7},{6,4},{7,5}} | collective-permute-start | bytes 98312 | tf_op jit(solution)/shard_map/ppermute | solution.py:130
  615.0 1.3 collective-permute-start.6
  633.1 1.4 collective-permute-start.7
  634.9 4.5 collective-permute-start.8
  659.4 28.8 %collective-permute-start.9 = (f32[4,6144]{1,0:T(4,128)}, f32[4,6144]{1,0:T(4,128)}, u32[]{:S(2)}, u32[]{:S(2)}) collective-permute-start(f32[4,6144]{1,0:T(4,128)} %fusion.40), channel_id=1, source_target_pairs={{0,4},{4,0},{1,5},{5,1},{2,6},{6,2},{3,7},{7,3}} | collective-permute-start | bytes 294920 | tf_op jit(solution)/shard_map/ppermute | solution.py:133
  (5 other events, 74.9 us)

commit v2 on v1

--- a/solution.py
+++ b/solution.py
@@ -1,3 +1,5 @@
+import functools
+
 import jax
 import jax.numpy as jnp
 from jax import lax
@@ -45,23 +47,58 @@
 
 
 def pack(out, stats):
-    rows, _, heads, group = stats.shape
-    tail = jnp.transpose(stats, (2, 3, 0, 1)).reshape(1, heads, group, 2 * rows)
-    return jnp.concatenate([out, jnp.pad(tail, ((0, 0), (0, 0), (0, 0), (0, out.shape[-1] - 2 * rows)))])
-
-
-def unpack(packed):
-    rows, heads, group = packed.shape[0] - 1, packed.shape[1], packed.shape[2]
-    tail = packed[rows, :, :, :2 * rows].reshape(heads, group, rows, 2)
-    return packed[:rows], jnp.transpose(tail, (2, 3, 0, 1))
-
-
-def place_last_block(src_ref, total_ref, out_ref, buf, in_sems, out_sems):
+    dim = out.shape[-1]
+    tail = stats.reshape(-1, dim)
+    return jnp.concatenate([out.reshape(-1, dim), jnp.pad(tail, ((0, 8 - tail.shape[0]), (0, 0)))])
+
+
+def unpack(packed, heads, group):
+    lines, dim = packed.shape[0] - 8, packed.shape[1]
+    rows = lines // (heads * group)
+    tail = packed[lines:lines + 2 * lines // dim]
+    return packed[:lines].reshape(rows, heads, group, dim), tail.reshape(rows, 2, heads, group)
+
+
+def partner(me, mask):
+    if mask == 1:
+        return me + 1 - 2 * lax.rem(me, 2)
+    if mask == 2:
+        return lax.rem(me + 2, 4)
+    return 3 - me if mask == 3 else me
+
+
+def grab_block(rows, mask, row, first_head, src_ref, out_ref, sem):
+    first = rows * partner(lax.axis_index('sp'), mask) + row
+    copy = pltpu.make_async_copy(src_ref.at[pl.ds(first, 1), pl.ds(first_head, out_ref.shape[1])], out_ref, sem)
+    copy.start()
+    copy.wait()
+
+
+def grab(cache, rows, mask, row, first_head, heads):
+    shape = (1, heads) + cache.shape[2:]
+    return pl.pallas_call(
+        functools.partial(grab_block, rows, mask, row, first_head),
+        in_specs=[pl.BlockSpec(memory_space=pltpu.HBM)],
+        out_specs=pl.BlockSpec(memory_space=pltpu.VMEM),
+        out_shape=pltpu.VMEM(shape, cache.dtype),
+        scratch_shapes=[pltpu.SemaphoreType.DMA],
+        compiler_params=pltpu.CompilerParams(vmem_limit_bytes=62 * 1024 * 1024),
+        name="grab",
+    )(cache)
+
+
+def place_block(count, own, mask, out_first, head_first, src_ref, *refs):
+    out_ref, buf, in_sems, out_sems = refs[-4:]
     heads, length = src_ref.shape[1], src_ref.shape[2]
-    row = out_ref.shape[0] - 1
-    pos = pl.multiple_of((3 - lax.axis_index('sp')) * length, length)
-    reads = [pltpu.make_async_copy(src_ref.at[0, j], buf.at[j], in_sems.at[j]) for j in range(heads)]
-    writes = [pltpu.make_async_copy(buf.at[j], out_ref.at[row, j, pl.ds(pos, length)], out_sems.at[j]) for j in range(heads)]
+    me = lax.axis_index('sp')
+    src_first = me * count if own else 0
+    pos = pl.multiple_of(partner(me, mask) * length, length)
+    reads, writes = [], []
+    for i in range(count):
+        for j in range(heads):
+            n = i * heads + j
+            reads.append(pltpu.make_async_copy(src_ref.at[src_first + i, j], buf.at[n], in_sems.at[n]))
+            writes.append(pltpu.make_async_copy(buf.at[n], out_ref.at[out_first + i, head_first + j, pl.ds(pos, length)], out_sems.at[n]))
     for copy in reads:
         copy.start()
     for read, write in zip(reads, writes):
@@ -71,55 +108,43 @@
         copy.wait()
 
 
-def place_last(total, block):
-    heads, length, dim = block.shape[1:]
+def place(total, block, mask, out_shape, own=False, out_first=0, head_first=0):
+    count = out_shape[0] if own else block.shape[0]
+    pieces = count * block.shape[1]
+    operands = [block] if total is None else [block, total]
+    nbytes = 2 * pieces * block.shape[2] * block.shape[3] * 2
     return pl.pallas_call(
-        place_last_block,
-        in_specs=[pl.BlockSpec(memory_space=pl.ANY), pl.BlockSpec(memory_space=pl.ANY)],
-        out_specs=pl.BlockSpec(memory_space=pl.ANY),
-        out_shape=jax.ShapeDtypeStruct(total.shape, total.dtype),
-        scratch_shapes=[pltpu.VMEM((heads, length, dim), block.dtype), pltpu.SemaphoreType.DMA((heads,)), pltpu.SemaphoreType.DMA((heads,))],
-        input_output_aliases={1: 0},
-        compiler_params=pltpu.CompilerParams(vmem_limit_bytes=67043328),
-        name="place_last",
-    )(block, total)
-
-
-def copy_block(_, src_ref, *refs):
-    refs[-1][...] = src_ref[...]
-
-
-def place(total, block, first, pos_block, out_shape, count=None, out_first=0):
-    rows, heads, _, dim = out_shape
-    length = block.shape[2]
-    if length > CACHE_EXTRA:
-        count = rows if count is None else count
-        grid, shape = (count, heads // 2), (1, 2, length, dim)
-    else:
-        count, grid, shape = rows, (1, 1), (rows, heads, length, dim)
-    scalars = jnp.stack([jnp.asarray(first, jnp.int32), jnp.asarray(pos_block, jnp.int32)])
-    in_specs = [pl.BlockSpec(shape, lambda i, j, s: (s[0] + i, j, 0, 0))]
-    operands = [scalars, block]
-    aliases = {}
-    if total is not None:
-        in_specs.append(pl.BlockSpec(memory_space=pl.ANY))
-        operands.append(total)
-        aliases = {2: 0}
-    nbytes = 2 * count * heads * length * dim * 2
-    return pl.pallas_call(
-        copy_block,
-        grid_spec=pltpu.PrefetchScalarGridSpec(
-            num_scalar_prefetch=1,
-            grid=grid,
-            in_specs=in_specs,
-            out_specs=pl.BlockSpec(shape, lambda i, j, s: (out_first + i, j, s[1], 0)),
-        ),
+        functools.partial(place_block, count, own, mask, out_first, head_first),
+        in_specs=[pl.BlockSpec(memory_space=pltpu.HBM)] * len(operands),
+        out_specs=pl.BlockSpec(memory_space=pltpu.HBM),
         out_shape=jax.ShapeDtypeStruct(out_shape, block.dtype),
-        input_output_aliases=aliases,
-        compiler_params=pltpu.CompilerParams(vmem_limit_bytes=67043328),
+        scratch_shapes=[pltpu.VMEM((pieces,) + block.shape[2:], block.dtype), pltpu.SemaphoreType.DMA((pieces,)), pltpu.SemaphoreType.DMA((pieces,))],
+        input_output_aliases={} if total is None else {1: 0},
+        compiler_params=pltpu.CompilerParams(vmem_limit_bytes=62 * 1024 * 1024),
         cost_estimate=pl.CostEstimate(flops=nbytes * 30, bytes_accessed=nbytes, transcendentals=0),
         name="place",
     )(*operands)
+
+
+def write_block(mask, row, head, src_ref, total_ref, out_ref, sem):
+    length = src_ref.shape[2]
+    pos = total_ref.shape[2] - length if mask is None else pl.multiple_of(partner(lax.axis_index('sp'), mask) * length, length)
+    copy = pltpu.make_async_copy(src_ref, out_ref.at[pl.ds(row, src_ref.shape[0]), pl.ds(head, src_ref.shape[1]), pl.ds(pos, length)], sem)
+    copy.start()
+    copy.wait()
+
+
+def write(total, block, mask, row=0, head=0):
+    return pl.pallas_call(
+        functools.partial(write_block, mask, row, head),
+        in_specs=[pl.BlockSpec(memory_space=pltpu.VMEM), pl.BlockSpec(memory_space=pltpu.HBM)],
+        out_specs=pl.BlockSpec(memory_space=pltpu.HBM),
+        out_shape=jax.ShapeDtypeStruct(total.shape, total.dtype),
+        scratch_shapes=[pltpu.SemaphoreType.DMA],
+        input_output_aliases={1: 0},
+        compiler_params=pltpu.CompilerParams(vmem_limit_bytes=62 * 1024 * 1024),
+        name="write",
+    )(pltpu.with_memory_space_constraint(block, pltpu.VMEM), total)
 
 
 def solution(mesh):
@@ -145,11 +170,14 @@
         def rows_of(value, mask, first=0, count=rows):
             return lax.dynamic_slice_in_dim(value, rows * (me ^ mask) + first, count, 0)
 
-        kx0_rows = rows_of(k_cache, 2, 0, 1)
+        kx0_rows = grab(k_cache, rows, 2, 0, 0, 1)
         kx0 = send(kx0_rows, 2)
-        k_src, slopes_a = lax.optimization_barrier((k_cache, slopes, kx0_rows))[:2]
-        kx1_rows = rows_of(k_src, 2, 1, rows - 1)
+        k_src, _ = lax.optimization_barrier((k_cache, kx0_rows))
+        kx1_rows = grab(k_src, rows, 2, 0, 1, kv_dev - 1)
         kx1 = send(kx1_rows, 2)
+        k_src, slopes_a, _ = lax.optimization_barrier((k_cache, slopes, kx1_rows))
+        kx2_rows = rows_of(k_src, 2, 1, rows - 1)
+        kx2 = send(kx2_rows, 2)
 
         own = states[0]
         offset = (shard_len * (seq_shards - 1 - me)).astype(F32)
@@ -172,7 +200,9 @@
         vd_rows = rows_of(v_src, 1)
         vx_rows = rows_of(v_src, 2)
         vy0_rows = rows_of(v_src, 3, 0, rows - 1)
-        vy1_rows = rows_of(v_src, 3, rows - 1, 1)
+        last_row = rows_of(v_src, 3, rows - 1, 1)
+        vy1_rows = last_row[:, :kv_dev - 1]
+        vy2_rows = last_row[:, kv_dev - 1:]
         ky = send(ky_rows, 3)
         kd = send(kd_rows, 1)
         vd = send(vd_rows, 1)
@@ -210,11 +240,12 @@
         stats = jnp.stack([part_max, part_sum], axis=1)
 
         pair = pack(jnp.concatenate([rows_of(part_out, 3), rows_of(part_out, 1)]), jnp.concatenate([rows_of(stats, 3), rows_of(stats, 1)]))
-        pair_out, pair_stats = unpack(send(pair, 1))
+        pair_out, pair_stats = unpack(send(pair, 1), kv_dev, group)
         far = pack(*merge(rows_of(part_out, 2), rows_of(stats, 2), pair_out[:rows], pair_stats[:rows]))
-        ax, axs = unpack(send(far, 2))
+        ax, axs = unpack(send(far, 2), kv_dev, group)
         vy0 = send(vy0_rows, 3)
         vy1 = send(vy1_rows, 3)
+        vy2 = send(vy2_rows, 3)
 
         near_out, near_stats = merge(rows_of(part_out, 0), rows_of(stats, 0), pair_out[rows:], pair_stats[rows:])
         all_out, all_stats = merge(near_out, near_stats, ax, axs)
@@ -232,24 +263,25 @@
 
         out_shape = (rows, kv_dev, prompt_len + CACHE_EXTRA, head_dim)
         tail_zeros = jnp.zeros((rows, kv_dev, CACHE_EXTRA - 1, head_dim), BF16)
-        late, _ = lax.optimization_barrier((me, part_x))
+        k_src, v_src, _ = lax.optimization_barrier((k_cache, v_cache, part_x))
 
         def add_tail(total, new_row):
-            tail = jnp.concatenate([new_row[:, :, None, :], tail_zeros], axis=2)
-            return place(total, tail, 0, prompt_len // CACHE_EXTRA, out_shape)
-
-        k_out = place(None, k_cache, late * rows, late, out_shape)
-        k_out = place(k_out, kd, 0, me ^ 1, out_shape)
-        v_out = place(None, v_cache, late * rows, late, out_shape)
-        v_out = place(v_out, vd, 0, me ^ 1, out_shape)
-        k_out = place(k_out, kx0, 0, me ^ 2, out_shape, 1, 0)
-        k_out = place(k_out, kx1, 0, me ^ 2, out_shape, rows - 1, 1)
+            return write(total, jnp.concatenate([new_row[:, :, None, :], tail_zeros], axis=2), None)
+
+        k_out = place(None, k_src, 0, out_shape, own=True)
+        k_out = place(k_out, kd, 1, out_shape)
+        v_out = place(None, v_src, 0, out_shape, own=True)
+        v_out = place(v_out, vd, 1, out_shape)
+        k_out = place(k_out, kx2, 2, out_shape, out_first=1)
+        k_out = place(k_out, kx0, 2, out_shape)
+        k_out = place(k_out, kx1, 2, out_shape, head_first=1)
         k_out = add_tail(k_out, key_new)
         v_out = add_tail(v_out, value_new)
-        k_out = place(k_out, ky, 0, me ^ 3, out_shape)
-        v_out = place(v_out, vx, 0, me ^ 2, out_shape)
-        v_out = place(v_out, vy0, 0, me ^ 3, out_shape, rows - 1, 0)
-        v_out = place_last(v_out, vy1)
+        k_out = place(k_out, ky, 3, out_shape)
+        v_out = place(v_out, vx, 2, out_shape)
+        v_out = place(v_out, vy0, 3, out_shape)
+        v_out = place(v_out, vy1, 3, out_shape, out_first=rows - 1)
+        v_out = write(v_out, vy2, 3, rows - 1, kv_dev - 1)
         return hidden_out, state_new, k_out, v_out
 
     batch_spec = P(('dp', 'sp'), None)

time: 692 us -> 639 us (0.923)
  Pallas kernels: 64.8 us -> 39.9 us
  waiting for transfers between devices: 377 us -> 359 us
    pallas_call x12 -> x16, Pallas kernels: 64.8 us -> 39.9 us  [the longest x11 34.2 us: place(): pl.pallas_call(functools.partial(place_block, count, own, mask, out_first...]
    ppermute x15 -> x17, waiting for transfers between devices: 375 us -> 357 us  [send(): return lax.ppermute(value, 'sp', [(i, i ^ mask) for i in range(seq_shards)])]
    dynamic_slice x7 -> x5, local copies, waits for them, and re-layouts: 27.3 us -> 22.9 us  [rows_of(): return lax.dynamic_slice_in_dim(value, rows * (me ^ mask) + first, count, 0)]
    ppermute x15 -> x17, starting transfers between devices: 12.7 us -> 13.9 us  [send(): return lax.ppermute(value, 'sp', [(i, i ^ mask) for i in range(seq_shards)])]
  transfers between devices with their start and end apart: 18 -> 20, of which waited for: 7 -> 8; matrix products, arithmetic and copies ran while one was open for 31% -> 32% of each run, Pallas kernels for 9% -> 6%
where the time goes in v2:
time: 639 us; the launch traced here: 638 us
  waiting for transfers between devices  359 us (56%)
  matrix products  153 us (24%)
  Pallas kernels  39.9 us (6%)
  other arithmetic  36.4 us (6%)
  local copies, waits for them, and re-layouts  30.1 us (5%)
  starting transfers between devices  18.6 us (3%)
    ppermute x17, waiting for transfers between devices, send(): return lax.ppermute(value, 'sp', [(i, i ^ mask) for i in range(seq_shards)])  357 us
    dot_general x1, matrix products, step(): jnp.einsum('bd,dkn->bkn', normed, w_lin_qkv, preferred_element_type=F32)  48.1 us
    pallas_call x11, Pallas kernels, place(): pl.pallas_call(functools.partial(place_block, count, own, mask, out_first...  34.2 us
    dot_general x1, matrix products, step(): jnp.einsum('bd,dkjn->bkjn', normed_two, w_attn_in, preferred_element_type...  30.7 us
    dynamic_slice x5, local copies, waits for them, and re-layouts, rows_of(): return lax.dynamic_slice_in_dim(value, rows * (me ^ mask) + first, count, 0)  22.9 us
    dot_general x1, matrix products, step(): attn_out = jnp.dot(head_out, w_attn_out, preferred_element_type=F32)  19.1 us
    dot_general x1, matrix products, step(): jnp.dot(normed, w_lin_gate, preferred_element_type=F32)  18.9 us
    dot_general x1, matrix products, step(): lin_out = jnp.dot(mixed_out, w_lin_out, preferred_element_type=F32)  18.8 us
  transfers between devices with their start and end apart: 20, of which 8 were waited for; matrix products, arithmetic and copies ran while one was open for 32% of the time, Pallas kernels for 6%

profile of v2, /device:TPU:0, one launch (start us, length us, event | category | flops | bytes accessed | tf_op | source)
XLA Modules:
  0.0 638.1 jit_solution(16068950303167841279)
XLA Ops:
  4.4 11.1 %bitcast_multiply_fusion.2 = (f32[4,32,128,128]{3,2,1,0:T(8,128)}, f32[4,32,128,128]{3,2,1,0:T(8,128)}) fusion(f32[1,16,32,128,128]{4,3,2,1,0:T(8,128)} %param.14, s32[]{:T(128)S(6)} %select_n.53, f32[32]{0:T(128)S(1)} %multiply_exponential_fusion, s32[]{:T(128)S(6)} %select_n.55), kind=kLoop, calls=%fused_computation.6 | loop fusion | flops 4194304 | bytes 33554568 | tf_op jit(solution)/shard_map/mul | solution.py:186
  19.2 10.2 %collective-permute-done.1 = f32[4,32,128,128]{3,2,1,0:T(8,128)} collective-permute-done((f32[4,32,128,128]{3,2,1,0:T(8,128)}, f32[4,32,128,128]{3,2,1,0:T(8,128)}, u32[]{:S(2)}, u32[]{:S(2)}) %collective-permute-start.1) | collective-permute-done | bytes 8388640 | tf_op jit(solution)/shard_map/ppermute | solution.py:155
  29.5 12.2 %fusion.2 = f32[4,32,128,128]{3,2,1,0:T(8,128)} fusion(f32[4,32,128,128]{3,2,1,0:T(8,128)} %collective-permute-done.1, f32[1,16,32,128,128]{4,3,2,1,0:T(8,128)} %param.14, s32[]{:T(128)S(6)} %select_n.54, f32[32]{0:T(128)S(1)} %multiply_exponential_fusion), kind=kLoop, calls=%fused_computation.5 | loop fusion | flops 4194304 | bytes 25165956 | tf_op jit(solution)/shard_map/add | solution.py:194
  44.5 48.1 %fusion.16 = bf16[4,3,4096]{2,0,1:T(4,128)(2,1)S(1)} fusion(bf16[6144,3,4096]{2,0,1:T(8,128)(2,1)} %param.19, bf16[4,6144]{1,0:T(4,128)(2,1)S(1)} %copy-done.1, f32[6144]{0:T(1024)S(1)} %copy-done.2, f32[4]{0:T(128)S(1)} %add_rsqrt_fusion.1), kind=kOutput, calls=%fused_computation.24 | convolution fusion | flops 604323840 | bytes 151166992 | tf_op jit(solution)/shard_map/bd,dkn->bkn/dot_general | solution.py:191
  92.7 18.9 %fusion.9 = f32[4,4096]{1,0:T(4,128)S(1)} fusion(bf16[6144,4096]{1,0:T(8,128)(2,1)} %param.20, bf16[4,6144]{1,0:T(4,128)(2,1)S(1)} %copy-done.1, f32[6144]{0:T(1024)S(1)} %copy-done.2, f32[4]{0:T(128)S(1)} %add_rsqrt_fusion.1), kind=kOutput, calls=%fused_computation.15 | convolution fusion | flops 201474048 | bytes 50470928 | tf_op jit(solution)/shard_map/dot_general | solution.py:210
  111.9 3.8 constant_dynamic-slice_fusion.5
  115.7 7.7 %constant_dynamic-slice_fusion = (bf16[4,4,1024,128]{3,2,1,0:T(8,128)(2,1)}, bf16[4,4,1024,128]{3,2,1,0:T(8,128)(2,1)}) fusion(bf16[16,4,1024,128]{3,2,1,0:T(8,128)(2,1)} %src_ref.4, s32[]{:T(128)S(6)} %select_n.53, s32[]{:T(128)S(6)} %select_n.54), kind=kLoop, calls=%fused_computation.125 | loop fusion | bytes 16777224 | tf_op jit(solution)/shard_map/dynamic_slice | solution.py:171
  125.6 3.7 constant_dynamic-slice_fusion.2
  129.3 7.7 %constant_dynamic-slice_fusion.4 = (bf16[4,4,1024,128]{3,2,1,0:T(8,128)(2,1)}, bf16[4,4,1024,128]{3,2,1,0:T(8,128)(2,1)}) fusion(bf16[16,4,1024,128]{3,2,1,0:T(8,128)(2,1)} %src_ref.3, s32[]{:T(128)S(6)} %select_n.53, s32[]{:T(128)S(6)} %select_n.55), kind=kLoop, calls=%fused_computation.129 | loop fusion | bytes 16777224 | tf_op jit(solution)/shard_map/dynamic_slice | solution.py:171
  137.5 88.1 %collective-permute-done.2 = f32[4,32,128,128]{3,2,1,0:T(8,128)} collective-permute-done((f32[4,32,128,128]{3,2,1,0:T(8,128)}, f32[4,32,128,128]{3,2,1,0:T(8,128)}, u32[]{:S(2)}, u32[]{:S(2)}) %collective-permute-start.2) | collective-permute-done | bytes 8388640 | tf_op jit(solution)/shard_map/ppermute | solution.py:155
  225.6 10.0 %fusion.6 = f32[4,32,128,128]{3,2,1,0:T(8,128)S(1)} fusion(f32[4,32,128,128]{3,2,1,0:T(8,128)} %collective-permute-done.2, f32[4,32,128,128]{3,2,1,0:T(8,128)} %collective-permute-done, f32[1,16,32,128,128]{4,3,2,1,0:T(8,128)} %param.14, s32[]{:T(128)S(6)} %select_n.52, f32[4,32,128]{2,1,0:T(8,128)S(1)} %get-tuple-element.39, ...), kind=kLoop, calls=%fused_computation.11 | loop fusion | flops 12582912 | bytes 33685764 | tf_op jit(solution)/shard_map/add | solution.py:214
  245.7 18.8 %fusion.30 = f32[4,6144]{1,0:T(4,128)S(1)} fusion(bf16[4096,6144]{1,0:T(8,128)(2,1)} %param.22, f32[4,4096]{1,0:T(4,128)S(1)} %fusion.9, f32[1,4,32,128]{3,2,1,0:T(8,128)S(1)} %bitcast.158, f32[4096]{0:T(1024)S(1)} %copy-done.4, f32[4]{0:T(128)S(1)} %rsqrt_bitcast_fusion), kind=kOutput, calls=%fused_computation.68 | convolution fusion | flops 201392128 | bytes 50577424 | tf_op jit(solution)/shard_map/dot_general | solution.py:219
  266.0 3.8 place.17.refs_0_
  269.9 3.9 place.11.refs_0_
  273.8 3.9 place.12.refs_0_
  277.6 35.0 %collective-permute-done.13.src_ref = bf16[3,4,1024,128]{3,2,1,0:T(8,128)(2,1)} collective-permute-done((bf16[3,4,1024,128]{3,2,1,0:T(8,128)(2,1)}, bf16[3,4,1024,128]{3,2,1,0:T(8,128)(2,1)}, u32[]{:S(2)}, u32[]{:S(2)}) %collective-permute-start.13) | collective-permute-done | bytes 3145760 | tf_op jit(solution)/shard_map/ppermute | solution.py:155
  322.3 3.9 place.18.total_ref
  326.5 30.7 %fusion = bf16[4,4,10,128]{3,0,2,1:T(4,128)(2,1)S(1)} fusion(bf16[6144,4,10,128]{3,1,2,0:T(4,128)(2,1)} %param.24, bf16[4,6144]{1,0:T(4,128)(2,1)S(1)} %get-tuple-element.25, f32[6144]{0:T(1024)S(1)} %copy-done.3, f32[4]{0:T(128)S(1)} %add_rsqrt_fusion), kind=kOutput, calls=%fused_computation.1 | convolution fusion | flops 251756544 | bytes 63029264 | tf_op jit(solution)/shard_map/bd,dkjn->bkjn/dot_general | solution.py:223
  358.3 219.4 %collective-permute-done.5 = bf16[4,4,8,128]{3,2,1,0:T(8,128)(2,1)S(1)} collective-permute-done((bf16[4,4,8,128]{3,2,1,0:T(8,128)(2,1)S(1)}, bf16[4,4,8,128]{3,2,1,0:T(8,128)(2,1)S(1)}, u32[]{:S(2)}, u32[]{:S(2)}) %collective-permute-start.5) | collective-permute-done | bytes 32800 | tf_op jit(solution)/shard_map/ppermute | solution.py:155
  579.9 8.1 %multiply_reduce_fusion = (f32[16,4,8]{2,1,0:T(4,128)S(1)}, f32[16,4,8,1024]{3,2,1,0:T(8,128)S(1)}) fusion(bf16[16,4,8,128]{3,2,1,0:T(8,128)(2,1)S(1)} %bitcast_select_fusion, bf16[16,4,1024,128]{3,2,1,0:T(8,128)(2,1)} %src_ref.3), kind=kOutput, calls=%fused_computation.17 | convolution fusion | flops 135265792 | bytes 19007488 | tf_op jit(solution)/shard_map/bkgd,bktd->bkgt/dot_general | solution.py:235
  588.0 7.0 %fusion.12 = f32[16,4,8,128]{3,2,1,0:T(8,128)S(1)} fusion(bf16[16,4,1024,128]{3,2,1,0:T(8,128)(2,1)} %src_ref.4, f32[16,4,8,1024]{3,2,1,0:T(8,128)S(1)} %get-tuple-element.58, f32[16,4,8]{2,1,0:T(4,128)S(1)} %get-tuple-element.57), kind=kOutput, calls=%fused_computation.20 | convolution fusion | flops 135790592 | bytes 19138560 | tf_op jit(solution)/shard_map/bkgt,bktd->bkgd/dot_general | solution.py:239
  602.3 19.1 %fusion.32 = f32[4,6144]{1,0:T(4,128)S(1)} fusion(bf16[4096,6144]{1,0:T(8,128)(2,1)} %param.25, bf16[1,4,32,128]{3,2,1,0:T(8,128)(2,1)S(1)} %fusion.39), kind=kOutput, calls=%fused_computation.69 | convolution fusion | flops 201326592 | bytes 50462720 | tf_op jit(solution)/shard_map/dot_general | solution.py:260
  624.1 3.9 place.19.refs_0_
  633.5 3.9 place.16
  (124 shorter events, 54.0 us)
Async XLA Ops:
  4.4 14.7 %copy-start.1 = (bf16[4,6144]{1,0:T(4,128)(2,1)S(1)}, bf16[4,6144]{1,0:T(4,128)(2,1)}, u32[]{:S(2)}) copy-start(bf16[4,6144]{1,0:T(4,128)(2,1)} %param.13) | copy-start | bytes 147460
  15.5 14.0 %collective-permute-start.1 = (f32[4,32,128,128]{3,2,1,0:T(8,128)}, f32[4,32,128,128]{3,2,1,0:T(8,128)}, u32[]{:S(2)}, u32[]{:S(2)}) collective-permute-start(f32[4,32,128,128]{3,2,1,0:T(8,128)} %get-tuple-element.27), channel_id=1, source_target_pairs={{0,1},{1,0},{2,3},{3,2},{4,5},{5,4},{6,7},{7,6}} | collective-permute-start | bytes 25165832 | tf_op jit(solution)/shard_map/ppermute | solution.py:155
  16.3 300.6 %collective-permute-start.12 = (bf16[1,1,1024,128]{3,2,1,0:T(8,128)(2,1)}, bf16[1,1,1024,128]{3,2,1,0:T(8,128)(2,1)}, u32[]{:S(2)}, u32[]{:S(2)}) collective-permute-start(bf16[1,1,1024,128]{3,2,1,0:T(8,128)(2,1)} %grab.2), channel_id=1, source_target_pairs={{0,2},{1,3},{2,0},{3,1},{4,6},{5,7},{6,4},{7,5}} | collective-permute-start | bytes 786440 | tf_op jit(solution)/shard_map/ppermute | solution.py:155
  18.8 299.8 %collective-permute-start.11 = (bf16[1,3,1024,128]{3,2,1,0:T(8,128)(2,1)}, bf16[1,3,1024,128]{3,2,1,0:T(8,128)(2,1)}, u32[]{:S(2)}, u32[]{:S(2)}) collective-permute-start(bf16[1,3,1024,128]{3,2,1,0:T(8,128)(2,1)} %grab.3), channel_id=1, source_target_pairs={{0,2},{1,3},{2,0},{3,1},{4,6},{5,7},{6,4},{7,5}} | collective-permute-start | bytes 2359304 | tf_op jit(solution)/shard_map/ppermute | solution.py:155
  18.8 118.1 %collective-permute-start = (f32[4,32,128,128]{3,2,1,0:T(8,128)}, f32[4,32,128,128]{3,2,1,0:T(8,128)}, u32[]{:S(2)}, u32[]{:S(2)}) collective-permute-start(f32[4,32,128,128]{3,2,1,0:T(8,128)} %get-tuple-element.26), channel_id=1, source_target_pairs={{0,1},{1,0},{2,3},{3,2},{4,5},{5,4},{6,7},{7,6}} | collective-permute-start | bytes 25165832 | tf_op jit(solution)/shard_map/ppermute | solution.py:155
  19.2 25.3 %copy-start.2 = (f32[6144]{0:T(1024)S(1)}, f32[6144]{0:T(1024)}, u32[]{:S(2)}) copy-start(f32[6144]{0:T(1024)} %param.18) | copy-start | bytes 73732
  41.7 183.9 %collective-permute-start.2 = (f32[4,32,128,128]{3,2,1,0:T(8,128)}, f32[4,32,128,128]{3,2,1,0:T(8,128)}, u32[]{:S(2)}, u32[]{:S(2)}) collective-permute-start(f32[4,32,128,128]{3,2,1,0:T(8,128)} %fusion.2), channel_id=1, source_target_pairs={{0,2},{1,3},{2,0},{3,1},{4,6},{5,7},{6,4},{7,5}} | collective-permute-start | bytes 25165832 | tf_op jit(solution)/shard_map/ppermute | solution.py:155
  123.4 198.9 %collective-permute-start.19 = (bf16[4,4,1024,128]{3,2,1,0:T(8,128)(2,1)}, bf16[4,4,1024,128]{3,2,1,0:T(8,128)(2,1)}, u32[]{:S(2)}, u32[]{:S(2)}) collective-permute-start(bf16[4,4,1024,128]{3,2,1,0:T(8,128)(2,1)} %get-tuple-element.28), channel_id=1, source_target_pairs={{0,1},{1,0},{2,3},{3,2},{4,5},{5,4},{6,7},{7,6}} | collective-permute-start | bytes 12582920 | tf_op jit(solution)/shard_map/ppermute | solution.py:155
  137.0 127.5 %collective-permute-start.14 = (bf16[4,4,1024,128]{3,2,1,0:T(8,128)(2,1)}, bf16[4,4,1024,128]{3,2,1,0:T(8,128)(2,1)}, u32[]{:S(2)}, u32[]{:S(2)}) collective-permute-start(bf16[4,4,1024,128]{3,2,1,0:T(8,128)(2,1)} %get-tuple-element.30), channel_id=1, source_target_pairs={{0,1},{1,0},{2,3},{3,2},{4,5},{5,4},{6,7},{7,6}} | collective-permute-start | bytes 12582920 | tf_op jit(solution)/shard_map/ppermute | solution.py:155
  235.6 10.0 %copy-start.4 = (f32[4096]{0:T(1024)S(1)}, f32[4096]{0:T(1024)}, u32[]{:S(2)}) copy-start(f32[4096]{0:T(1024)} %param.21) | copy-start | bytes 49156
  240.3 3.6 collective-permute-start.3
  243.9 68.7 %collective-permute-start.13 = (bf16[3,4,1024,128]{3,2,1,0:T(8,128)(2,1)}, bf16[3,4,1024,128]{3,2,1,0:T(8,128)(2,1)}, u32[]{:S(2)}, u32[]{:S(2)}) collective-permute-start(bf16[3,4,1024,128]{3,2,1,0:T(8,128)(2,1)} %constant_dynamic-slice_fusion.5), channel_id=1, source_target_pairs={{0,2},{1,3},{2,0},{3,1},{4,6},{5,7},{6,4},{7,5}} | collective-permute-start | bytes 9437192 | tf_op jit(solution)/shard_map/ppermute | solution.py:155
  264.5 61.7 %collective-permute-start.4 = (f32[4,6144]{1,0:T(4,128)S(1)}, f32[4,6144]{1,0:T(4,128)S(1)}, u32[]{:S(2)}, u32[]{:S(2)}) collective-permute-start(f32[4,6144]{1,0:T(4,128)S(1)} %fusion.30), channel_id=1, source_target_pairs={{0,4},{4,0},{1,5},{5,1},{2,6},{6,2},{3,7},{7,3}} | collective-permute-start | bytes 294920 | tf_op jit(solution)/shard_map/ppermute | solution.py:158
  312.6 308.7 %collective-permute-start.18 = (bf16[4,4,1024,128]{3,2,1,0:T(8,128)(2,1)}, bf16[4,4,1024,128]{3,2,1,0:T(8,128)(2,1)}, u32[]{:S(2)}, u32[]{:S(2)}) collective-permute-start(bf16[4,4,1024,128]{3,2,1,0:T(8,128)(2,1)} %get-tuple-element.29), channel_id=1, source_target_pairs={{0,2},{1,3},{2,0},{3,1},{4,6},{5,7},{6,4},{7,5}} | collective-permute-start | bytes 12582920 | tf_op jit(solution)/shard_map/ppermute | solution.py:155
  316.9 311.1 %collective-permute-start.17 = (bf16[3,4,1024,128]{3,2,1,0:T(8,128)(2,1)}, bf16[3,4,1024,128]{3,2,1,0:T(8,128)(2,1)}, u32[]{:S(2)}, u32[]{:S(2)}) collective-permute-start(bf16[3,4,1024,128]{3,2,1,0:T(8,128)(2,1)} %constant_dynamic-slice_fusion.2), channel_id=1, source_target_pairs={{0,3},{1,2},{2,1},{3,0},{4,7},{5,6},{6,5},{7,4}} | collective-permute-start | bytes 9437192 | tf_op jit(solution)/shard_map/ppermute | solution.py:155
  318.6 312.2 %collective-permute-start.16 = (bf16[1,3,1024,128]{3,2,1,0:T(8,128)(2,1)S(1)}, bf16[1,3,1024,128]{3,2,1,0:T(8,128)(2,1)}, u32[]{:S(2)}, u32[]{:S(2)}) collective-permute-start(bf16[1,3,1024,128]{3,2,1,0:T(8,128)(2,1)S(1)} %constant_dynamic-slice_fusion.3), channel_id=1, source_target_pairs={{0,3},{1,2},{2,1},{3,0},{4,7},{5,6},{6,5},{7,4}} | collective-permute-start | bytes 2359304 | tf_op jit(solution)/shard_map/ppermute | solution.py:155
  322.3 311.2 %collective-permute-start.10 = (bf16[4,4,1024,128]{3,2,1,0:T(8,128)(2,1)}, bf16[4,4,1024,128]{3,2,1,0:T(8,128)(2,1)}, u32[]{:S(2)}, u32[]{:S(2)}) collective-permute-start(bf16[4,4,1024,128]{3,2,1,0:T(8,128)(2,1)} %get-tuple-element.31), channel_id=1, source_target_pairs={{0,3},{1,2},{2,1},{3,0},{4,7},{5,6},{6,5},{7,4}} | collective-permute-start | bytes 12582920 | tf_op jit(solution)/shard_map/ppermute | solution.py:155
  357.5 220.2 %copy-start.5 = (bf16[4,4,8,128]{3,2,1,0:T(8,128)(2,1)}, bf16[4,4,8,128]{3,2,1,0:T(8,128)(2,1)S(1)}, u32[]{:S(2)}) copy-start(bf16[4,4,8,128]{3,2,1,0:T(8,128)(2,1)S(1)} %pad_maximum_fusion.3) | copy-start | bytes 98308
  357.6 220.2 %collective-permute-start.5 = (bf16[4,4,8,128]{3,2,1,0:T(8,128)(2,1)S(1)}, bf16[4,4,8,128]{3,2,1,0:T(8,128)(2,1)S(1)}, u32[]{:S(2)}, u32[]{:S(2)}) collective-permute-start(bf16[4,4,8,128]{3,2,1,0:T(8,128)(2,1)S(1)} %pad_maximum_fusion.3), channel_id=1, source_target_pairs={{0,2},{1,3},{2,0},{3,1},{4,6},{5,7},{6,4},{7,5}} | collective-permute-start | bytes 98312 | tf_op jit(solution)/shard_map/ppermute | solution.py:155
  577.8 1.3 collective-permute-start.6
  595.8 1.4 collective-permute-start.7
  597.6 4.3 collective-permute-start.8
  601.9 30.8 %collective-permute-start.15 = (bf16[1,1,1024,128]{3,2,1,0:T(8,128)(2,1)S(1)}, bf16[1,1,1024,128]{3,2,1,0:T(8,128)(2,1)S(1)}, u32[]{:S(2)}, u32[]{:S(2)}) collective-permute-start(bf16[1,1,1024,128]{3,2,1,0:T(8,128)(2,1)S(1)} %constant_dynamic-slice_fusion.7), channel_id=1, source_target_pairs={{0,3},{1,2},{2,1},{3,0},{4,7},{5,6},{6,5},{7,4}} | collective-permute-start | bytes 786440 | tf_op jit(solution)/shard_map/ppermute | solution.py:155
  621.4 16.0 %collective-permute-start.9 = (f32[4,6144]{1,0:T(4,128)S(1)}, f32[4,6144]{1,0:T(4,128)S(1)}, u32[]{:S(2)}, u32[]{:S(2)}) collective-permute-start(f32[4,6144]{1,0:T(4,128)S(1)} %fusion.32), channel_id=1, source_target_pairs={{0,4},{4,0},{1,5},{5,1},{2,6},{6,2},{3,7},{7,3}} | collective-permute-start | bytes 294920 | tf_op jit(solution)/shard_map/ppermute | solution.py:158
  (3 other events, 9.6 us)

commit v3 on v2

--- a/solution.py
+++ b/solution.py
@@ -48,15 +48,23 @@
 
 def pack(out, stats):
     dim = out.shape[-1]
-    tail = stats.reshape(-1, dim)
-    return jnp.concatenate([out.reshape(-1, dim), jnp.pad(tail, ((0, 8 - tail.shape[0]), (0, 0)))])
+    tail = jnp.pad(stats.reshape(-1), (0, 8 * dim - stats.size)).reshape(8, dim)
+    return jnp.concatenate([out.reshape(-1, dim), tail])
 
 
 def unpack(packed, heads, group):
     lines, dim = packed.shape[0] - 8, packed.shape[1]
     rows = lines // (heads * group)
-    tail = packed[lines:lines + 2 * lines // dim]
+    tail = packed[lines:].reshape(-1)[:2 * lines]
     return packed[:lines].reshape(rows, heads, group, dim), tail.reshape(rows, 2, heads, group)
+
+
+def attend(query, keys, values):
+    scores = jnp.einsum('bkgd,bktd->bkgt', query, keys, preferred_element_type=F32) * query.shape[-1] ** -0.5
+    top = jnp.max(scores, axis=-1)
+    probs = jnp.exp(scores - top[..., None])
+    out = jnp.einsum('bkgt,bktd->bkgd', probs.astype(BF16), values, preferred_element_type=F32)
+    return out, jnp.stack([top, jnp.sum(probs, axis=-1)], axis=1)
 
 
 def partner(me, mask):
@@ -87,18 +95,18 @@
     )(cache)
 
 
-def place_block(count, own, mask, out_first, head_first, src_ref, *refs):
+def move_block(rows, source, target, src_ref, *refs):
     out_ref, buf, in_sems, out_sems = refs[-4:]
-    heads, length = src_ref.shape[1], src_ref.shape[2]
+    pieces, heads, length = buf.shape[:3]
     me = lax.axis_index('sp')
-    src_first = me * count if own else 0
-    pos = pl.multiple_of(partner(me, mask) * length, length)
+    src_mask, src_row, src_head = source
+    dst_mask, dst_row, dst_head = target
+    src_row = src_row if src_mask is None else rows * partner(me, src_mask) + src_row
+    pos = 0 if dst_mask is None else pl.multiple_of(partner(me, dst_mask) * length, length)
     reads, writes = [], []
-    for i in range(count):
-        for j in range(heads):
-            n = i * heads + j
-            reads.append(pltpu.make_async_copy(src_ref.at[src_first + i, j], buf.at[n], in_sems.at[n]))
-            writes.append(pltpu.make_async_copy(buf.at[n], out_ref.at[out_first + i, head_first + j, pl.ds(pos, length)], out_sems.at[n]))
+    for n in range(pieces):
+        reads.append(pltpu.make_async_copy(src_ref.at[src_row + n, pl.ds(src_head, heads)], buf.at[n], in_sems.at[n]))
+        writes.append(pltpu.make_async_copy(buf.at[n], out_ref.at[dst_row + n, pl.ds(dst_head, heads), pl.ds(pos, length)], out_sems.at[n]))
     for copy in reads:
         copy.start()
     for read, write in zip(reads, writes):
@@ -108,22 +116,31 @@
         copy.wait()
 
 
-def place(total, block, mask, out_shape, own=False, out_first=0, head_first=0):
-    count = out_shape[0] if own else block.shape[0]
-    pieces = count * block.shape[1]
+def move(block, total, out_shape, count, heads, source, target, rows):
     operands = [block] if total is None else [block, total]
-    nbytes = 2 * pieces * block.shape[2] * block.shape[3] * 2
+    length, dim = block.shape[2:]
+    nbytes = 2 * count * heads * length * dim * 2
     return pl.pallas_call(
-        functools.partial(place_block, count, own, mask, out_first, head_first),
+        functools.partial(move_block, rows, source, target),
         in_specs=[pl.BlockSpec(memory_space=pltpu.HBM)] * len(operands),
         out_specs=pl.BlockSpec(memory_space=pltpu.HBM),
         out_shape=jax.ShapeDtypeStruct(out_shape, block.dtype),
-        scratch_shapes=[pltpu.VMEM((pieces,) + block.shape[2:], block.dtype), pltpu.SemaphoreType.DMA((pieces,)), pltpu.SemaphoreType.DMA((pieces,))],
+        scratch_shapes=[pltpu.VMEM((count, heads, length, dim), block.dtype), pltpu.SemaphoreType.DMA((count,)), pltpu.SemaphoreType.DMA((count,))],
         input_output_aliases={} if total is None else {1: 0},
         compiler_params=pltpu.CompilerParams(vmem_limit_bytes=62 * 1024 * 1024),
         cost_estimate=pl.CostEstimate(flops=nbytes * 30, bytes_accessed=nbytes, transcendentals=0),
-        name="place",
+        name="move",
     )(*operands)
+
+
+def place(total, block, mask, out_shape, own=False, out_first=0, head_first=0):
+    count = out_shape[0] if own else block.shape[0]
+    return move(block, total, out_shape, count, block.shape[1], (0 if own else None, 0, 0), (mask, out_first, head_first), out_shape[0])
+
+
+def cut(cache, rows, mask, first, count, head=0, heads=None):
+    heads = cache.shape[1] if heads is None else heads
+    return move(cache, None, (count, heads) + cache.shape[2:], count, heads, (mask, first, head), (None, 0, 0), rows)
 
 
 def write_block(mask, row, head, src_ref, total_ref, out_ref, sem):
@@ -176,7 +193,7 @@
         kx1_rows = grab(k_src, rows, 2, 0, 1, kv_dev - 1)
         kx1 = send(kx1_rows, 2)
         k_src, slopes_a, _ = lax.optimization_barrier((k_cache, slopes, kx1_rows))
-        kx2_rows = rows_of(k_src, 2, 1, rows - 1)
+        kx2_rows = cut(k_src, rows, 2, 1, rows - 1)
         kx2 = send(kx2_rows, 2)
 
         own = states[0]
@@ -195,14 +212,16 @@
         sx = send(part_x, 2)
 
         k_src, v_src, _ = lax.optimization_barrier((k_cache, v_cache, part_x))
-        ky_rows = rows_of(k_src, 3)
-        kd_rows = rows_of(k_src, 1)
-        vd_rows = rows_of(v_src, 1)
-        vx_rows = rows_of(v_src, 2)
-        vy0_rows = rows_of(v_src, 3, 0, rows - 1)
-        last_row = rows_of(v_src, 3, rows - 1, 1)
-        vy1_rows = last_row[:, :kv_dev - 1]
-        vy2_rows = last_row[:, kv_dev - 1:]
+        ky_rows = cut(k_src, rows, 3, 1, rows - 1)
+        ky0_rows = cut(k_src, rows, 3, 0, 1)
+        kd_rows = cut(k_src, rows, 1, 0, rows)
+        vd_rows = cut(v_src, rows, 1, 0, rows)
+        vx_rows = cut(v_src, rows, 2, 1, rows - 1)
+        vx0_rows = cut(v_src, rows, 2, 0, 1)
+        vy_rows = cut(v_src, rows, 3, 1, rows - 1)
+        vy0_rows = cut(v_src, rows, 3, 0, 1, 0, kv_dev - 1)
+        vy1_rows = cut(v_src, rows, 3, 0, 1, kv_dev - 1, 1)
+        ky0 = send(ky0_rows, 3)
         ky = send(ky_rows, 3)
         kd = send(kd_rows, 1)
         vd = send(vd_rows, 1)
@@ -225,30 +244,31 @@
         key_new = rotary(attn_proj[:, :, group], prompt_len)
         value_new = attn_proj[:, :, group + 1]
 
-        qx = send(query_rot, 2)
+        qx = send(query_rot[:1], 2)
         vx = send(vx_rows, 2)
-        qd = send(jnp.stack([query_rot, qx]), 1)
-
-        score_scale = head_dim ** -0.5
+        qd = send(jnp.concatenate([query_rot, qx]), 1)
+
         order = jnp.arange(seq_shards) ^ me
-        query_all = jnp.take(jnp.stack([query_rot, qd[0], qx, qd[1]]), order, axis=0).reshape(seq_shards * rows, kv_dev, group, head_dim)
-        scores = jnp.einsum('bkgd,bktd->bkgt', query_all, k_cache, preferred_element_type=F32) * score_scale
-        part_max = jnp.max(scores, axis=-1)
-        probs = jnp.exp(scores - part_max[..., None])
-        part_sum = jnp.sum(probs, axis=-1)
-        part_out = jnp.einsum('bkgt,bktd->bkgd', probs.astype(BF16), v_cache, preferred_element_type=F32)
-        stats = jnp.stack([part_max, part_sum], axis=1)
-
-        pair = pack(jnp.concatenate([rows_of(part_out, 3), rows_of(part_out, 1)]), jnp.concatenate([rows_of(stats, 3), rows_of(stats, 1)]))
+        unused = jnp.zeros((rows - 1,) + query_rot.shape[1:], BF16)
+        query_all = jnp.stack([query_rot, qd[:rows], jnp.concatenate([qx, unused]), jnp.concatenate([qd[rows:], unused])])
+        query_all = jnp.take(query_all, order, axis=0).reshape(seq_shards * rows, kv_dev, group, head_dim)
+        part_out, stats = attend(query_all, k_cache, v_cache)
+
+        pair = pack(jnp.concatenate([rows_of(part_out, 3, 0, 1), rows_of(part_out, 1)]), jnp.concatenate([rows_of(stats, 3, 0, 1), rows_of(stats, 1)]))
         pair_out, pair_stats = unpack(send(pair, 1), kv_dev, group)
-        far = pack(*merge(rows_of(part_out, 2), rows_of(stats, 2), pair_out[:rows], pair_stats[:rows]))
+        far = pack(*merge(rows_of(part_out, 2, 0, 1), rows_of(stats, 2, 0, 1), pair_out[:1], pair_stats[:1]))
         ax, axs = unpack(send(far, 2), kv_dev, group)
+        vy = send(vy_rows, 3)
+        vx0 = send(vx0_rows, 2)
         vy0 = send(vy0_rows, 3)
         vy1 = send(vy1_rows, 3)
-        vy2 = send(vy2_rows, 3)
-
-        near_out, near_stats = merge(rows_of(part_out, 0), rows_of(stats, 0), pair_out[rows:], pair_stats[rows:])
-        all_out, all_stats = merge(near_out, near_stats, ax, axs)
+
+        home_x = attend(query_rot[1:], kx2, vx)
+        home_y = attend(query_rot[1:], ky, vy)
+        near_out, near_stats = merge(rows_of(part_out, 0), rows_of(stats, 0), pair_out[1:], pair_stats[1:])
+        home_out, home_stats = merge(*home_x, *home_y)
+        all_out, all_stats = merge(near_out, near_stats, jnp.concatenate([ax, home_out]), jnp.concatenate([axs, home_stats]))
+        score_scale = head_dim ** -0.5
         new_score = jnp.einsum('clhe,cle->clh', query_rot, key_new, preferred_element_type=F32) * score_scale
         row_max = jnp.maximum(all_stats[:, 0], new_score)
         scale = jnp.exp(all_stats[:, 0] - row_max)
@@ -277,11 +297,13 @@
         k_out = place(k_out, kx1, 2, out_shape, head_first=1)
         k_out = add_tail(k_out, key_new)
         v_out = add_tail(v_out, value_new)
-        k_out = place(k_out, ky, 3, out_shape)
-        v_out = place(v_out, vx, 2, out_shape)
+        k_out = place(k_out, ky0, 3, out_shape)
+        k_out = place(k_out, ky, 3, out_shape, out_first=1)
+        v_out = place(v_out, vx, 2, out_shape, out_first=1)
+        v_out = place(v_out, vy, 3, out_shape, out_first=1)
+        v_out = place(v_out, vx0, 2, out_shape)
         v_out = place(v_out, vy0, 3, out_shape)
-        v_out = place(v_out, vy1, 3, out_shape, out_first=rows - 1)
-        v_out = write(v_out, vy2, 3, rows - 1, kv_dev - 1)
+        v_out = write(v_out, vy1, 3, 0, kv_dev - 1)
         return hidden_out, state_new, k_out, v_out
 
     batch_spec = P(('dp', 'sp'), None)

time: 639 us -> 664 us (1.039)
  Pallas kernels: 39.9 us -> 68.5 us
  local copies, waits for them, and re-layouts: 30.1 us -> 5.82 us
  matrix products: 153 us -> 161 us
    pallas_call x11 -> x23, Pallas kernels: 34.2 us -> 61.8 us  [move(): pl.pallas_call(functools.partial(move_block, rows, source, target), in_sp...]
    dynamic_slice x5 -> x2, local copies, waits for them, and re-layouts: 22.9 us -> 0.02 us  [rows_of(): return lax.dynamic_slice_in_dim(value, rows * (me ^ mask) + first, count, 0)]
    dot_general x2 -> x6, matrix products: 15.2 us -> 24.2 us  [the longest x3 12.2 us: attend(): jnp.einsum('bkgt,bktd->bkgd', probs.astype(BF16), values, preferred_eleme...]
    ppermute x17 -> x19, waiting for transfers between devices: 357 us -> 361 us  [send(): return lax.ppermute(value, 'sp', [(i, i ^ mask) for i in range(seq_shards)])]
    ppermute x17 -> x19, starting transfers between devices: 13.9 us -> 15.5 us  [send(): return lax.ppermute(value, 'sp', [(i, i ^ mask) for i in range(seq_shards)])]
  transfers between devices with their start and end apart: 20 -> 22, of which waited for: 8 -> 8; matrix products, arithmetic and copies ran while one was open for 32% -> 29% of each run, Pallas kernels for 6% -> 10%
where the time goes in v3:
time: 664 us
  waiting for transfers between devices  363 us (55%)
  matrix products  161 us (24%)
  Pallas kernels  68.5 us (10%)
  other arithmetic  42.7 us (6%)
  starting transfers between devices  20.8 us (3%)
    ppermute x19, waiting for transfers between devices, send(): return lax.ppermute(value, 'sp', [(i, i ^ mask) for i in range(seq_shards)])  361 us
    pallas_call x23, Pallas kernels, move(): pl.pallas_call(functools.partial(move_block, rows, source, target), in_sp...  61.8 us
    dot_general x1, matrix products, step(): jnp.einsum('bd,dkn->bkn', normed, w_lin_qkv, preferred_element_type=F32)  48.1 us
    dot_general x1, matrix products, step(): jnp.einsum('bd,dkjn->bkjn', normed_two, w_attn_in, preferred_element_type...  30.4 us
    dot_general x1, matrix products, step(): lin_out = jnp.dot(mixed_out, w_lin_out, preferred_element_type=F32)  18.8 us
    dot_general x1, matrix products, step(): attn_out = jnp.dot(head_out, w_attn_out, preferred_element_type=F32)  18.8 us
    dot_general x1, matrix products, step(): jnp.dot(normed, w_lin_gate, preferred_element_type=F32)  18.8 us
    ppermute x19, starting transfers between devices, send(): return lax.ppermute(value, 'sp', [(i, i ^ mask) for i in range(seq_shards)])  15.5 us
  transfers between devices with their start and end apart: 22, of which 8 were waited for; matrix products, arithmetic and copies ran while one was open for 29% of the time, Pallas kernels for 10%

profile of v3, /device:TPU:0, one launch (start us, length us, event | category | flops | bytes accessed | tf_op | source)
XLA Modules:
  0.0 663.5 jit_solution(6868914404146448933)
XLA Ops:
  4.5 11.1 %bitcast_multiply_fusion.2 = (f32[4,32,128,128]{3,2,1,0:T(8,128)}, f32[4,32,128,128]{3,2,1,0:T(8,128)}) fusion(f32[1,16,32,128,128]{4,3,2,1,0:T(8,128)} %param.14, s32[]{:T(128)S(6)} %select_n.42, f32[32]{0:T(128)S(1)} %multiply_exponential_fusion, s32[]{:T(128)S(6)} %select_n.44), kind=kLoop, calls=%fused_computation.6 | loop fusion | flops 4194304 | bytes 33554568 | tf_op jit(solution)/shard_map/mul | solution.py:203
  20.0 18.8 %fusion.9 = f32[4,4096]{1,0:T(4,128)S(1)} fusion(bf16[6144,4096]{1,0:T(8,128)(2,1)} %param.20, bf16[4,6144]{1,0:T(4,128)(2,1)S(1)} %copy-done.3, f32[6144]{0:T(1024)S(1)} %copy-done.5, f32[4]{0:T(128)S(1)} %add_rsqrt_fusion.1), kind=kOutput, calls=%fused_computation.15 | convolution fusion | flops 201474048 | bytes 50470928 | tf_op jit(solution)/shard_map/dot_general | solution.py:229
  38.8 12.2 %fusion.2 = f32[4,32,128,128]{3,2,1,0:T(8,128)} fusion(f32[4,32,128,128]{3,2,1,0:T(8,128)} %collective-permute-done.1, f32[1,16,32,128,128]{4,3,2,1,0:T(8,128)} %param.14, s32[]{:T(128)S(6)} %select_n.43, f32[32]{0:T(128)S(1)} %multiply_exponential_fusion), kind=kLoop, calls=%fused_computation.5 | loop fusion | flops 4194304 | bytes 25165956 | tf_op jit(solution)/shard_map/add | solution.py:211
  52.8 48.1 %fusion.25 = bf16[4,3,4096]{2,0,1:T(4,128)(2,1)S(1)} fusion(bf16[6144,3,4096]{2,0,1:T(8,128)(2,1)} %param.19, bf16[4,6144]{1,0:T(4,128)(2,1)S(1)} %copy-done.3, f32[6144]{0:T(1024)S(1)} %copy-done.5, f32[4]{0:T(128)S(1)} %add_rsqrt_fusion.1), kind=kOutput, calls=%fused_computation.37 | convolution fusion | flops 604323840 | bytes 151166992 | tf_op jit(solution)/shard_map/bd,dkn->bkn/dot_general | solution.py:208
  105.2 3.4 move.39
  115.0 2.9 move.24
  120.9 3.0 move.25
  123.9 3.3 move.28
  127.2 3.3 move.29.refs_0_
  130.8 103.4 %collective-permute-done.2 = f32[4,32,128,128]{3,2,1,0:T(8,128)} collective-permute-done((f32[4,32,128,128]{3,2,1,0:T(8,128)}, f32[4,32,128,128]{3,2,1,0:T(8,128)}, u32[]{:S(2)}, u32[]{:S(2)}) %collective-permute-start.2) | collective-permute-done | bytes 8388640 | tf_op jit(solution)/shard_map/ppermute | solution.py:172
  234.2 10.0 %fusion.6 = f32[4,32,128,128]{3,2,1,0:T(8,128)S(1)} fusion(f32[4,32,128,128]{3,2,1,0:T(8,128)} %collective-permute-done.2, f32[4,32,128,128]{3,2,1,0:T(8,128)} %collective-permute-done, f32[1,16,32,128,128]{4,3,2,1,0:T(8,128)} %param.14, s32[]{:T(128)S(6)} %select_n.41, f32[4,32,128]{2,1,0:T(8,128)S(1)} %get-tuple-element.29, ...), kind=kLoop, calls=%fused_computation.11 | loop fusion | flops 12582912 | bytes 33685764 | tf_op jit(solution)/shard_map/add | solution.py:233
  244.3 3.4 copy-done
  254.3 18.8 %fusion.44 = f32[4,6144]{1,0:T(4,128)S(1)} fusion(bf16[4096,6144]{1,0:T(8,128)(2,1)} %param.22, f32[4,4096]{1,0:T(4,128)S(1)} %fusion.9, f32[1,4,32,128]{3,2,1,0:T(8,128)S(1)} %bitcast.214, f32[4096]{0:T(1024)S(1)} %copy-done.10, f32[4]{0:T(128)S(1)} %rsqrt_bitcast_fusion), kind=kOutput, calls=%fused_computation.82 | convolution fusion | flops 201392128 | bytes 50577424 | tf_op jit(solution)/shard_map/dot_general | solution.py:238
  276.7 3.3 move.40.refs_0_
  280.0 3.3 move.30.refs_0_
  283.3 38.0 %collective-permute-done.9.src_ref = bf16[3,4,1024,128]{3,2,1,0:T(8,128)(2,1)} collective-permute-done((bf16[3,4,1024,128]{3,2,1,0:T(8,128)(2,1)}, bf16[3,4,1024,128]{3,2,1,0:T(8,128)(2,1)}, u32[]{:S(2)}, u32[]{:S(2)}) %collective-permute-start.9) | collective-permute-done | bytes 3145760 | tf_op jit(solution)/shard_map/ppermute | solution.py:172
  331.7 3.3 move.41.total_ref
  337.0 30.4 %fusion = bf16[4,4,10,128]{3,0,2,1:T(4,128)(2,1)S(1)} fusion(bf16[6144,4,10,128]{3,1,2,0:T(4,128)(2,1)} %param.24, bf16[4,6144]{1,0:T(4,128)(2,1)S(1)} %get-tuple-element.25, f32[6144]{0:T(1024)S(1)} %copy-done.8, f32[4]{0:T(128)S(1)} %add_rsqrt_fusion), kind=kOutput, calls=%fused_computation.1 | convolution fusion | flops 251756544 | bytes 63029264 | tf_op jit(solution)/shard_map/bd,dkjn->bkjn/dot_general | solution.py:242
  368.7 180.3 %collective-permute-done.10.src_ref = bf16[3,4,1024,128]{3,2,1,0:T(8,128)(2,1)S(1)} collective-permute-done((bf16[3,4,1024,128]{3,2,1,0:T(8,128)(2,1)}, bf16[3,4,1024,128]{3,2,1,0:T(8,128)(2,1)S(1)}, u32[]{:S(2)}, u32[]{:S(2)}) %collective-permute-start.10) | collective-permute-done | bytes 3145760 | tf_op jit(solution)/shard_map/ppermute | solution.py:172
  562.5 34.6 %collective-permute-done.5 = bf16[1,4,8,128]{3,2,1,0:T(8,128)(2,1)S(1)} collective-permute-done((bf16[1,4,8,128]{3,2,1,0:T(8,128)(2,1)S(1)}, bf16[1,4,8,128]{3,2,1,0:T(8,128)(2,1)S(1)}, u32[]{:S(2)}, u32[]{:S(2)}) %collective-permute-start.5) | collective-permute-done | bytes 8224 | tf_op jit(solution)/shard_map/ppermute | solution.py:172
  599.3 8.1 %multiply_reduce_fusion = (f32[16,4,8]{2,1,0:T(4,128)S(1)}, f32[16,4,8,1024]{3,2,1,0:T(8,128)S(1)}) fusion(bf16[16,4,8,128]{3,2,1,0:T(8,128)(2,1)S(1)} %bitcast_select_fusion, bf16[16,4,1024,128]{3,2,1,0:T(8,128)(2,1)} %src_ref.9), kind=kOutput, calls=%fused_computation.17 | convolution fusion | flops 135265792 | bytes 19007488 | tf_op jit(solution)/shard_map/bkgd,bktd->bkgt/dot_general | solution.py:63
  608.0 7.3 %fusion.13 = f32[16,4,8,128]{3,2,1,0:T(8,128)S(1)} fusion(bf16[16,4,1024,128]{3,2,1,0:T(8,128)(2,1)} %src_ref.14, f32[16,4,8,1024]{3,2,1,0:T(8,128)S(1)} %get-tuple-element.54, f32[16,4,8]{2,1,0:T(4,128)S(1)} %get-tuple-element.53), kind=kOutput, calls=%fused_computation.25 | convolution fusion | flops 135790592 | bytes 19138560 | tf_op jit(solution)/shard_map/bkgt,bktd->bkgd/dot_general | solution.py:66
  617.6 3.4 collective-permute-done.8
  623.5 18.8 %fusion.46 = f32[4,6144]{1,0:T(4,128)S(1)} fusion(bf16[4096,6144]{1,0:T(8,128)(2,1)} %param.25, bf16[1,4,32,128]{3,2,1,0:T(8,128)(2,1)S(1)} %fusion.53), kind=kOutput, calls=%fused_computation.83 | convolution fusion | flops 201326592 | bytes 50462720 | tf_op jit(solution)/shard_map/dot_general | solution.py:280
  (185 shorter events, 89.4 us)
Async XLA Ops:
  15.6 23.2 %collective-permute-start.1 = (f32[4,32,128,128]{3,2,1,0:T(8,128)}, f32[4,32,128,128]{3,2,1,0:T(8,128)}, u32[]{:S(2)}, u32[]{:S(2)}) collective-permute-start(f32[4,32,128,128]{3,2,1,0:T(8,128)} %get-tuple-element.27), channel_id=1, source_target_pairs={{0,1},{1,0},{2,3},{3,2},{4,5},{5,4},{6,7},{7,6}} | collective-permute-start | bytes 25165832 | tf_op jit(solution)/shard_map/ppermute | solution.py:172
  16.4 307.9 %collective-permute-start.16 = (bf16[1,1,1024,128]{3,2,1,0:T(8,128)(2,1)}, bf16[1,1,1024,128]{3,2,1,0:T(8,128)(2,1)}, u32[]{:S(2)}, u32[]{:S(2)}) collective-permute-start(bf16[1,1,1024,128]{3,2,1,0:T(8,128)(2,1)} %grab.2), channel_id=1, source_target_pairs={{0,2},{1,3},{2,0},{3,1},{4,6},{5,7},{6,4},{7,5}} | collective-permute-start | bytes 786440 | tf_op jit(solution)/shard_map/ppermute | solution.py:172
  18.9 308.9 %collective-permute-start.15 = (bf16[1,3,1024,128]{3,2,1,0:T(8,128)(2,1)}, bf16[1,3,1024,128]{3,2,1,0:T(8,128)(2,1)}, u32[]{:S(2)}, u32[]{:S(2)}) collective-permute-start(bf16[1,3,1024,128]{3,2,1,0:T(8,128)(2,1)} %grab.3), channel_id=1, source_target_pairs={{0,2},{1,3},{2,0},{3,1},{4,6},{5,7},{6,4},{7,5}} | collective-permute-start | bytes 2359304 | tf_op jit(solution)/shard_map/ppermute | solution.py:172
  18.9 111.6 %collective-permute-start = (f32[4,32,128,128]{3,2,1,0:T(8,128)}, f32[4,32,128,128]{3,2,1,0:T(8,128)}, u32[]{:S(2)}, u32[]{:S(2)}) collective-permute-start(f32[4,32,128,128]{3,2,1,0:T(8,128)} %get-tuple-element.26), channel_id=1, source_target_pairs={{0,1},{1,0},{2,3},{3,2},{4,5},{5,4},{6,7},{7,6}} | collective-permute-start | bytes 25165832 | tf_op jit(solution)/shard_map/ppermute | solution.py:172
  51.0 183.2 %collective-permute-start.2 = (f32[4,32,128,128]{3,2,1,0:T(8,128)}, f32[4,32,128,128]{3,2,1,0:T(8,128)}, u32[]{:S(2)}, u32[]{:S(2)}) collective-permute-start(f32[4,32,128,128]{3,2,1,0:T(8,128)} %fusion.2), channel_id=1, source_target_pairs={{0,2},{1,3},{2,0},{3,1},{4,6},{5,7},{6,4},{7,5}} | collective-permute-start | bytes 25165832 | tf_op jit(solution)/shard_map/ppermute | solution.py:172
  108.6 223.0 %collective-permute-start.21 = (bf16[4,4,1024,128]{3,2,1,0:T(8,128)(2,1)}, bf16[4,4,1024,128]{3,2,1,0:T(8,128)(2,1)}, u32[]{:S(2)}, u32[]{:S(2)}) collective-permute-start(bf16[4,4,1024,128]{3,2,1,0:T(8,128)(2,1)} %move.39), channel_id=1, source_target_pairs={{0,1},{1,0},{2,3},{3,2},{4,5},{5,4},{6,7},{7,6}} | collective-permute-start | bytes 12582920 | tf_op jit(solution)/shard_map/ppermute | solution.py:172
  130.5 142.6 %collective-permute-start.17 = (bf16[4,4,1024,128]{3,2,1,0:T(8,128)(2,1)}, bf16[4,4,1024,128]{3,2,1,0:T(8,128)(2,1)}, u32[]{:S(2)}, u32[]{:S(2)}) collective-permute-start(bf16[4,4,1024,128]{3,2,1,0:T(8,128)(2,1)} %move.28), channel_id=1, source_target_pairs={{0,1},{1,0},{2,3},{3,2},{4,5},{5,4},{6,7},{7,6}} | collective-permute-start | bytes 12582920 | tf_op jit(solution)/shard_map/ppermute | solution.py:172
  249.0 3.6 collective-permute-start.3
  252.5 68.9 %collective-permute-start.9 = (bf16[3,4,1024,128]{3,2,1,0:T(8,128)(2,1)}, bf16[3,4,1024,128]{3,2,1,0:T(8,128)(2,1)}, u32[]{:S(2)}, u32[]{:S(2)}) collective-permute-start(bf16[3,4,1024,128]{3,2,1,0:T(8,128)(2,1)} %move.23), channel_id=1, source_target_pairs={{0,2},{1,3},{2,0},{3,1},{4,6},{5,7},{6,4},{7,5}} | collective-permute-start | bytes 9437192 | tf_op jit(solution)/shard_map/ppermute | solution.py:172
  273.1 61.8 %collective-permute-start.4 = (f32[4,6144]{1,0:T(4,128)S(1)}, f32[4,6144]{1,0:T(4,128)S(1)}, u32[]{:S(2)}, u32[]{:S(2)}) collective-permute-start(f32[4,6144]{1,0:T(4,128)S(1)} %fusion.44), channel_id=1, source_target_pairs={{0,4},{4,0},{1,5},{5,1},{2,6},{6,2},{3,7},{7,3}} | collective-permute-start | bytes 294920 | tf_op jit(solution)/shard_map/ppermute | solution.py:175
  321.4 334.5 %collective-permute-start.18 = (bf16[1,1,1024,128]{3,2,1,0:T(8,128)(2,1)}, bf16[1,1,1024,128]{3,2,1,0:T(8,128)(2,1)}, u32[]{:S(2)}, u32[]{:S(2)}) collective-permute-start(bf16[1,1,1024,128]{3,2,1,0:T(8,128)(2,1)} %move.36), channel_id=1, source_target_pairs={{0,3},{1,2},{2,1},{3,0},{4,7},{5,6},{6,5},{7,4}} | collective-permute-start | bytes 786440 | tf_op jit(solution)/shard_map/ppermute | solution.py:172
  324.3 329.5 %collective-permute-start.19 = (bf16[1,3,1024,128]{3,2,1,0:T(8,128)(2,1)}, bf16[1,3,1024,128]{3,2,1,0:T(8,128)(2,1)}, u32[]{:S(2)}, u32[]{:S(2)}) collective-permute-start(bf16[1,3,1024,128]{3,2,1,0:T(8,128)(2,1)} %move.37), channel_id=1, source_target_pairs={{0,3},{1,2},{2,1},{3,0},{4,7},{5,6},{6,5},{7,4}} | collective-permute-start | bytes 2359304 | tf_op jit(solution)/shard_map/ppermute | solution.py:172
  327.8 230.8 %collective-permute-start.11 = (bf16[3,4,1024,128]{3,2,1,0:T(8,128)(2,1)}, bf16[3,4,1024,128]{3,2,1,0:T(8,128)(2,1)}, u32[]{:S(2)}, u32[]{:S(2)}) collective-permute-start(bf16[3,4,1024,128]{3,2,1,0:T(8,128)(2,1)} %move.25), channel_id=1, source_target_pairs={{0,2},{1,3},{2,0},{3,1},{4,6},{5,7},{6,4},{7,5}} | collective-permute-start | bytes 9437192 | tf_op jit(solution)/shard_map/ppermute | solution.py:172
  331.6 223.8 %collective-permute-start.12 = (bf16[3,4,1024,128]{3,2,1,0:T(8,128)(2,1)}, bf16[3,4,1024,128]{3,2,1,0:T(8,128)(2,1)}, u32[]{:S(2)}, u32[]{:S(2)}) collective-permute-start(bf16[3,4,1024,128]{3,2,1,0:T(8,128)(2,1)} %move.26), channel_id=1, source_target_pairs={{0,3},{1,2},{2,1},{3,0},{4,7},{5,6},{6,5},{7,4}} | collective-permute-start | bytes 9437192 | tf_op jit(solution)/shard_map/ppermute | solution.py:172
  335.0 214.1 %collective-permute-start.10 = (bf16[3,4,1024,128]{3,2,1,0:T(8,128)(2,1)}, bf16[3,4,1024,128]{3,2,1,0:T(8,128)(2,1)S(1)}, u32[]{:S(2)}, u32[]{:S(2)}) collective-permute-start(bf16[3,4,1024,128]{3,2,1,0:T(8,128)(2,1)} %move.24), channel_id=1, source_target_pairs={{0,3},{1,2},{2,1},{3,0},{4,7},{5,6},{6,5},{7,4}} | collective-permute-start | bytes 9437192 | tf_op jit(solution)/shard_map/ppermute | solution.py:172
  368.4 190.8 %copy-start.13 = (bf16[4,4,32]{2,1,0:T(4,128)(2,1)}, bf16[4,4,32]{2,1,0:T(4,128)(2,1)S(1)}, u32[]{:S(2)}) copy-start(bf16[4,4,32]{2,1,0:T(4,128)(2,1)S(1)} %get-tuple-element.47) | copy-start | bytes 3076
  368.4 190.8 %copy-start.15 = (bf16[4,4,32]{2,1,0:T(4,128)(2,1)}, bf16[4,4,32]{2,1,0:T(4,128)(2,1)S(1)}, u32[]{:S(2)}) copy-start(bf16[4,4,32]{2,1,0:T(4,128)(2,1)S(1)} %get-tuple-element.48) | copy-start | bytes 3076
  549.0 102.6 %collective-permute-start.20 = (bf16[1,4,1024,128]{3,2,1,0:T(8,128)(2,1)}, bf16[1,4,1024,128]{3,2,1,0:T(8,128)(2,1)}, u32[]{:S(2)}, u32[]{:S(2)}) collective-permute-start(bf16[1,4,1024,128]{3,2,1,0:T(8,128)(2,1)} %move.38), channel_id=1, source_target_pairs={{0,2},{1,3},{2,0},{3,1},{4,6},{5,7},{6,4},{7,5}} | collective-permute-start | bytes 3145736 | tf_op jit(solution)/shard_map/ppermute | solution.py:172
  555.4 102.1 %collective-permute-start.14 = (bf16[1,4,1024,128]{3,2,1,0:T(8,128)(2,1)S(1)}, bf16[1,4,1024,128]{3,2,1,0:T(8,128)(2,1)}, u32[]{:S(2)}, u32[]{:S(2)}) collective-permute-start(bf16[1,4,1024,128]{3,2,1,0:T(8,128)(2,1)S(1)} %copy-done.2), channel_id=1, source_target_pairs={{0,3},{1,2},{2,1},{3,0},{4,7},{5,6},{6,5},{7,4}} | collective-permute-start | bytes 3145736 | tf_op jit(solution)/shard_map/ppermute | solution.py:172
  558.6 38.5 %collective-permute-start.5 = (bf16[1,4,8,128]{3,2,1,0:T(8,128)(2,1)S(1)}, bf16[1,4,8,128]{3,2,1,0:T(8,128)(2,1)S(1)}, u32[]{:S(2)}, u32[]{:S(2)}) collective-permute-start(bf16[1,4,8,128]{3,2,1,0:T(8,128)(2,1)S(1)} %pad_maximum_fusion.7), channel_id=1, source_target_pairs={{0,2},{1,3},{2,0},{3,1},{4,6},{5,7},{6,4},{7,5}} | collective-permute-start | bytes 24584 | tf_op jit(solution)/shard_map/ppermute | solution.py:172
  597.2 1.2 collective-permute-start.6
  615.5 1.3 collective-permute-start.7
  617.2 3.8 collective-permute-start.8
  642.3 20.5 %collective-permute-start.13 = (f32[4,6144]{1,0:T(4,128)S(1)}, f32[4,6144]{1,0:T(4,128)S(1)}, u32[]{:S(2)}, u32[]{:S(2)}) collective-permute-start(f32[4,6144]{1,0:T(4,128)S(1)} %fusion.46), channel_id=1, source_target_pairs={{0,4},{4,0},{1,5},{5,1},{2,6},{6,2},{3,7},{7,3}} | collective-permute-start | bytes 294920 | tf_op jit(solution)/shard_map/ppermute | solution.py:175
  (22 other events, 553.1 us)

commit v4 on v3

--- a/solution.py
+++ b/solution.py
@@ -95,18 +95,21 @@
     )(cache)
 
 
-def move_block(rows, source, target, src_ref, *refs):
-    out_ref, buf, in_sems, out_sems = refs[-4:]
-    pieces, heads, length = buf.shape[:3]
+def move_block(rows, jobs, n_src, n_out, aliased, *refs):
+    srcs, outs = refs[:n_src], refs[n_src + aliased:n_src + aliased + n_out]
+    bufs, in_sems, out_sems = refs[n_src + aliased + n_out:-2], refs[-2], refs[-1]
     me = lax.axis_index('sp')
-    src_mask, src_row, src_head = source
-    dst_mask, dst_row, dst_head = target
-    src_row = src_row if src_mask is None else rows * partner(me, src_mask) + src_row
-    pos = 0 if dst_mask is None else pl.multiple_of(partner(me, dst_mask) * length, length)
     reads, writes = [], []
-    for n in range(pieces):
-        reads.append(pltpu.make_async_copy(src_ref.at[src_row + n, pl.ds(src_head, heads)], buf.at[n], in_sems.at[n]))
-        writes.append(pltpu.make_async_copy(buf.at[n], out_ref.at[dst_row + n, pl.ds(dst_head, heads), pl.ds(pos, length)], out_sems.at[n]))
+    for (src, source, out, target, count, heads), buf in zip(jobs, bufs):
+        length = buf.shape[2]
+        src_mask, src_row, src_head = source
+        dst_mask, dst_row, dst_head = target
+        src_row = src_row if src_mask is None else rows * partner(me, src_mask) + src_row
+        pos = 0 if dst_mask is None else pl.multiple_of(partner(me, dst_mask) * length, length)
+        for i in range(count):
+            n = len(reads)
+            reads.append(pltpu.make_async_copy(srcs[src].at[src_row + i, pl.ds(src_head, heads)], buf.at[i], in_sems.at[n]))
+            writes.append(pltpu.make_async_copy(buf.at[i], outs[out].at[dst_row + i, pl.ds(dst_head, heads), pl.ds(pos, length)], out_sems.at[n]))
     for copy in reads:
         copy.start()
     for read, write in zip(reads, writes):
@@ -116,31 +119,37 @@
         copy.wait()
 
 
-def move(block, total, out_shape, count, heads, source, target, rows):
-    operands = [block] if total is None else [block, total]
-    length, dim = block.shape[2:]
-    nbytes = 2 * count * heads * length * dim * 2
+def move(srcs, jobs, out_shapes, rows, total=None):
+    length, dim = srcs[0].shape[2:]
+    dtype = srcs[0].dtype
+    operands = list(srcs) if total is None else list(srcs) + [total]
+    pieces = sum(job[4] for job in jobs)
+    nbytes = 2 * sum(job[4] * job[5] for job in jobs) * length * dim * 2
     return pl.pallas_call(
-        functools.partial(move_block, rows, source, target),
+        functools.partial(move_block, rows, jobs, len(srcs), len(out_shapes), len(operands) - len(srcs)),
         in_specs=[pl.BlockSpec(memory_space=pltpu.HBM)] * len(operands),
-        out_specs=pl.BlockSpec(memory_space=pltpu.HBM),
-        out_shape=jax.ShapeDtypeStruct(out_shape, block.dtype),
-        scratch_shapes=[pltpu.VMEM((count, heads, length, dim), block.dtype), pltpu.SemaphoreType.DMA((count,)), pltpu.SemaphoreType.DMA((count,))],
-        input_output_aliases={} if total is None else {1: 0},
+        out_specs=[pl.BlockSpec(memory_space=pltpu.HBM)] * len(out_shapes),
+        out_shape=[jax.ShapeDtypeStruct(shape, dtype) for shape in out_shapes],
+        scratch_shapes=[pltpu.VMEM((job[4], job[5], length, dim), dtype) for job in jobs] + [pltpu.SemaphoreType.DMA((pieces,)), pltpu.SemaphoreType.DMA((pieces,))],
+        input_output_aliases={} if total is None else {len(srcs): 0},
         compiler_params=pltpu.CompilerParams(vmem_limit_bytes=62 * 1024 * 1024),
         cost_estimate=pl.CostEstimate(flops=nbytes * 30, bytes_accessed=nbytes, transcendentals=0),
         name="move",
     )(*operands)
 
 
-def place(total, block, mask, out_shape, own=False, out_first=0, head_first=0):
-    count = out_shape[0] if own else block.shape[0]
-    return move(block, total, out_shape, count, block.shape[1], (0 if own else None, 0, 0), (mask, out_first, head_first), out_shape[0])
-
-
-def cut(cache, rows, mask, first, count, head=0, heads=None):
-    heads = cache.shape[1] if heads is None else heads
-    return move(cache, None, (count, heads) + cache.shape[2:], count, heads, (mask, first, head), (None, 0, 0), rows)
+def place(total, blocks, out_shape):
+    rows = out_shape[0]
+    jobs = []
+    for n, (block, mask, row, head) in enumerate(blocks):
+        own = mask == 0
+        jobs.append((n, (0 if own else None, 0, 0), 0, (mask, row, head), rows if own else block.shape[0], block.shape[1]))
+    return move([block[0] for block in blocks], jobs, [out_shape], rows, total)[0]
+
+
+def cut(cache, rows, parts):
+    jobs = [(0, (mask, first, head), n, (None, 0, 0), count, heads) for n, (mask, first, count, head, heads) in enumerate(parts)]
+    return move([cache], jobs, [(part[2], part[4]) + cache.shape[2:] for part in parts], rows)
 
 
 def write_block(mask, row, head, src_ref, total_ref, out_ref, sem):
@@ -193,7 +202,7 @@
         kx1_rows = grab(k_src, rows, 2, 0, 1, kv_dev - 1)
         kx1 = send(kx1_rows, 2)
         k_src, slopes_a, _ = lax.optimization_barrier((k_cache, slopes, kx1_rows))
-        kx2_rows = cut(k_src, rows, 2, 1, rows - 1)
+        kx2_rows, = cut(k_src, rows, [(2, 1, rows - 1, 0, kv_dev)])
         kx2 = send(kx2_rows, 2)
 
         own = states[0]
@@ -212,15 +221,15 @@
         sx = send(part_x, 2)
 
         k_src, v_src, _ = lax.optimization_barrier((k_cache, v_cache, part_x))
-        ky_rows = cut(k_src, rows, 3, 1, rows - 1)
-        ky0_rows = cut(k_src, rows, 3, 0, 1)
-        kd_rows = cut(k_src, rows, 1, 0, rows)
-        vd_rows = cut(v_src, rows, 1, 0, rows)
-        vx_rows = cut(v_src, rows, 2, 1, rows - 1)
-        vx0_rows = cut(v_src, rows, 2, 0, 1)
-        vy_rows = cut(v_src, rows, 3, 1, rows - 1)
-        vy0_rows = cut(v_src, rows, 3, 0, 1, 0, kv_dev - 1)
-        vy1_rows = cut(v_src, rows, 3, 0, 1, kv_dev - 1, 1)
+        ky0_rows, ky_rows, kd_rows = cut(k_src, rows, [(3, 0, 1, 0, kv_dev), (3, 1, rows - 1, 0, kv_dev), (1, 0, rows, 0, kv_dev)])
+        vd_rows, vx_rows, vy_rows, vx0_rows, vy0_rows, vy1_rows = cut(v_src, rows, [
+            (1, 0, rows, 0, kv_dev),
+            (2, 1, rows - 1, 0, kv_dev),
+            (3, 1, rows - 1, 0, kv_dev),
+            (2, 0, 1, 0, kv_dev),
+            (3, 0, 1, 0, kv_dev - 1),
+            (3, 0, 1, kv_dev - 1, 1),
+        ])
         ky0 = send(ky0_rows, 3)
         ky = send(ky_rows, 3)
         kd = send(kd_rows, 1)
@@ -288,21 +297,13 @@
         def add_tail(total, new_row):
             return write(total, jnp.concatenate([new_row[:, :, None, :], tail_zeros], axis=2), None)
 
-        k_out = place(None, k_src, 0, out_shape, own=True)
-        k_out = place(k_out, kd, 1, out_shape)
-        v_out = place(None, v_src, 0, out_shape, own=True)
-        v_out = place(v_out, vd, 1, out_shape)
-        k_out = place(k_out, kx2, 2, out_shape, out_first=1)
-        k_out = place(k_out, kx0, 2, out_shape)
-        k_out = place(k_out, kx1, 2, out_shape, head_first=1)
+        k_out = place(None, [(k_src, 0, 0, 0), (kd, 1, 0, 0), (kx0, 2, 0, 0), (kx1, 2, 0, 1), (kx2, 2, 1, 0)], out_shape)
+        v_out = place(None, [(v_src, 0, 0, 0), (vd, 1, 0, 0)], out_shape)
         k_out = add_tail(k_out, key_new)
         v_out = add_tail(v_out, value_new)
-        k_out = place(k_out, ky0, 3, out_shape)
-        k_out = place(k_out, ky, 3, out_shape, out_first=1)
-        v_out = place(v_out, vx, 2, out_shape, out_first=1)
-        v_out = place(v_out, vy, 3, out_shape, out_first=1)
-        v_out = place(v_out, vx0, 2, out_shape)
-        v_out = place(v_out, vy0, 3, out_shape)
+        k_out = place(k_out, [(ky0, 3, 0, 0), (ky, 3, 1, 0)], out_shape)
+        v_out = place(v_out, [(vx, 2, 1, 0), (vy, 3, 1, 0), (vx0, 2, 0, 0)], out_shape)
+        v_out = place(v_out, [(vy0, 3, 0, 0)], out_shape)
         v_out = write(v_out, vy1, 3, 0, kv_dev - 1)
         return hidden_out, state_new, k_out, v_out
 

time: 664 us -> 666 us (level); the launches traced: 664 us -> 657 us
  Pallas kernels: 68.5 us -> 49.8 us
    pallas_call x23 -> x8, Pallas kernels: 61.8 us -> 45.7 us  [move(): pl.pallas_call(functools.partial(move_block, rows, jobs, len(srcs), len(o...]
  transfers between devices with their start and end apart: 22 -> 22, of which waited for: 8 -> 9; matrix products, arithmetic and copies ran while one was open for 29% -> 30% of each run, Pallas kernels for 10% -> 7%
where the time goes in v4:
time: 666 us; the launch traced here: 657 us
  waiting for transfers between devices  368 us (55%)
  matrix products  166 us (25%)
  Pallas kernels  49.8 us (7%)
  other arithmetic  41 us (6%)
  starting transfers between devices  22.3 us (3%)
  local copies, waits for them, and re-layouts  8.96 us (1%)
    ppermute x19, waiting for transfers between devices, send(): return lax.ppermute(value, 'sp', [(i, i ^ mask) for i in range(seq_shards)])  366 us
    dot_general x1, matrix products, step(): jnp.einsum('bd,dkn->bkn', normed, w_lin_qkv, preferred_element_type=F32)  48.1 us
    pallas_call x8, Pallas kernels, move(): pl.pallas_call(functools.partial(move_block, rows, jobs, len(srcs), len(o...  45.7 us
    dot_general x1, matrix products, step(): jnp.einsum('bd,dkjn->bkjn', normed_two, w_attn_in, preferred_element_type...  30.6 us
    dot_general x1, matrix products, step(): attn_out = jnp.dot(head_out, w_attn_out, preferred_element_type=F32)  19 us
    dot_general x1, matrix products, step(): lin_out = jnp.dot(mixed_out, w_lin_out, preferred_element_type=F32)  18.8 us
    dot_general x1, matrix products, step(): jnp.dot(normed, w_lin_gate, preferred_element_type=F32)  18.8 us
    dot_general x3, matrix products, attend(): jnp.einsum('bkgd,bktd->bkgt', query, keys, preferred_element_type=F32)  17.3 us
  transfers between devices with their start and end apart: 22, of which 9 were waited for; matrix products, arithmetic and copies ran while one was open for 30% of the time, Pallas kernels for 7%

profile of v4, /device:TPU:0, one launch (start us, length us, event | category | flops | bytes accessed | tf_op | source)
XLA Modules:
  0.0 657.2 jit_solution(11097572193886567262)
XLA Ops:
  2.9 11.1 %bitcast_multiply_fusion.2 = (f32[4,32,128,128]{3,2,1,0:T(8,128)}, f32[4,32,128,128]{3,2,1,0:T(8,128)}) fusion(f32[1,16,32,128,128]{4,3,2,1,0:T(8,128)} %param.14, s32[]{:T(128)S(6)} %select_n.42, f32[32]{0:T(128)S(1)} %multiply_exponential_fusion, s32[]{:T(128)S(6)} %select_n.44), kind=kLoop, calls=%fused_computation.6 | loop fusion | flops 4194304 | bytes 33554568 | tf_op jit(solution)/shard_map/mul | solution.py:212
  18.5 18.8 %fusion.9 = f32[4,4096]{1,0:T(4,128)S(1)} fusion(bf16[6144,4096]{1,0:T(8,128)(2,1)} %param.20, bf16[4,6144]{1,0:T(4,128)(2,1)S(1)} %copy-done.3, f32[6144]{0:T(1024)S(1)} %copy-done.4, f32[4]{0:T(128)S(1)} %add_rsqrt_fusion.1), kind=kOutput, calls=%fused_computation.15 | convolution fusion | flops 201474048 | bytes 50470928 | tf_op jit(solution)/shard_map/dot_general | solution.py:238
  37.3 12.2 %fusion.2 = f32[4,32,128,128]{3,2,1,0:T(8,128)} fusion(f32[4,32,128,128]{3,2,1,0:T(8,128)} %collective-permute-done.1, f32[1,16,32,128,128]{4,3,2,1,0:T(8,128)} %param.14, s32[]{:T(128)S(6)} %select_n.43, f32[32]{0:T(128)S(1)} %multiply_exponential_fusion), kind=kLoop, calls=%fused_computation.5 | loop fusion | flops 4194304 | bytes 25165956 | tf_op jit(solution)/shard_map/add | solution.py:220
  51.3 48.1 %fusion.25 = bf16[4,3,4096]{2,0,1:T(4,128)(2,1)S(1)} fusion(bf16[6144,3,4096]{2,0,1:T(8,128)(2,1)} %param.19, bf16[4,6144]{1,0:T(4,128)(2,1)S(1)} %copy-done.3, f32[6144]{0:T(1024)S(1)} %copy-done.4, f32[4]{0:T(128)S(1)} %add_rsqrt_fusion.1), kind=kOutput, calls=%fused_computation.37 | convolution fusion | flops 604323840 | bytes 151166992 | tf_op jit(solution)/shard_map/bd,dkn->bkn/dot_general | solution.py:217
  99.5 3.0 move.8
  103.7 6.5 move.9
  110.4 9.2 %move.10 = (bf16[4,4,1024,128]{3,2,1,0:T(8,128)(2,1)}, bf16[3,4,1024,128]{3,2,1,0:T(8,128)(2,1)}, bf16[3,4,1024,128]{3,2,1,0:T(8,128)(2,1)}, bf16[1,4,1024,128]{...) custom-call(bf16[16,4,1024,128]{3,2,1,0:T(8,128)(2,1)} %refs_0_.4), custom_call_target="tpu_custom_call" | custom-call | flops 754974720 | bytes 25165824 | tf_op jit(solution)/shard_map/move/pallas_call | solution.py:128
  120.0 112.7 %collective-permute-done.2 = f32[4,32,128,128]{3,2,1,0:T(8,128)} collective-permute-done((f32[4,32,128,128]{3,2,1,0:T(8,128)}, f32[4,32,128,128]{3,2,1,0:T(8,128)}, u32[]{:S(2)}, u32[]{:S(2)}) %collective-permute-start.2) | collective-permute-done | bytes 8388640 | tf_op jit(solution)/shard_map/ppermute | solution.py:181
  232.7 10.5 %fusion.6 = f32[4,32,128,128]{3,2,1,0:T(8,128)S(1)} fusion(f32[4,32,128,128]{3,2,1,0:T(8,128)} %collective-permute-done.2, f32[4,32,128,128]{3,2,1,0:T(8,128)} %collective-permute-done, f32[1,16,32,128,128]{4,3,2,1,0:T(8,128)} %param.14, s32[]{:T(128)S(6)} %select_n.41, f32[4,32,128]{2,1,0:T(8,128)S(1)} %get-tuple-element.47, ...), kind=kLoop, calls=%fused_computation.11 | loop fusion | flops 12582912 | bytes 33685764 | tf_op jit(solution)/shard_map/add | solution.py:242
  243.2 3.4 copy-done
  253.2 18.8 %fusion.44 = f32[4,6144]{1,0:T(4,128)S(1)} fusion(bf16[4096,6144]{1,0:T(8,128)(2,1)} %param.22, f32[4,4096]{1,0:T(4,128)S(1)} %fusion.9, f32[1,4,32,128]{3,2,1,0:T(8,128)S(1)} %bitcast.214, f32[4096]{0:T(1024)S(1)} %copy-done.7, f32[4]{0:T(128)S(1)} %rsqrt_bitcast_fusion), kind=kOutput, calls=%fused_computation.82 | convolution fusion | flops 201392128 | bytes 50577424 | tf_op jit(solution)/shard_map/dot_general | solution.py:247
  273.6 6.4 move.13.total_ref
  282.5 40.3 %collective-permute-done.9.refs_4_ = bf16[3,4,1024,128]{3,2,1,0:T(8,128)(2,1)} collective-permute-done((bf16[3,4,1024,128]{3,2,1,0:T(8,128)(2,1)}, bf16[3,4,1024,128]{3,2,1,0:T(8,128)(2,1)}, u32[]{:S(2)}, u32[]{:S(2)}) %collective-permute-start.9) | collective-permute-done | bytes 3145760 | tf_op jit(solution)/shard_map/ppermute | solution.py:181
  324.6 9.2 %move.11.total_ref = bf16[4,4,4112,128]{3,2,1,0:T(8,128)(2,1)} custom-call(bf16[16,4,1024,128]{3,2,1,0:T(8,128)(2,1)} %refs_0_.3, bf16[4,4,1024,128]{3,2,1,0:T(8,128)(2,1)} %collective-permute-done.15.refs_1_, bf16[1,1,1024,128]{3,2,1,0:T(8,128)(2,1)} %copy-done.5, bf16[1,3,1024,128]{3,2,1,0:T(8,128)(2,1)} %collective-permute-done.17.refs_3_, ...), custom_call_target="tpu_custom_call" | custom-call | flops 754974720 | bytes 25165824 | tf_op jit(solution)/shard_map/move/pallas_call | solution.py:128
  336.4 30.6 %fusion = bf16[4,4,10,128]{3,0,2,1:T(4,128)(2,1)S(1)} fusion(bf16[6144,4,10,128]{3,1,2,0:T(4,128)(2,1)} %param.24, bf16[4,6144]{1,0:T(4,128)(2,1)S(1)} %get-tuple-element.43, f32[6144]{0:T(1024)S(1)} %copy-done.6, f32[4]{0:T(128)S(1)} %add_rsqrt_fusion), kind=kOutput, calls=%fused_computation.1 | convolution fusion | flops 251756544 | bytes 63029264 | tf_op jit(solution)/shard_map/bd,dkjn->bkjn/dot_general | solution.py:251
  367.7 44.2 %collective-permute-done.10.refs_1_ = bf16[3,4,1024,128]{3,2,1,0:T(8,128)(2,1)} collective-permute-done((bf16[3,4,1024,128]{3,2,1,0:T(8,128)(2,1)}, bf16[3,4,1024,128]{3,2,1,0:T(8,128)(2,1)}, u32[]{:S(2)}, u32[]{:S(2)}) %collective-permute-start.10) | collective-permute-done | bytes 3145760 | tf_op jit(solution)/shard_map/ppermute | solution.py:181
  417.1 2.9 fusion.94
  420.3 132.1 %collective-permute-done.12.refs_1_ = bf16[3,4,1024,128]{3,2,1,0:T(8,128)(2,1)S(1)} collective-permute-done((bf16[3,4,1024,128]{3,2,1,0:T(8,128)(2,1)}, bf16[3,4,1024,128]{3,2,1,0:T(8,128)(2,1)S(1)}, u32[]{:S(2)}, u32[]{:S(2)}) %collective-permute-start.12) | collective-permute-done | bytes 3145760 | tf_op jit(solution)/shard_map/ppermute | solution.py:181
  557.7 32.4 %collective-permute-done.5 = bf16[1,4,8,128]{3,2,1,0:T(8,128)(2,1)S(1)} collective-permute-done((bf16[1,4,8,128]{3,2,1,0:T(8,128)(2,1)S(1)}, bf16[1,4,8,128]{3,2,1,0:T(8,128)(2,1)S(1)}, u32[]{:S(2)}, u32[]{:S(2)}) %collective-permute-start.5) | collective-permute-done | bytes 8224 | tf_op jit(solution)/shard_map/ppermute | solution.py:181
  592.3 11.6 %multiply_reduce_fusion = (f32[16,4,8]{2,1,0:T(4,128)S(1)}, f32[16,4,8,1024]{3,2,1,0:T(8,128)}) fusion(bf16[16,4,8,128]{3,2,1,0:T(8,128)(2,1)S(1)} %bitcast_select_fusion, bf16[16,4,1024,128]{3,2,1,0:T(8,128)(2,1)} %refs_0_.3), kind=kOutput, calls=%fused_computation.17 | convolution fusion | flops 135265792 | bytes 19007488 | tf_op jit(solution)/shard_map/bkgd,bktd->bkgt/dot_general | solution.py:63
  606.0 8.8 %fusion.13 = f32[16,4,8,128]{3,2,1,0:T(8,128)S(1)} fusion(bf16[16,4,1024,128]{3,2,1,0:T(8,128)(2,1)} %refs_0_.4, f32[16,4,8,1024]{3,2,1,0:T(8,128)} %get-tuple-element.72, f32[16,4,8]{2,1,0:T(4,128)S(1)} %get-tuple-element.71), kind=kOutput, calls=%fused_computation.25 | convolution fusion | flops 135790592 | bytes 19138560 | tf_op jit(solution)/shard_map/bkgt,bktd->bkgd/dot_general | solution.py:66
  620.9 19.0 %fusion.46 = f32[4,6144]{1,0:T(4,128)S(1)} fusion(bf16[4096,6144]{1,0:T(8,128)(2,1)} %param.25, bf16[1,4,32,128]{3,2,1,0:T(8,128)(2,1)S(1)} %fusion.53), kind=kOutput, calls=%fused_computation.83 | convolution fusion | flops 201326592 | bytes 50462720 | tf_op jit(solution)/shard_map/dot_general | solution.py:289
  643.1 6.1 move.14.refs_1_
  652.9 3.3 move.12
  (154 shorter events, 54.6 us)
Async XLA Ops:
  14.0 23.3 %collective-permute-start.1 = (f32[4,32,128,128]{3,2,1,0:T(8,128)}, f32[4,32,128,128]{3,2,1,0:T(8,128)}, u32[]{:S(2)}, u32[]{:S(2)}) collective-permute-start(f32[4,32,128,128]{3,2,1,0:T(8,128)} %get-tuple-element.45), channel_id=1, source_target_pairs={{0,1},{1,0},{2,3},{3,2},{4,5},{5,4},{6,7},{7,6}} | collective-permute-start | bytes 25165832 | tf_op jit(solution)/shard_map/ppermute | solution.py:181
  14.8 265.2 %collective-permute-start.16 = (bf16[1,1,1024,128]{3,2,1,0:T(8,128)(2,1)S(1)}, bf16[1,1,1024,128]{3,2,1,0:T(8,128)(2,1)S(1)}, u32[]{:S(2)}, u32[]{:S(2)}) collective-permute-start(bf16[1,1,1024,128]{3,2,1,0:T(8,128)(2,1)S(1)} %grab.2), channel_id=1, source_target_pairs={{0,2},{1,3},{2,0},{3,1},{4,6},{5,7},{6,4},{7,5}} | collective-permute-start | bytes 786440 | tf_op jit(solution)/shard_map/ppermute | solution.py:181
  17.3 263.5 %collective-permute-start.17 = (bf16[1,3,1024,128]{3,2,1,0:T(8,128)(2,1)S(1)}, bf16[1,3,1024,128]{3,2,1,0:T(8,128)(2,1)}, u32[]{:S(2)}, u32[]{:S(2)}) collective-permute-start(bf16[1,3,1024,128]{3,2,1,0:T(8,128)(2,1)S(1)} %grab.3), channel_id=1, source_target_pairs={{0,2},{1,3},{2,0},{3,1},{4,6},{5,7},{6,4},{7,5}} | collective-permute-start | bytes 2359304 | tf_op jit(solution)/shard_map/ppermute | solution.py:181
  17.3 102.3 %collective-permute-start = (f32[4,32,128,128]{3,2,1,0:T(8,128)}, f32[4,32,128,128]{3,2,1,0:T(8,128)}, u32[]{:S(2)}, u32[]{:S(2)}) collective-permute-start(f32[4,32,128,128]{3,2,1,0:T(8,128)} %get-tuple-element.44), channel_id=1, source_target_pairs={{0,1},{1,0},{2,3},{3,2},{4,5},{5,4},{6,7},{7,6}} | collective-permute-start | bytes 25165832 | tf_op jit(solution)/shard_map/ppermute | solution.py:181
  18.5 32.8 %copy-start.8 = (f32[4]{0:T(128)}, f32[4]{0:T(128)S(1)}, u32[]{:S(2)}) copy-start(f32[4]{0:T(128)S(1)} %add_rsqrt_fusion.1) | copy-start | bytes 52
  49.5 183.2 %collective-permute-start.2 = (f32[4,32,128,128]{3,2,1,0:T(8,128)}, f32[4,32,128,128]{3,2,1,0:T(8,128)}, u32[]{:S(2)}, u32[]{:S(2)}) collective-permute-start(f32[4,32,128,128]{3,2,1,0:T(8,128)} %fusion.2), channel_id=1, source_target_pairs={{0,2},{1,3},{2,0},{3,1},{4,6},{5,7},{6,4},{7,5}} | collective-permute-start | bytes 25165832 | tf_op jit(solution)/shard_map/ppermute | solution.py:181
  110.2 212.6 %collective-permute-start.15 = (bf16[4,4,1024,128]{3,2,1,0:T(8,128)(2,1)}, bf16[4,4,1024,128]{3,2,1,0:T(8,128)(2,1)}, u32[]{:S(2)}, u32[]{:S(2)}) collective-permute-start(bf16[4,4,1024,128]{3,2,1,0:T(8,128)(2,1)} %get-tuple-element.27), channel_id=1, source_target_pairs={{0,1},{1,0},{2,3},{3,2},{4,5},{5,4},{6,7},{7,6}} | collective-permute-start | bytes 12582920 | tf_op jit(solution)/shard_map/ppermute | solution.py:181
  119.7 152.4 %collective-permute-start.21 = (bf16[4,4,1024,128]{3,2,1,0:T(8,128)(2,1)}, bf16[4,4,1024,128]{3,2,1,0:T(8,128)(2,1)}, u32[]{:S(2)}, u32[]{:S(2)}) collective-permute-start(bf16[4,4,1024,128]{3,2,1,0:T(8,128)(2,1)} %get-tuple-element.31), channel_id=1, source_target_pairs={{0,1},{1,0},{2,3},{3,2},{4,5},{5,4},{6,7},{7,6}} | collective-permute-start | bytes 12582920 | tf_op jit(solution)/shard_map/ppermute | solution.py:181
  247.9 3.6 collective-permute-start.3
  251.5 71.3 %collective-permute-start.9 = (bf16[3,4,1024,128]{3,2,1,0:T(8,128)(2,1)}, bf16[3,4,1024,128]{3,2,1,0:T(8,128)(2,1)}, u32[]{:S(2)}, u32[]{:S(2)}) collective-permute-start(bf16[3,4,1024,128]{3,2,1,0:T(8,128)(2,1)} %move.8), channel_id=1, source_target_pairs={{0,2},{1,3},{2,0},{3,1},{4,6},{5,7},{6,4},{7,5}} | collective-permute-start | bytes 9437192 | tf_op jit(solution)/shard_map/ppermute | solution.py:181
  272.1 61.7 %collective-permute-start.4 = (f32[4,6144]{1,0:T(4,128)S(1)}, f32[4,6144]{1,0:T(4,128)}, u32[]{:S(2)}, u32[]{:S(2)}) collective-permute-start(f32[4,6144]{1,0:T(4,128)S(1)} %fusion.44), channel_id=1, source_target_pairs={{0,4},{4,0},{1,5},{5,1},{2,6},{6,2},{3,7},{7,3}} | collective-permute-start | bytes 294920 | tf_op jit(solution)/shard_map/ppermute | solution.py:184
  280.7 371.2 %collective-permute-start.14 = (bf16[1,4,1024,128]{3,2,1,0:T(8,128)(2,1)}, bf16[1,4,1024,128]{3,2,1,0:T(8,128)(2,1)S(1)}, u32[]{:S(2)}, u32[]{:S(2)}) collective-permute-start(bf16[1,4,1024,128]{3,2,1,0:T(8,128)(2,1)} %get-tuple-element.26), channel_id=1, source_target_pairs={{0,3},{1,2},{2,1},{3,0},{4,7},{5,6},{6,5},{7,4}} | collective-permute-start | bytes 3145736 | tf_op jit(solution)/shard_map/ppermute | solution.py:181
  280.8 131.2 %collective-permute-start.10 = (bf16[3,4,1024,128]{3,2,1,0:T(8,128)(2,1)}, bf16[3,4,1024,128]{3,2,1,0:T(8,128)(2,1)}, u32[]{:S(2)}, u32[]{:S(2)}) collective-permute-start(bf16[3,4,1024,128]{3,2,1,0:T(8,128)(2,1)} %get-tuple-element.22), channel_id=1, source_target_pairs={{0,3},{1,2},{2,1},{3,0},{4,7},{5,6},{6,5},{7,4}} | collective-permute-start | bytes 9437192 | tf_op jit(solution)/shard_map/ppermute | solution.py:181
  322.8 328.4 %collective-permute-start.18 = (bf16[1,1,1024,128]{3,2,1,0:T(8,128)(2,1)}, bf16[1,1,1024,128]{3,2,1,0:T(8,128)(2,1)S(1)}, u32[]{:S(2)}, u32[]{:S(2)}) collective-permute-start(bf16[1,1,1024,128]{3,2,1,0:T(8,128)(2,1)} %get-tuple-element.28), channel_id=1, source_target_pairs={{0,3},{1,2},{2,1},{3,0},{4,7},{5,6},{6,5},{7,4}} | collective-permute-start | bytes 786440 | tf_op jit(solution)/shard_map/ppermute | solution.py:181
  322.8 231.9 %collective-permute-start.11 = (bf16[3,4,1024,128]{3,2,1,0:T(8,128)(2,1)}, bf16[3,4,1024,128]{3,2,1,0:T(8,128)(2,1)}, u32[]{:S(2)}, u32[]{:S(2)}) collective-permute-start(bf16[3,4,1024,128]{3,2,1,0:T(8,128)(2,1)} %get-tuple-element.24), channel_id=1, source_target_pairs={{0,2},{1,3},{2,0},{3,1},{4,6},{5,7},{6,4},{7,5}} | collective-permute-start | bytes 9437192 | tf_op jit(solution)/shard_map/ppermute | solution.py:181
  333.8 218.6 %collective-permute-start.12 = (bf16[3,4,1024,128]{3,2,1,0:T(8,128)(2,1)}, bf16[3,4,1024,128]{3,2,1,0:T(8,128)(2,1)S(1)}, u32[]{:S(2)}, u32[]{:S(2)}) collective-permute-start(bf16[3,4,1024,128]{3,2,1,0:T(8,128)(2,1)} %get-tuple-element.25), channel_id=1, source_target_pairs={{0,3},{1,2},{2,1},{3,0},{4,7},{5,6},{6,5},{7,4}} | collective-permute-start | bytes 9437192 | tf_op jit(solution)/shard_map/ppermute | solution.py:181
  411.9 237.2 %collective-permute-start.19 = (bf16[1,3,1024,128]{3,2,1,0:T(8,128)(2,1)}, bf16[1,3,1024,128]{3,2,1,0:T(8,128)(2,1)}, u32[]{:S(2)}, u32[]{:S(2)}) collective-permute-start(bf16[1,3,1024,128]{3,2,1,0:T(8,128)(2,1)} %get-tuple-element.29), channel_id=1, source_target_pairs={{0,3},{1,2},{2,1},{3,0},{4,7},{5,6},{6,5},{7,4}} | collective-permute-start | bytes 2359304 | tf_op jit(solution)/shard_map/ppermute | solution.py:181
  416.9 175.3 %copy-start.14 = (pred[16]{0:T(512)(128)(4,1)S(1)}, pred[16]{0:T(512)(128)(4,1)}, u32[]{:S(2)}) copy-start(pred[16]{0:T(512)(128)(4,1)} %broadcast_in_dim.15) | copy-start | bytes 52
  552.4 90.7 %collective-permute-start.20 = (bf16[1,4,1024,128]{3,2,1,0:T(8,128)(2,1)}, bf16[1,4,1024,128]{3,2,1,0:T(8,128)(2,1)}, u32[]{:S(2)}, u32[]{:S(2)}) collective-permute-start(bf16[1,4,1024,128]{3,2,1,0:T(8,128)(2,1)} %get-tuple-element.30), channel_id=1, source_target_pairs={{0,2},{1,3},{2,0},{3,1},{4,6},{5,7},{6,4},{7,5}} | collective-permute-start | bytes 3145736 | tf_op jit(solution)/shard_map/ppermute | solution.py:181
  554.7 35.4 %collective-permute-start.5 = (bf16[1,4,8,128]{3,2,1,0:T(8,128)(2,1)S(1)}, bf16[1,4,8,128]{3,2,1,0:T(8,128)(2,1)S(1)}, u32[]{:S(2)}, u32[]{:S(2)}) collective-permute-start(bf16[1,4,8,128]{3,2,1,0:T(8,128)(2,1)S(1)} %pad_maximum_fusion.7), channel_id=1, source_target_pairs={{0,2},{1,3},{2,0},{3,1},{4,6},{5,7},{6,4},{7,5}} | collective-permute-start | bytes 24584 | tf_op jit(solution)/shard_map/ppermute | solution.py:181
  590.2 1.2 collective-permute-start.6
  615.0 1.3 collective-permute-start.7
  616.7 3.8 collective-permute-start.8
  639.9 16.3 %collective-permute-start.13 = (f32[4,6144]{1,0:T(4,128)S(1)}, f32[4,6144]{1,0:T(4,128)S(1)}, u32[]{:S(2)}, u32[]{:S(2)}) collective-permute-start(f32[4,6144]{1,0:T(4,128)S(1)} %fusion.46), channel_id=1, source_target_pairs={{0,4},{4,0},{1,5},{5,1},{2,6},{6,2},{3,7},{7,3}} | collective-permute-start | bytes 294920 | tf_op jit(solution)/shard_map/ppermute | solution.py:184
  (14 other events, 171.8 us)

commit v5 on v4

--- a/solution.py
+++ b/solution.py
@@ -112,9 +112,10 @@
             writes.append(pltpu.make_async_copy(buf.at[i], outs[out].at[dst_row + i, pl.ds(dst_head, heads), pl.ds(pos, length)], out_sems.at[n]))
     for copy in reads:
         copy.start()
-    for read, write in zip(reads, writes):
-        read.wait()
-        write.start()
+    for copy in reversed(reads):
+        copy.wait()
+    for copy in writes:
+        copy.start()
     for copy in writes:
         copy.wait()
 

time: 666 us -> 667 us (level)
  transfers between devices with their start and end apart: 22 -> 22, of which waited for: 9 -> 9; matrix products, arithmetic and copies ran while one was open for 30% -> 30% of each run, Pallas kernels for 7% -> 8%
where the time goes in v5:
time: 667 us; the launch traced here: 658 us
  waiting for transfers between devices  366 us (55%)
  matrix products  166 us (25%)
  Pallas kernels  52.6 us (8%)
  other arithmetic  41 us (6%)
  starting transfers between devices  22.3 us (3%)
  local copies, waits for them, and re-layouts  8.96 us (1%)
    ppermute x19, waiting for transfers between devices, send(): return lax.ppermute(value, 'sp', [(i, i ^ mask) for i in range(seq_shards)])  364 us
    pallas_call x8, Pallas kernels, move(): pl.pallas_call(functools.partial(move_block, rows, jobs, len(srcs), len(o...  48.5 us
    dot_general x1, matrix products, step(): jnp.einsum('bd,dkn->bkn', normed, w_lin_qkv, preferred_element_type=F32)  48.1 us
    dot_general x1, matrix products, step(): jnp.einsum('bd,dkjn->bkjn', normed_two, w_attn_in, preferred_element_type...  30.6 us
    dot_general x1, matrix products, step(): attn_out = jnp.dot(head_out, w_attn_out, preferred_element_type=F32)  19 us
    dot_general x1, matrix products, step(): lin_out = jnp.dot(mixed_out, w_lin_out, preferred_element_type=F32)  18.8 us
    dot_general x1, matrix products, step(): jnp.dot(normed, w_lin_gate, preferred_element_type=F32)  18.8 us
    dot_general x3, matrix products, attend(): jnp.einsum('bkgd,bktd->bkgt', query, keys, preferred_element_type=F32)  17.3 us
  transfers between devices with their start and end apart: 22, of which 9 were waited for; matrix products, arithmetic and copies ran while one was open for 30% of the time, Pallas kernels for 8%

profile of v5, /device:TPU:0, one launch (start us, length us, event | category | flops | bytes accessed | tf_op | source)
XLA Modules:
  0.0 658.3 jit_solution(7116345954349707767)
XLA Ops:
  2.9 11.1 %bitcast_multiply_fusion.2 = (f32[4,32,128,128]{3,2,1,0:T(8,128)}, f32[4,32,128,128]{3,2,1,0:T(8,128)}) fusion(f32[1,16,32,128,128]{4,3,2,1,0:T(8,128)} %param.14, s32[]{:T(128)S(6)} %select_n.42, f32[32]{0:T(128)S(1)} %multiply_exponential_fusion, s32[]{:T(128)S(6)} %select_n.44), kind=kLoop, calls=%fused_computation.6 | loop fusion | flops 4194304 | bytes 33554568 | tf_op jit(solution)/shard_map/mul | solution.py:213
  18.5 18.8 %fusion.9 = f32[4,4096]{1,0:T(4,128)S(1)} fusion(bf16[6144,4096]{1,0:T(8,128)(2,1)} %param.20, bf16[4,6144]{1,0:T(4,128)(2,1)S(1)} %copy-done.3, f32[6144]{0:T(1024)S(1)} %copy-done.4, f32[4]{0:T(128)S(1)} %add_rsqrt_fusion.1), kind=kOutput, calls=%fused_computation.15 | convolution fusion | flops 201474048 | bytes 50470928 | tf_op jit(solution)/shard_map/dot_general | solution.py:239
  37.3 12.2 %fusion.2 = f32[4,32,128,128]{3,2,1,0:T(8,128)} fusion(f32[4,32,128,128]{3,2,1,0:T(8,128)} %collective-permute-done.1, f32[1,16,32,128,128]{4,3,2,1,0:T(8,128)} %param.14, s32[]{:T(128)S(6)} %select_n.43, f32[32]{0:T(128)S(1)} %multiply_exponential_fusion), kind=kLoop, calls=%fused_computation.5 | loop fusion | flops 4194304 | bytes 25165956 | tf_op jit(solution)/shard_map/add | solution.py:221
  51.3 48.1 %fusion.25 = bf16[4,3,4096]{2,0,1:T(4,128)(2,1)S(1)} fusion(bf16[6144,3,4096]{2,0,1:T(8,128)(2,1)} %param.19, bf16[4,6144]{1,0:T(4,128)(2,1)S(1)} %copy-done.3, f32[6144]{0:T(1024)S(1)} %copy-done.4, f32[4]{0:T(128)S(1)} %add_rsqrt_fusion.1), kind=kOutput, calls=%fused_computation.37 | convolution fusion | flops 604323840 | bytes 151166992 | tf_op jit(solution)/shard_map/bd,dkn->bkn/dot_general | solution.py:218
  99.5 3.6 move.8
  104.3 6.9 %move.9 = (bf16[1,4,1024,128]{3,2,1,0:T(8,128)(2,1)}, bf16[3,4,1024,128]{3,2,1,0:T(8,128)(2,1)}, bf16[4,4,1024,128]{3,2,1,0:T(8,128)(2,1)}) custom-call(bf16[16,4,1024,128]{3,2,1,0:T(8,128)(2,1)} %refs_0_.3), custom_call_target="tpu_custom_call" | custom-call | flops 503316480 | bytes 16777216 | tf_op jit(solution)/shard_map/move/pallas_call | solution.py:129
  111.4 9.3 %move.10 = (bf16[4,4,1024,128]{3,2,1,0:T(8,128)(2,1)}, bf16[3,4,1024,128]{3,2,1,0:T(8,128)(2,1)}, bf16[3,4,1024,128]{3,2,1,0:T(8,128)(2,1)}, bf16[1,4,1024,128]{...) custom-call(bf16[16,4,1024,128]{3,2,1,0:T(8,128)(2,1)} %refs_0_.4), custom_call_target="tpu_custom_call" | custom-call | flops 754974720 | bytes 25165824 | tf_op jit(solution)/shard_map/move/pallas_call | solution.py:129
  121.1 111.7 %collective-permute-done.2 = f32[4,32,128,128]{3,2,1,0:T(8,128)} collective-permute-done((f32[4,32,128,128]{3,2,1,0:T(8,128)}, f32[4,32,128,128]{3,2,1,0:T(8,128)}, u32[]{:S(2)}, u32[]{:S(2)}) %collective-permute-start.2) | collective-permute-done | bytes 8388640 | tf_op jit(solution)/shard_map/ppermute | solution.py:182
  232.7 10.5 %fusion.6 = f32[4,32,128,128]{3,2,1,0:T(8,128)S(1)} fusion(f32[4,32,128,128]{3,2,1,0:T(8,128)} %collective-permute-done.2, f32[4,32,128,128]{3,2,1,0:T(8,128)} %collective-permute-done, f32[1,16,32,128,128]{4,3,2,1,0:T(8,128)} %param.14, s32[]{:T(128)S(6)} %select_n.41, f32[4,32,128]{2,1,0:T(8,128)S(1)} %get-tuple-element.47, ...), kind=kLoop, calls=%fused_computation.11 | loop fusion | flops 12582912 | bytes 33685764 | tf_op jit(solution)/shard_map/add | solution.py:243
  243.2 3.4 copy-done
  253.2 18.8 %fusion.44 = f32[4,6144]{1,0:T(4,128)S(1)} fusion(bf16[4096,6144]{1,0:T(8,128)(2,1)} %param.22, f32[4,4096]{1,0:T(4,128)S(1)} %fusion.9, f32[1,4,32,128]{3,2,1,0:T(8,128)S(1)} %bitcast.214, f32[4096]{0:T(1024)S(1)} %copy-done.7, f32[4]{0:T(128)S(1)} %rsqrt_bitcast_fusion), kind=kOutput, calls=%fused_computation.82 | convolution fusion | flops 201392128 | bytes 50577424 | tf_op jit(solution)/shard_map/dot_general | solution.py:248
  273.6 6.8 %move.13.total_ref = bf16[4,4,4112,128]{3,2,1,0:T(8,128)(2,1)} custom-call(bf16[16,4,1024,128]{3,2,1,0:T(8,128)(2,1)} %refs_0_.4, bf16[4,4,1024,128]{3,2,1,0:T(8,128)(2,1)} %collective-permute-done.21.refs_1_), custom_call_target="tpu_custom_call" | custom-call | flops 503316480 | bytes 16777216 | tf_op jit(solution)/shard_map/move/pallas_call | solution.py:129
  282.9 39.8 %collective-permute-done.9.refs_4_ = bf16[3,4,1024,128]{3,2,1,0:T(8,128)(2,1)} collective-permute-done((bf16[3,4,1024,128]{3,2,1,0:T(8,128)(2,1)}, bf16[3,4,1024,128]{3,2,1,0:T(8,128)(2,1)}, u32[]{:S(2)}, u32[]{:S(2)}) %collective-permute-start.9) | collective-permute-done | bytes 3145760 | tf_op jit(solution)/shard_map/ppermute | solution.py:182
  324.6 9.4 %move.11.total_ref = bf16[4,4,4112,128]{3,2,1,0:T(8,128)(2,1)} custom-call(bf16[16,4,1024,128]{3,2,1,0:T(8,128)(2,1)} %refs_0_.3, bf16[4,4,1024,128]{3,2,1,0:T(8,128)(2,1)} %collective-permute-done.15.refs_1_, bf16[1,1,1024,128]{3,2,1,0:T(8,128)(2,1)} %copy-done.5, bf16[1,3,1024,128]{3,2,1,0:T(8,128)(2,1)} %collective-permute-done.17.refs_3_, ...), custom_call_target="tpu_custom_call" | custom-call | flops 754974720 | bytes 25165824 | tf_op jit(solution)/shard_map/move/pallas_call | solution.py:129
  336.6 30.6 %fusion = bf16[4,4,10,128]{3,0,2,1:T(4,128)(2,1)S(1)} fusion(bf16[6144,4,10,128]{3,1,2,0:T(4,128)(2,1)} %param.24, bf16[4,6144]{1,0:T(4,128)(2,1)S(1)} %get-tuple-element.43, f32[6144]{0:T(1024)S(1)} %copy-done.6, f32[4]{0:T(128)S(1)} %add_rsqrt_fusion), kind=kOutput, calls=%fused_computation.1 | convolution fusion | flops 251756544 | bytes 63029264 | tf_op jit(solution)/shard_map/bd,dkjn->bkjn/dot_general | solution.py:252
  367.9 44.0 %collective-permute-done.10.refs_1_ = bf16[3,4,1024,128]{3,2,1,0:T(8,128)(2,1)} collective-permute-done((bf16[3,4,1024,128]{3,2,1,0:T(8,128)(2,1)}, bf16[3,4,1024,128]{3,2,1,0:T(8,128)(2,1)}, u32[]{:S(2)}, u32[]{:S(2)}) %collective-permute-start.10) | collective-permute-done | bytes 3145760 | tf_op jit(solution)/shard_map/ppermute | solution.py:182
  417.1 2.9 fusion.94
  420.3 132.1 %collective-permute-done.12.refs_1_ = bf16[3,4,1024,128]{3,2,1,0:T(8,128)(2,1)S(1)} collective-permute-done((bf16[3,4,1024,128]{3,2,1,0:T(8,128)(2,1)}, bf16[3,4,1024,128]{3,2,1,0:T(8,128)(2,1)S(1)}, u32[]{:S(2)}, u32[]{:S(2)}) %collective-permute-start.12) | collective-permute-done | bytes 3145760 | tf_op jit(solution)/shard_map/ppermute | solution.py:182
  557.7 32.4 %collective-permute-done.5 = bf16[1,4,8,128]{3,2,1,0:T(8,128)(2,1)S(1)} collective-permute-done((bf16[1,4,8,128]{3,2,1,0:T(8,128)(2,1)S(1)}, bf16[1,4,8,128]{3,2,1,0:T(8,128)(2,1)S(1)}, u32[]{:S(2)}, u32[]{:S(2)}) %collective-permute-start.5) | collective-permute-done | bytes 8224 | tf_op jit(solution)/shard_map/ppermute | solution.py:182
  592.3 11.6 %multiply_reduce_fusion = (f32[16,4,8]{2,1,0:T(4,128)S(1)}, f32[16,4,8,1024]{3,2,1,0:T(8,128)}) fusion(bf16[16,4,8,128]{3,2,1,0:T(8,128)(2,1)S(1)} %bitcast_select_fusion, bf16[16,4,1024,128]{3,2,1,0:T(8,128)(2,1)} %refs_0_.3), kind=kOutput, calls=%fused_computation.17 | convolution fusion | flops 135265792 | bytes 19007488 | tf_op jit(solution)/shard_map/bkgd,bktd->bkgt/dot_general | solution.py:63
  606.0 8.8 %fusion.13 = f32[16,4,8,128]{3,2,1,0:T(8,128)S(1)} fusion(bf16[16,4,1024,128]{3,2,1,0:T(8,128)(2,1)} %refs_0_.4, f32[16,4,8,1024]{3,2,1,0:T(8,128)} %get-tuple-element.72, f32[16,4,8]{2,1,0:T(4,128)S(1)} %get-tuple-element.71), kind=kOutput, calls=%fused_computation.25 | convolution fusion | flops 135790592 | bytes 19138560 | tf_op jit(solution)/shard_map/bkgt,bktd->bkgd/dot_general | solution.py:66
  620.9 19.0 %fusion.46 = f32[4,6144]{1,0:T(4,128)S(1)} fusion(bf16[4096,6144]{1,0:T(8,128)(2,1)} %param.25, bf16[1,4,32,128]{3,2,1,0:T(8,128)(2,1)S(1)} %fusion.53), kind=kOutput, calls=%fused_computation.83 | convolution fusion | flops 201326592 | bytes 50462720 | tf_op jit(solution)/shard_map/dot_general | solution.py:290
  643.1 6.2 move.14.refs_1_
  653.1 4.2 move.12
  (154 shorter events, 54.6 us)
Async XLA Ops:
  14.0 23.3 %collective-permute-start.1 = (f32[4,32,128,128]{3,2,1,0:T(8,128)}, f32[4,32,128,128]{3,2,1,0:T(8,128)}, u32[]{:S(2)}, u32[]{:S(2)}) collective-permute-start(f32[4,32,128,128]{3,2,1,0:T(8,128)} %get-tuple-element.45), channel_id=1, source_target_pairs={{0,1},{1,0},{2,3},{3,2},{4,5},{5,4},{6,7},{7,6}} | collective-permute-start | bytes 25165832 | tf_op jit(solution)/shard_map/ppermute | solution.py:182
  14.8 265.7 %collective-permute-start.16 = (bf16[1,1,1024,128]{3,2,1,0:T(8,128)(2,1)S(1)}, bf16[1,1,1024,128]{3,2,1,0:T(8,128)(2,1)S(1)}, u32[]{:S(2)}, u32[]{:S(2)}) collective-permute-start(bf16[1,1,1024,128]{3,2,1,0:T(8,128)(2,1)S(1)} %grab.2), channel_id=1, source_target_pairs={{0,2},{1,3},{2,0},{3,1},{4,6},{5,7},{6,4},{7,5}} | collective-permute-start | bytes 786440 | tf_op jit(solution)/shard_map/ppermute | solution.py:182
  17.3 263.9 %collective-permute-start.17 = (bf16[1,3,1024,128]{3,2,1,0:T(8,128)(2,1)S(1)}, bf16[1,3,1024,128]{3,2,1,0:T(8,128)(2,1)}, u32[]{:S(2)}, u32[]{:S(2)}) collective-permute-start(bf16[1,3,1024,128]{3,2,1,0:T(8,128)(2,1)S(1)} %grab.3), channel_id=1, source_target_pairs={{0,2},{1,3},{2,0},{3,1},{4,6},{5,7},{6,4},{7,5}} | collective-permute-start | bytes 2359304 | tf_op jit(solution)/shard_map/ppermute | solution.py:182
  17.3 103.4 %collective-permute-start = (f32[4,32,128,128]{3,2,1,0:T(8,128)}, f32[4,32,128,128]{3,2,1,0:T(8,128)}, u32[]{:S(2)}, u32[]{:S(2)}) collective-permute-start(f32[4,32,128,128]{3,2,1,0:T(8,128)} %get-tuple-element.44), channel_id=1, source_target_pairs={{0,1},{1,0},{2,3},{3,2},{4,5},{5,4},{6,7},{7,6}} | collective-permute-start | bytes 25165832 | tf_op jit(solution)/shard_map/ppermute | solution.py:182
  18.5 32.8 %copy-start.8 = (f32[4]{0:T(128)}, f32[4]{0:T(128)S(1)}, u32[]{:S(2)}) copy-start(f32[4]{0:T(128)S(1)} %add_rsqrt_fusion.1) | copy-start | bytes 52
  49.5 183.2 %collective-permute-start.2 = (f32[4,32,128,128]{3,2,1,0:T(8,128)}, f32[4,32,128,128]{3,2,1,0:T(8,128)}, u32[]{:S(2)}, u32[]{:S(2)}) collective-permute-start(f32[4,32,128,128]{3,2,1,0:T(8,128)} %fusion.2), channel_id=1, source_target_pairs={{0,2},{1,3},{2,0},{3,1},{4,6},{5,7},{6,4},{7,5}} | collective-permute-start | bytes 25165832 | tf_op jit(solution)/shard_map/ppermute | solution.py:182
  111.2 211.6 %collective-permute-start.15 = (bf16[4,4,1024,128]{3,2,1,0:T(8,128)(2,1)}, bf16[4,4,1024,128]{3,2,1,0:T(8,128)(2,1)}, u32[]{:S(2)}, u32[]{:S(2)}) collective-permute-start(bf16[4,4,1024,128]{3,2,1,0:T(8,128)(2,1)} %get-tuple-element.27), channel_id=1, source_target_pairs={{0,1},{1,0},{2,3},{3,2},{4,5},{5,4},{6,7},{7,6}} | collective-permute-start | bytes 12582920 | tf_op jit(solution)/shard_map/ppermute | solution.py:182
  120.8 151.3 %collective-permute-start.21 = (bf16[4,4,1024,128]{3,2,1,0:T(8,128)(2,1)}, bf16[4,4,1024,128]{3,2,1,0:T(8,128)(2,1)}, u32[]{:S(2)}, u32[]{:S(2)}) collective-permute-start(bf16[4,4,1024,128]{3,2,1,0:T(8,128)(2,1)} %get-tuple-element.31), channel_id=1, source_target_pairs={{0,1},{1,0},{2,3},{3,2},{4,5},{5,4},{6,7},{7,6}} | collective-permute-start | bytes 12582920 | tf_op jit(solution)/shard_map/ppermute | solution.py:182
  247.9 3.6 collective-permute-start.3
  251.5 71.3 %collective-permute-start.9 = (bf16[3,4,1024,128]{3,2,1,0:T(8,128)(2,1)}, bf16[3,4,1024,128]{3,2,1,0:T(8,128)(2,1)}, u32[]{:S(2)}, u32[]{:S(2)}) collective-permute-start(bf16[3,4,1024,128]{3,2,1,0:T(8,128)(2,1)} %move.8), channel_id=1, source_target_pairs={{0,2},{1,3},{2,0},{3,1},{4,6},{5,7},{6,4},{7,5}} | collective-permute-start | bytes 9437192 | tf_op jit(solution)/shard_map/ppermute | solution.py:182
  272.1 61.9 %collective-permute-start.4 = (f32[4,6144]{1,0:T(4,128)S(1)}, f32[4,6144]{1,0:T(4,128)}, u32[]{:S(2)}, u32[]{:S(2)}) collective-permute-start(f32[4,6144]{1,0:T(4,128)S(1)} %fusion.44), channel_id=1, source_target_pairs={{0,4},{4,0},{1,5},{5,1},{2,6},{6,2},{3,7},{7,3}} | collective-permute-start | bytes 294920 | tf_op jit(solution)/shard_map/ppermute | solution.py:185
  281.2 370.9 %collective-permute-start.14 = (bf16[1,4,1024,128]{3,2,1,0:T(8,128)(2,1)}, bf16[1,4,1024,128]{3,2,1,0:T(8,128)(2,1)S(1)}, u32[]{:S(2)}, u32[]{:S(2)}) collective-permute-start(bf16[1,4,1024,128]{3,2,1,0:T(8,128)(2,1)} %get-tuple-element.26), channel_id=1, source_target_pairs={{0,3},{1,2},{2,1},{3,0},{4,7},{5,6},{6,5},{7,4}} | collective-permute-start | bytes 3145736 | tf_op jit(solution)/shard_map/ppermute | solution.py:182
  281.2 130.7 %collective-permute-start.10 = (bf16[3,4,1024,128]{3,2,1,0:T(8,128)(2,1)}, bf16[3,4,1024,128]{3,2,1,0:T(8,128)(2,1)}, u32[]{:S(2)}, u32[]{:S(2)}) collective-permute-start(bf16[3,4,1024,128]{3,2,1,0:T(8,128)(2,1)} %get-tuple-element.22), channel_id=1, source_target_pairs={{0,3},{1,2},{2,1},{3,0},{4,7},{5,6},{6,5},{7,4}} | collective-permute-start | bytes 9437192 | tf_op jit(solution)/shard_map/ppermute | solution.py:182
  322.8 328.6 %collective-permute-start.18 = (bf16[1,1,1024,128]{3,2,1,0:T(8,128)(2,1)}, bf16[1,1,1024,128]{3,2,1,0:T(8,128)(2,1)S(1)}, u32[]{:S(2)}, u32[]{:S(2)}) collective-permute-start(bf16[1,1,1024,128]{3,2,1,0:T(8,128)(2,1)} %get-tuple-element.28), channel_id=1, source_target_pairs={{0,3},{1,2},{2,1},{3,0},{4,7},{5,6},{6,5},{7,4}} | collective-permute-start | bytes 786440 | tf_op jit(solution)/shard_map/ppermute | solution.py:182
  322.8 231.9 %collective-permute-start.11 = (bf16[3,4,1024,128]{3,2,1,0:T(8,128)(2,1)}, bf16[3,4,1024,128]{3,2,1,0:T(8,128)(2,1)}, u32[]{:S(2)}, u32[]{:S(2)}) collective-permute-start(bf16[3,4,1024,128]{3,2,1,0:T(8,128)(2,1)} %get-tuple-element.24), channel_id=1, source_target_pairs={{0,2},{1,3},{2,0},{3,1},{4,6},{5,7},{6,4},{7,5}} | collective-permute-start | bytes 9437192 | tf_op jit(solution)/shard_map/ppermute | solution.py:182
  334.0 218.4 %collective-permute-start.12 = (bf16[3,4,1024,128]{3,2,1,0:T(8,128)(2,1)}, bf16[3,4,1024,128]{3,2,1,0:T(8,128)(2,1)S(1)}, u32[]{:S(2)}, u32[]{:S(2)}) collective-permute-start(bf16[3,4,1024,128]{3,2,1,0:T(8,128)(2,1)} %get-tuple-element.25), channel_id=1, source_target_pairs={{0,3},{1,2},{2,1},{3,0},{4,7},{5,6},{6,5},{7,4}} | collective-permute-start | bytes 9437192 | tf_op jit(solution)/shard_map/ppermute | solution.py:182
  411.9 237.4 %collective-permute-start.19 = (bf16[1,3,1024,128]{3,2,1,0:T(8,128)(2,1)}, bf16[1,3,1024,128]{3,2,1,0:T(8,128)(2,1)}, u32[]{:S(2)}, u32[]{:S(2)}) collective-permute-start(bf16[1,3,1024,128]{3,2,1,0:T(8,128)(2,1)} %get-tuple-element.29), channel_id=1, source_target_pairs={{0,3},{1,2},{2,1},{3,0},{4,7},{5,6},{6,5},{7,4}} | collective-permute-start | bytes 2359304 | tf_op jit(solution)/shard_map/ppermute | solution.py:182
  416.9 175.3 %copy-start.14 = (pred[16]{0:T(512)(128)(4,1)S(1)}, pred[16]{0:T(512)(128)(4,1)}, u32[]{:S(2)}) copy-start(pred[16]{0:T(512)(128)(4,1)} %broadcast_in_dim.15) | copy-start | bytes 52
  552.4 90.7 %collective-permute-start.20 = (bf16[1,4,1024,128]{3,2,1,0:T(8,128)(2,1)}, bf16[1,4,1024,128]{3,2,1,0:T(8,128)(2,1)}, u32[]{:S(2)}, u32[]{:S(2)}) collective-permute-start(bf16[1,4,1024,128]{3,2,1,0:T(8,128)(2,1)} %get-tuple-element.30), channel_id=1, source_target_pairs={{0,2},{1,3},{2,0},{3,1},{4,6},{5,7},{6,4},{7,5}} | collective-permute-start | bytes 3145736 | tf_op jit(solution)/shard_map/ppermute | solution.py:182
  554.7 35.4 %collective-permute-start.5 = (bf16[1,4,8,128]{3,2,1,0:T(8,128)(2,1)S(1)}, bf16[1,4,8,128]{3,2,1,0:T(8,128)(2,1)S(1)}, u32[]{:S(2)}, u32[]{:S(2)}) collective-permute-start(bf16[1,4,8,128]{3,2,1,0:T(8,128)(2,1)S(1)} %pad_maximum_fusion.7), channel_id=1, source_target_pairs={{0,2},{1,3},{2,0},{3,1},{4,6},{5,7},{6,4},{7,5}} | collective-permute-start | bytes 24584 | tf_op jit(solution)/shard_map/ppermute | solution.py:182
  590.2 1.2 collective-permute-start.6
  615.0 1.3 collective-permute-start.7
  616.7 3.8 collective-permute-start.8
  639.9 17.4 %collective-permute-start.13 = (f32[4,6144]{1,0:T(4,128)S(1)}, f32[4,6144]{1,0:T(4,128)S(1)}, u32[]{:S(2)}, u32[]{:S(2)}) collective-permute-start(f32[4,6144]{1,0:T(4,128)S(1)} %fusion.46), channel_id=1, source_target_pairs={{0,4},{4,0},{1,5},{5,1},{2,6},{6,2},{3,7},{7,3}} | collective-permute-start | bytes 294920 | tf_op jit(solution)/shard_map/ppermute | solution.py:185
  (14 other events, 173.1 us)

commit v6 on v4

--- a/solution.py
+++ b/solution.py
@@ -152,17 +152,17 @@
     return move([cache], jobs, [(part[2], part[4]) + cache.shape[2:] for part in parts], rows)
 
 
-def write_block(mask, row, head, src_ref, total_ref, out_ref, sem):
+def write_block(mask, row, head, span, offset, src_ref, total_ref, out_ref, sem):
     length = src_ref.shape[2]
-    pos = total_ref.shape[2] - length if mask is None else pl.multiple_of(partner(lax.axis_index('sp'), mask) * length, length)
+    pos = total_ref.shape[2] - length if mask is None else pl.multiple_of(partner(lax.axis_index('sp'), mask) * span + offset, 256)
     copy = pltpu.make_async_copy(src_ref, out_ref.at[pl.ds(row, src_ref.shape[0]), pl.ds(head, src_ref.shape[1]), pl.ds(pos, length)], sem)
     copy.start()
     copy.wait()
 
 
-def write(total, block, mask, row=0, head=0):
+def write(total, block, mask, row=0, head=0, span=0, offset=0):
     return pl.pallas_call(
-        functools.partial(write_block, mask, row, head),
+        functools.partial(write_block, mask, row, head, span, offset),
         in_specs=[pl.BlockSpec(memory_space=pltpu.VMEM), pl.BlockSpec(memory_space=pltpu.HBM)],
         out_specs=pl.BlockSpec(memory_space=pltpu.HBM),
         out_shape=jax.ShapeDtypeStruct(total.shape, total.dtype),
@@ -230,6 +230,9 @@
             (3, 0, 1, 0, kv_dev - 1),
             (3, 0, 1, kv_dev - 1, 1),
         ])
+        early = shard_len // 2
+        vy2_rows = vy1_rows[:, :, early:]
+        vy1_rows = vy1_rows[:, :, :early]
         ky0 = send(ky0_rows, 3)
         ky = send(ky_rows, 3)
         kd = send(kd_rows, 1)
@@ -271,6 +274,7 @@
         vx0 = send(vx0_rows, 2)
         vy0 = send(vy0_rows, 3)
         vy1 = send(vy1_rows, 3)
+        vy2 = send(vy2_rows, 3)
 
         home_x = attend(query_rot[1:], kx2, vx)
         home_y = attend(query_rot[1:], ky, vy)
@@ -304,7 +308,8 @@
         k_out = place(k_out, [(ky0, 3, 0, 0), (ky, 3, 1, 0)], out_shape)
         v_out = place(v_out, [(vx, 2, 1, 0), (vy, 3, 1, 0), (vx0, 2, 0, 0)], out_shape)
         v_out = place(v_out, [(vy0, 3, 0, 0)], out_shape)
-        v_out = write(v_out, vy1, 3, 0, kv_dev - 1)
+        v_out = write(v_out, vy1, 3, 0, kv_dev - 1, shard_len)
+        v_out = write(v_out, vy2, 3, 0, kv_dev - 1, shard_len, early)
         return hidden_out, state_new, k_out, v_out
 
     batch_spec = P(('dp', 'sp'), None)

time: 666 us -> 650 us (0.976)
  waiting for transfers between devices: 368 us -> 349 us
    ppermute x19 -> x20, waiting for transfers between devices: 366 us -> 347 us  [send(): return lax.ppermute(value, 'sp', [(i, i ^ mask) for i in range(seq_shards)])]
    ppermute x19 -> x20, starting transfers between devices: 17.2 us -> 17.9 us  [send(): return lax.ppermute(value, 'sp', [(i, i ^ mask) for i in range(seq_shards)])]
  transfers between devices with their start and end apart: 22 -> 23, of which waited for: 9 -> 10; matrix products, arithmetic and copies ran while one was open for 30% -> 31% of each run, Pallas kernels for 7% -> 8%
where the time goes in v6:
time: 650 us; the launch traced here: 641 us
  waiting for transfers between devices  349 us (54%)
  matrix products  166 us (26%)
  Pallas kernels  50.5 us (8%)
  other arithmetic  41.7 us (6%)
  starting transfers between devices  22.8 us (4%)
  local copies, waits for them, and re-layouts  9.25 us (1%)
    ppermute x20, waiting for transfers between devices, send(): return lax.ppermute(value, 'sp', [(i, i ^ mask) for i in range(seq_shards)])  347 us
    dot_general x1, matrix products, step(): jnp.einsum('bd,dkn->bkn', normed, w_lin_qkv, preferred_element_type=F32)  48.1 us
    pallas_call x8, Pallas kernels, move(): pl.pallas_call(functools.partial(move_block, rows, jobs, len(srcs), len(o...  45.7 us
    dot_general x1, matrix products, step(): jnp.einsum('bd,dkjn->bkjn', normed_two, w_attn_in, preferred_element_type...  30.6 us
    dot_general x1, matrix products, step(): attn_out = jnp.dot(head_out, w_attn_out, preferred_element_type=F32)  19 us
    dot_general x1, matrix products, step(): lin_out = jnp.dot(mixed_out, w_lin_out, preferred_element_type=F32)  18.8 us
    dot_general x1, matrix products, step(): jnp.dot(normed, w_lin_gate, preferred_element_type=F32)  18.8 us
    ppermute x20, starting transfers between devices, send(): return lax.ppermute(value, 'sp', [(i, i ^ mask) for i in range(seq_shards)])  17.9 us
  transfers between devices with their start and end apart: 23, of which 10 were waited for; matrix products, arithmetic and copies ran while one was open for 31% of the time, Pallas kernels for 8%

profile of v6, /device:TPU:0, one launch (start us, length us, event | category | flops | bytes accessed | tf_op | source)
XLA Modules:
  0.0 641.2 jit_solution(8644314636084789484)
XLA Ops:
  2.9 11.1 %bitcast_multiply_fusion.2 = (f32[4,32,128,128]{3,2,1,0:T(8,128)}, f32[4,32,128,128]{3,2,1,0:T(8,128)}) fusion(f32[1,16,32,128,128]{4,3,2,1,0:T(8,128)} %param.14, s32[]{:T(128)S(6)} %select_n.42, f32[32]{0:T(128)S(1)} %multiply_exponential_fusion, s32[]{:T(128)S(6)} %select_n.44), kind=kLoop, calls=%fused_computation.6 | loop fusion | flops 4194304 | bytes 33554568 | tf_op jit(solution)/shard_map/mul | solution.py:212
  18.5 18.8 %fusion.9 = f32[4,4096]{1,0:T(4,128)S(1)} fusion(bf16[6144,4096]{1,0:T(8,128)(2,1)} %param.20, bf16[4,6144]{1,0:T(4,128)(2,1)S(1)} %copy-done.4, f32[6144]{0:T(1024)S(1)} %copy-done.5, f32[4]{0:T(128)S(1)} %add_rsqrt_fusion.1), kind=kOutput, calls=%fused_computation.15 | convolution fusion | flops 201474048 | bytes 50470928 | tf_op jit(solution)/shard_map/dot_general | solution.py:241
  37.3 12.2 %fusion.2 = f32[4,32,128,128]{3,2,1,0:T(8,128)} fusion(f32[4,32,128,128]{3,2,1,0:T(8,128)} %collective-permute-done.1, f32[1,16,32,128,128]{4,3,2,1,0:T(8,128)} %param.14, s32[]{:T(128)S(6)} %select_n.43, f32[32]{0:T(128)S(1)} %multiply_exponential_fusion), kind=kLoop, calls=%fused_computation.5 | loop fusion | flops 4194304 | bytes 25165956 | tf_op jit(solution)/shard_map/add | solution.py:220
  51.3 48.1 %fusion.25 = bf16[4,3,4096]{2,0,1:T(4,128)(2,1)S(1)} fusion(bf16[6144,3,4096]{2,0,1:T(8,128)(2,1)} %param.19, bf16[4,6144]{1,0:T(4,128)(2,1)S(1)} %copy-done.4, f32[6144]{0:T(1024)S(1)} %copy-done.5, f32[4]{0:T(128)S(1)} %add_rsqrt_fusion.1), kind=kOutput, calls=%fused_computation.37 | convolution fusion | flops 604323840 | bytes 151166992 | tf_op jit(solution)/shard_map/bd,dkn->bkn/dot_general | solution.py:217
  103.7 6.5 %move.9 = (bf16[1,4,1024,128]{3,2,1,0:T(8,128)(2,1)}, bf16[3,4,1024,128]{3,2,1,0:T(8,128)(2,1)}, bf16[4,4,1024,128]{3,2,1,0:T(8,128)(2,1)}) custom-call(bf16[16,4,1024,128]{3,2,1,0:T(8,128)(2,1)} %refs_0_.3), custom_call_target="tpu_custom_call" | custom-call | flops 503316480 | bytes 16777216 | tf_op jit(solution)/shard_map/move/pallas_call | solution.py:128
  110.5 9.2 %move.10 = (bf16[4,4,1024,128]{3,2,1,0:T(8,128)(2,1)}, bf16[3,4,1024,128]{3,2,1,0:T(8,128)(2,1)}, bf16[3,4,1024,128]{3,2,1,0:T(8,128)(2,1)}, bf16[1,4,1024,128]{...) custom-call(bf16[16,4,1024,128]{3,2,1,0:T(8,128)(2,1)} %refs_0_.4), custom_call_target="tpu_custom_call" | custom-call | flops 754974720 | bytes 25165824 | tf_op jit(solution)/shard_map/move/pallas_call | solution.py:128
  121.7 111.0 %collective-permute-done.2 = f32[4,32,128,128]{3,2,1,0:T(8,128)} collective-permute-done((f32[4,32,128,128]{3,2,1,0:T(8,128)}, f32[4,32,128,128]{3,2,1,0:T(8,128)}, u32[]{:S(2)}, u32[]{:S(2)}) %collective-permute-start.2) | collective-permute-done | bytes 8388640 | tf_op jit(solution)/shard_map/ppermute | solution.py:181
  232.7 10.5 %fusion.6 = f32[4,32,128,128]{3,2,1,0:T(8,128)S(1)} fusion(f32[4,32,128,128]{3,2,1,0:T(8,128)} %collective-permute-done.2, f32[4,32,128,128]{3,2,1,0:T(8,128)} %collective-permute-done, f32[1,16,32,128,128]{4,3,2,1,0:T(8,128)} %param.14, s32[]{:T(128)S(6)} %select_n.41, f32[4,32,128]{2,1,0:T(8,128)S(1)} %get-tuple-element.49, ...), kind=kLoop, calls=%fused_computation.11 | loop fusion | flops 12582912 | bytes 33685764 | tf_op jit(solution)/shard_map/add | solution.py:245
  243.2 3.4 copy-done
  253.2 18.8 %fusion.44 = f32[4,6144]{1,0:T(4,128)S(1)} fusion(bf16[4096,6144]{1,0:T(8,128)(2,1)} %param.22, f32[4,4096]{1,0:T(4,128)S(1)} %fusion.9, f32[1,4,32,128]{3,2,1,0:T(8,128)S(1)} %bitcast.214, f32[4096]{0:T(1024)S(1)} %copy-done.9, f32[4]{0:T(128)S(1)} %rsqrt_bitcast_fusion), kind=kOutput, calls=%fused_computation.82 | convolution fusion | flops 201392128 | bytes 50577424 | tf_op jit(solution)/shard_map/dot_general | solution.py:250
  273.6 6.4 %move.13.total_ref = bf16[4,4,4112,128]{3,2,1,0:T(8,128)(2,1)} custom-call(bf16[16,4,1024,128]{3,2,1,0:T(8,128)(2,1)} %refs_0_.4, bf16[4,4,1024,128]{3,2,1,0:T(8,128)(2,1)} %collective-permute-done.22.refs_1_), custom_call_target="tpu_custom_call" | custom-call | flops 503316480 | bytes 16777216 | tf_op jit(solution)/shard_map/move/pallas_call | solution.py:128
  282.5 40.3 %collective-permute-done.9.refs_4_ = bf16[3,4,1024,128]{3,2,1,0:T(8,128)(2,1)} collective-permute-done((bf16[3,4,1024,128]{3,2,1,0:T(8,128)(2,1)}, bf16[3,4,1024,128]{3,2,1,0:T(8,128)(2,1)}, u32[]{:S(2)}, u32[]{:S(2)}) %collective-permute-start.9) | collective-permute-done | bytes 3145760 | tf_op jit(solution)/shard_map/ppermute | solution.py:181
  324.5 9.2 %move.11.total_ref = bf16[4,4,4112,128]{3,2,1,0:T(8,128)(2,1)} custom-call(bf16[16,4,1024,128]{3,2,1,0:T(8,128)(2,1)} %refs_0_.3, bf16[4,4,1024,128]{3,2,1,0:T(8,128)(2,1)} %collective-permute-done.15.refs_1_, bf16[1,1,1024,128]{3,2,1,0:T(8,128)(2,1)} %copy-done.6, bf16[1,3,1024,128]{3,2,1,0:T(8,128)(2,1)} %collective-permute-done.17.refs_3_, ...), custom_call_target="tpu_custom_call" | custom-call | flops 754974720 | bytes 25165824 | tf_op jit(solution)/shard_map/move/pallas_call | solution.py:128
  336.4 30.6 %fusion = bf16[4,4,10,128]{3,0,2,1:T(4,128)(2,1)S(1)} fusion(bf16[6144,4,10,128]{3,1,2,0:T(4,128)(2,1)} %param.24, bf16[4,6144]{1,0:T(4,128)(2,1)S(1)} %get-tuple-element.43, f32[6144]{0:T(1024)S(1)} %copy-done.8, f32[4]{0:T(128)S(1)} %add_rsqrt_fusion), kind=kOutput, calls=%fused_computation.1 | convolution fusion | flops 251756544 | bytes 63029264 | tf_op jit(solution)/shard_map/bd,dkjn->bkjn/dot_general | solution.py:254
  368.3 43.6 %collective-permute-done.10.refs_1_ = bf16[3,4,1024,128]{3,2,1,0:T(8,128)(2,1)} collective-permute-done((bf16[3,4,1024,128]{3,2,1,0:T(8,128)(2,1)}, bf16[3,4,1024,128]{3,2,1,0:T(8,128)(2,1)}, u32[]{:S(2)}, u32[]{:S(2)}) %collective-permute-start.10) | collective-permute-done | bytes 3145760 | tf_op jit(solution)/shard_map/ppermute | solution.py:181
  420.7 127.8 %collective-permute-done.12.refs_1_ = bf16[3,4,1024,128]{3,2,1,0:T(8,128)(2,1)S(1)} collective-permute-done((bf16[3,4,1024,128]{3,2,1,0:T(8,128)(2,1)}, bf16[3,4,1024,128]{3,2,1,0:T(8,128)(2,1)S(1)}, u32[]{:S(2)}, u32[]{:S(2)}) %collective-permute-start.12) | collective-permute-done | bytes 3145760 | tf_op jit(solution)/shard_map/ppermute | solution.py:181
  553.9 14.9 %collective-permute-done.5 = bf16[1,4,8,128]{3,2,1,0:T(8,128)(2,1)S(1)} collective-permute-done((bf16[1,4,8,128]{3,2,1,0:T(8,128)(2,1)S(1)}, bf16[1,4,8,128]{3,2,1,0:T(8,128)(2,1)S(1)}, u32[]{:S(2)}, u32[]{:S(2)}) %collective-permute-start.5) | collective-permute-done | bytes 8224 | tf_op jit(solution)/shard_map/ppermute | solution.py:181
  571.0 11.6 %multiply_reduce_fusion = (f32[16,4,8]{2,1,0:T(4,128)S(1)}, f32[16,4,8,1024]{3,2,1,0:T(8,128)}) fusion(bf16[16,4,8,128]{3,2,1,0:T(8,128)(2,1)S(1)} %bitcast_select_fusion, bf16[16,4,1024,128]{3,2,1,0:T(8,128)(2,1)} %refs_0_.3), kind=kOutput, calls=%fused_computation.17 | convolution fusion | flops 135265792 | bytes 19007488 | tf_op jit(solution)/shard_map/bkgd,bktd->bkgt/dot_general | solution.py:63
  584.7 8.8 %fusion.13 = f32[16,4,8,128]{3,2,1,0:T(8,128)S(1)} fusion(bf16[16,4,1024,128]{3,2,1,0:T(8,128)(2,1)} %refs_0_.4, f32[16,4,8,1024]{3,2,1,0:T(8,128)} %get-tuple-element.74, f32[16,4,8]{2,1,0:T(4,128)S(1)} %get-tuple-element.73), kind=kOutput, calls=%fused_computation.25 | convolution fusion | flops 135790592 | bytes 19138560 | tf_op jit(solution)/shard_map/bkgt,bktd->bkgd/dot_general | solution.py:66
  596.0 3.2 collective-permute-done.8
  600.2 19.0 %fusion.46 = f32[4,6144]{1,0:T(4,128)S(1)} fusion(bf16[4096,6144]{1,0:T(8,128)(2,1)} %param.25, bf16[1,4,32,128]{3,2,1,0:T(8,128)(2,1)S(1)} %fusion.53), kind=kOutput, calls=%fused_computation.83 | convolution fusion | flops 201326592 | bytes 50462720 | tf_op jit(solution)/shard_map/dot_general | solution.py:293
  619.2 4.3 collective-permute-done.21.refs_2_
  626.4 6.1 move.14.refs_1_
  637.0 3.3 move.12
  (176 shorter events, 61.1 us)
Async XLA Ops:
  14.0 23.3 %collective-permute-start.1 = (f32[4,32,128,128]{3,2,1,0:T(8,128)}, f32[4,32,128,128]{3,2,1,0:T(8,128)}, u32[]{:S(2)}, u32[]{:S(2)}) collective-permute-start(f32[4,32,128,128]{3,2,1,0:T(8,128)} %get-tuple-element.45), channel_id=1, source_target_pairs={{0,1},{1,0},{2,3},{3,2},{4,5},{5,4},{6,7},{7,6}} | collective-permute-start | bytes 25165832 | tf_op jit(solution)/shard_map/ppermute | solution.py:181
  14.8 265.2 %collective-permute-start.16 = (bf16[1,1,1024,128]{3,2,1,0:T(8,128)(2,1)S(1)}, bf16[1,1,1024,128]{3,2,1,0:T(8,128)(2,1)S(1)}, u32[]{:S(2)}, u32[]{:S(2)}) collective-permute-start(bf16[1,1,1024,128]{3,2,1,0:T(8,128)(2,1)S(1)} %grab.2), channel_id=1, source_target_pairs={{0,2},{1,3},{2,0},{3,1},{4,6},{5,7},{6,4},{7,5}} | collective-permute-start | bytes 786440 | tf_op jit(solution)/shard_map/ppermute | solution.py:181
  17.3 263.5 %collective-permute-start.17 = (bf16[1,3,1024,128]{3,2,1,0:T(8,128)(2,1)S(1)}, bf16[1,3,1024,128]{3,2,1,0:T(8,128)(2,1)}, u32[]{:S(2)}, u32[]{:S(2)}) collective-permute-start(bf16[1,3,1024,128]{3,2,1,0:T(8,128)(2,1)S(1)} %grab.3), channel_id=1, source_target_pairs={{0,2},{1,3},{2,0},{3,1},{4,6},{5,7},{6,4},{7,5}} | collective-permute-start | bytes 2359304 | tf_op jit(solution)/shard_map/ppermute | solution.py:181
  17.3 104.1 %collective-permute-start = (f32[4,32,128,128]{3,2,1,0:T(8,128)}, f32[4,32,128,128]{3,2,1,0:T(8,128)}, u32[]{:S(2)}, u32[]{:S(2)}) collective-permute-start(f32[4,32,128,128]{3,2,1,0:T(8,128)} %get-tuple-element.44), channel_id=1, source_target_pairs={{0,1},{1,0},{2,3},{3,2},{4,5},{5,4},{6,7},{7,6}} | collective-permute-start | bytes 25165832 | tf_op jit(solution)/shard_map/ppermute | solution.py:181
  49.5 183.2 %collective-permute-start.2 = (f32[4,32,128,128]{3,2,1,0:T(8,128)}, f32[4,32,128,128]{3,2,1,0:T(8,128)}, u32[]{:S(2)}, u32[]{:S(2)}) collective-permute-start(f32[4,32,128,128]{3,2,1,0:T(8,128)} %fusion.2), channel_id=1, source_target_pairs={{0,2},{1,3},{2,0},{3,1},{4,6},{5,7},{6,4},{7,5}} | collective-permute-start | bytes 25165832 | tf_op jit(solution)/shard_map/ppermute | solution.py:181
  110.2 212.5 %collective-permute-start.15 = (bf16[4,4,1024,128]{3,2,1,0:T(8,128)(2,1)}, bf16[4,4,1024,128]{3,2,1,0:T(8,128)(2,1)}, u32[]{:S(2)}, u32[]{:S(2)}) collective-permute-start(bf16[4,4,1024,128]{3,2,1,0:T(8,128)(2,1)} %get-tuple-element.27), channel_id=1, source_target_pairs={{0,1},{1,0},{2,3},{3,2},{4,5},{5,4},{6,7},{7,6}} | collective-permute-start | bytes 12582920 | tf_op jit(solution)/shard_map/ppermute | solution.py:181
  121.4 150.7 %collective-permute-start.22 = (bf16[4,4,1024,128]{3,2,1,0:T(8,128)(2,1)}, bf16[4,4,1024,128]{3,2,1,0:T(8,128)(2,1)}, u32[]{:S(2)}, u32[]{:S(2)}) collective-permute-start(bf16[4,4,1024,128]{3,2,1,0:T(8,128)(2,1)} %get-tuple-element.31), channel_id=1, source_target_pairs={{0,1},{1,0},{2,3},{3,2},{4,5},{5,4},{6,7},{7,6}} | collective-permute-start | bytes 12582920 | tf_op jit(solution)/shard_map/ppermute | solution.py:181
  247.9 3.6 collective-permute-start.3
  251.5 71.3 %collective-permute-start.9 = (bf16[3,4,1024,128]{3,2,1,0:T(8,128)(2,1)}, bf16[3,4,1024,128]{3,2,1,0:T(8,128)(2,1)}, u32[]{:S(2)}, u32[]{:S(2)}) collective-permute-start(bf16[3,4,1024,128]{3,2,1,0:T(8,128)(2,1)} %move.8), channel_id=1, source_target_pairs={{0,2},{1,3},{2,0},{3,1},{4,6},{5,7},{6,4},{7,5}} | collective-permute-start | bytes 9437192 | tf_op jit(solution)/shard_map/ppermute | solution.py:181
  272.1 61.7 %collective-permute-start.4 = (f32[4,6144]{1,0:T(4,128)S(1)}, f32[4,6144]{1,0:T(4,128)}, u32[]{:S(2)}, u32[]{:S(2)}) collective-permute-start(f32[4,6144]{1,0:T(4,128)S(1)} %fusion.44), channel_id=1, source_target_pairs={{0,4},{4,0},{1,5},{5,1},{2,6},{6,2},{3,7},{7,3}} | collective-permute-start | bytes 294920 | tf_op jit(solution)/shard_map/ppermute | solution.py:184
  280.7 355.2 %collective-permute-start.14 = (bf16[1,4,1024,128]{3,2,1,0:T(8,128)(2,1)}, bf16[1,4,1024,128]{3,2,1,0:T(8,128)(2,1)S(1)}, u32[]{:S(2)}, u32[]{:S(2)}) collective-permute-start(bf16[1,4,1024,128]{3,2,1,0:T(8,128)(2,1)} %get-tuple-element.26), channel_id=1, source_target_pairs={{0,3},{1,2},{2,1},{3,0},{4,7},{5,6},{6,5},{7,4}} | collective-permute-start | bytes 3145736 | tf_op jit(solution)/shard_map/ppermute | solution.py:181
  280.7 131.2 %collective-permute-start.10 = (bf16[3,4,1024,128]{3,2,1,0:T(8,128)(2,1)}, bf16[3,4,1024,128]{3,2,1,0:T(8,128)(2,1)}, u32[]{:S(2)}, u32[]{:S(2)}) collective-permute-start(bf16[3,4,1024,128]{3,2,1,0:T(8,128)(2,1)} %get-tuple-element.22), channel_id=1, source_target_pairs={{0,3},{1,2},{2,1},{3,0},{4,7},{5,6},{6,5},{7,4}} | collective-permute-start | bytes 9437192 | tf_op jit(solution)/shard_map/ppermute | solution.py:181
  322.8 311.8 %collective-permute-start.19 = (bf16[1,1,512,128]{3,2,1,0:T(8,128)(2,1)}, bf16[1,1,512,128]{3,2,1,0:T(8,128)(2,1)S(1)}, u32[]{:S(2)}, u32[]{:S(2)}) collective-permute-start(bf16[1,1,512,128]{3,2,1,0:T(8,128)(2,1)} %get-tuple-element.46), channel_id=1, source_target_pairs={{0,3},{1,2},{2,1},{3,0},{4,7},{5,6},{6,5},{7,4}} | collective-permute-start | bytes 393224 | tf_op jit(solution)/shard_map/ppermute | solution.py:181
  322.8 228.1 %collective-permute-start.11 = (bf16[3,4,1024,128]{3,2,1,0:T(8,128)(2,1)}, bf16[3,4,1024,128]{3,2,1,0:T(8,128)(2,1)}, u32[]{:S(2)}, u32[]{:S(2)}) collective-permute-start(bf16[3,4,1024,128]{3,2,1,0:T(8,128)(2,1)} %get-tuple-element.24), channel_id=1, source_target_pairs={{0,2},{1,3},{2,0},{3,1},{4,6},{5,7},{6,4},{7,5}} | collective-permute-start | bytes 9437192 | tf_op jit(solution)/shard_map/ppermute | solution.py:181
  333.8 214.7 %collective-permute-start.12 = (bf16[3,4,1024,128]{3,2,1,0:T(8,128)(2,1)}, bf16[3,4,1024,128]{3,2,1,0:T(8,128)(2,1)S(1)}, u32[]{:S(2)}, u32[]{:S(2)}) collective-permute-start(bf16[3,4,1024,128]{3,2,1,0:T(8,128)(2,1)} %get-tuple-element.25), channel_id=1, source_target_pairs={{0,3},{1,2},{2,1},{3,0},{4,7},{5,6},{6,5},{7,4}} | collective-permute-start | bytes 9437192 | tf_op jit(solution)/shard_map/ppermute | solution.py:181
  411.9 223.3 %collective-permute-start.18 = (bf16[1,1,512,128]{3,2,1,0:T(8,128)(2,1)S(1)}, bf16[1,1,512,128]{3,2,1,0:T(8,128)(2,1)S(1)}, u32[]{:S(2)}, u32[]{:S(2)}) collective-permute-start(bf16[1,1,512,128]{3,2,1,0:T(8,128)(2,1)S(1)} %copy-done.7), channel_id=1, source_target_pairs={{0,3},{1,2},{2,1},{3,0},{4,7},{5,6},{6,5},{7,4}} | collective-permute-start | bytes 393224 | tf_op jit(solution)/shard_map/ppermute | solution.py:181
  416.7 154.2 %copy-start.23 = (pred[16]{0:T(512)(128)(4,1)S(1)}, pred[16]{0:T(512)(128)(4,1)}, u32[]{:S(2)}) copy-start(pred[16]{0:T(512)(128)(4,1)} %broadcast_in_dim.15) | copy-start | bytes 52
  548.5 84.0 %collective-permute-start.20 = (bf16[1,3,1024,128]{3,2,1,0:T(8,128)(2,1)}, bf16[1,3,1024,128]{3,2,1,0:T(8,128)(2,1)}, u32[]{:S(2)}, u32[]{:S(2)}) collective-permute-start(bf16[1,3,1024,128]{3,2,1,0:T(8,128)(2,1)} %get-tuple-element.29), channel_id=1, source_target_pairs={{0,3},{1,2},{2,1},{3,0},{4,7},{5,6},{6,5},{7,4}} | collective-permute-start | bytes 2359304 | tf_op jit(solution)/shard_map/ppermute | solution.py:181
  550.9 17.9 %collective-permute-start.5 = (bf16[1,4,8,128]{3,2,1,0:T(8,128)(2,1)S(1)}, bf16[1,4,8,128]{3,2,1,0:T(8,128)(2,1)S(1)}, u32[]{:S(2)}, u32[]{:S(2)}) collective-permute-start(bf16[1,4,8,128]{3,2,1,0:T(8,128)(2,1)S(1)} %pad_maximum_fusion.7), channel_id=1, source_target_pairs={{0,2},{1,3},{2,0},{3,1},{4,6},{5,7},{6,4},{7,5}} | collective-permute-start | bytes 24584 | tf_op jit(solution)/shard_map/ppermute | solution.py:181
  568.9 1.2 collective-permute-start.6
  593.7 1.3 collective-permute-start.7
  595.4 3.8 collective-permute-start.8
  599.2 24.3 %collective-permute-start.21 = (bf16[1,4,1024,128]{3,2,1,0:T(8,128)(2,1)}, bf16[1,4,1024,128]{3,2,1,0:T(8,128)(2,1)S(1)}, u32[]{:S(2)}, u32[]{:S(2)}) collective-permute-start(bf16[1,4,1024,128]{3,2,1,0:T(8,128)(2,1)} %get-tuple-element.30), channel_id=1, source_target_pairs={{0,2},{1,3},{2,0},{3,1},{4,6},{5,7},{6,4},{7,5}} | collective-permute-start | bytes 3145736 | tf_op jit(solution)/shard_map/ppermute | solution.py:181
  623.5 16.8 %collective-permute-start.13 = (f32[4,6144]{1,0:T(4,128)S(1)}, f32[4,6144]{1,0:T(4,128)S(1)}, u32[]{:S(2)}, u32[]{:S(2)}) collective-permute-start(f32[4,6144]{1,0:T(4,128)S(1)} %fusion.46), channel_id=1, source_target_pairs={{0,4},{4,0},{1,5},{5,1},{2,6},{6,2},{3,7},{7,3}} | collective-permute-start | bytes 294920 | tf_op jit(solution)/shard_map/ppermute | solution.py:184
  (24 other events, 476.1 us)
